TPU v7x, 256 devices: a whole 4x4x8 slice. The times are simulated.
256 devices in a mesh: expert: 64 (over z, x, core), replica: 4 (over y).
Axes of the slice: x: 4, y: 4, z: 8, core: 2. Of those that a mesh axis runs over, the one named last changes fastest.
Arguments:
- tokens: bfloat16 [32768, 2048], P(('expert', 'replica')), may hold values from -24 to 24
- cotangent: bfloat16 [32768, 2048], P(('expert', 'replica')), may hold values from -6 to 6
- route_weights: float32 [32768, 8], P(('expert', 'replica')), may hold values from 0.02 to 0.4
- expert_ids: int32 [32768, 8], P(('expert', 'replica')), may hold values from 0 to 127, as said below
- slot_ids: int32 [32768, 8], P(('expert', 'replica')), may hold values from 0 to 7, as said below
- kept_mask: int32 [32768, 8], P(('expert', 'replica')), may hold values from 0 to 1, as said below
- gate_weight: bfloat16 [128, 2048, 384], P('expert'), may hold values from -0.125 to 0.125
- up_weight: bfloat16 [128, 2048, 384], P('expert'), may hold values from -0.125 to 0.125
- down_weight: bfloat16 [128, 384, 2048], P('expert'), may hold values from -0.3125 to 0.3125
- projector_basis: float32 [2048, 256], P('expert'), may hold values from -6 to 6
Outputs:
- token_grads: bfloat16 [32768, 2048], P(('expert', 'replica'))
- projected_grads: float32 [128, 3, 384, 256], P('expert')
- new_basis: float32 [2048, 256], P('expert')
Inputs may be any that keep to these rules, and one draw needn't show every extreme that they name: `expert_ids`: each row names 8 different experts. `slot_ids`: within one device's rows, the kept routes to one expert take slots 0, 1, 2, ... in the order of rows and then of the position in the row; a dropped route has slot 0; in every draw some expert receives 8 kept routes from every device's rows. `kept_mask`: a route is dropped exactly when 8 earlier routes of the same device's rows go to the same expert.
All inputs are finite; a program needn't handle non-finite values.
Results may differ from a plain program's by a relative error of at most 0.019.
Values may be sent and summed in bfloat16 or wider, within the bound.
No kernel may reach another device: no remote copies, remote signals or barrier semaphores. Data moves between devices by JAX's collectives and lax.ppermute only.
A program may use at most 128 MiB of HBM per device.

v0:
```python
import math

import jax
import jax.numpy as jnp
from jax import lax
from jax.sharding import Mesh
from jax.sharding import PartitionSpec as P

EXPERT = ("expert_0", "expert_1", "expert_2")
EXPERT_REPLICA = ("expert_0", "expert_1", "expert_2", "replica")


def from_everyone(array, axis):
    copies = jnp.broadcast_to(array, (lax.axis_size(axis), *array.shape))
    return lax.all_to_all(copies, axis, split_axis=0, concat_axis=0, tiled=True)


def laid_out(pieces, dim):
    pieces = jnp.moveaxis(pieces, 0, dim)
    lengths = pieces.shape
    return pieces.reshape(*lengths[:dim], lengths[dim] * lengths[dim + 1], *lengths[dim + 2 :])


def whole_of(array, axes, dim):
    far, near = axes
    pieces = from_everyone(from_everyone(array, far), near)
    return laid_out(pieces.swapaxes(0, 1).reshape(-1, *array.shape), dim)


def taken_together(array, axis):
    return from_everyone(array, axis).astype(jnp.float32).sum(axis=0)


def rows_for(lines, devices):
    spare = -len(lines) % devices
    return jnp.pad(lines, [(0, spare)] + [(0, 0)] * (lines.ndim - 1))


def cut_along(array, dim, devices):
    before, after = (array.shape[:dim], array.shape[dim + 1 :])
    return jnp.moveaxis(array.reshape(*before, devices, -1, *after), dim, 0)


def sent_and_summed(array, axis, dim):
    pieces = cut_along(array, dim, lax.axis_size(axis))
    arrived = lax.all_to_all(pieces, axis, split_axis=0, concat_axis=0, tiled=True)
    return arrived.astype(jnp.float32).sum(axis=0)


def sum_by_axis(array, axes, dim):
    far, near = axes
    own = sent_and_summed(cut_along(array, dim, lax.axis_size(far)), near, dim + 1)
    return jnp.sum(
        lax.all_to_all(own.astype(jnp.bfloat16), far, 0, 0, tiled=True).astype(jnp.float32), axis=0
    )


def nested_sum(array, axes):
    lines = array.reshape(-1, array.shape[-1])
    padded = rows_for(lines, lax.axis_size(axes[0]) * lax.axis_size(axes[1]))
    whole = whole_of(sum_by_axis(padded, axes, 0).astype(jnp.bfloat16), axes, 0)
    return lax.slice_in_dim(whole, 0, len(lines)).reshape(array.shape).astype(jnp.float32)


def body(
    tokens,
    cotangent,
    route_weights,
    expert_ids,
    slot_ids,
    kept_mask,
    gate_weight,
    up_weight,
    down_weight,
    projector_basis,
):
    tok_count, model_width = tokens.shape
    route_top = expert_ids.shape[1]
    local_count = gate_weight.shape[0]
    group_count = lax.axis_size(EXPERT)
    expert_total = local_count * group_count
    slot_cap = tok_count * route_top // expert_total
    slot_total = expert_total * slot_cap
    route_count = tok_count * route_top
    target = jnp.where(kept_mask > 0, expert_ids * slot_cap + slot_ids, slot_total).reshape(-1)
    table = (
        jnp.full((slot_total,), route_count, jnp.int32)
        .at[target]
        .set(jnp.arange(route_count, dtype=jnp.int32), mode="drop")
    )
    owner = table // route_top
    tokens_pad = jnp.concatenate([tokens, jnp.zeros((1, model_width), tokens.dtype)], 0)
    cotangent_pad = jnp.concatenate([cotangent, jnp.zeros((1, model_width), cotangent.dtype)], 0)
    weight_pad = jnp.concatenate([route_weights.reshape(-1), jnp.zeros((1,), jnp.float32)], 0)
    x_send = tokens_pad[owner].reshape(group_count, local_count * slot_cap, model_width)
    dy_send = (cotangent_pad[owner].astype(jnp.float32) * weight_pad[table][:, None]).astype(
        jnp.bfloat16
    )
    dy_send = dy_send.reshape(group_count, local_count * slot_cap, model_width)
    full_basis = whole_of(
        projector_basis.astype(jnp.bfloat16), (("expert_0", "expert_1"), "expert_2"), 0
    ).astype(projector_basis.dtype)
    projector = (full_basis * (1.0 / math.sqrt(model_width))).astype(jnp.bfloat16)
    block_shape = (group_count, local_count, slot_cap, model_width)
    x_recv = lax.all_to_all(x_send, EXPERT, split_axis=0, concat_axis=0, tiled=True)
    x_rows = x_recv.reshape(block_shape)
    gate = jnp.einsum("sjcd,jdf->sjcf", x_rows, gate_weight, preferred_element_type=jnp.float32)
    upper = jnp.einsum("sjcd,jdf->sjcf", x_rows, up_weight, preferred_element_type=jnp.float32)
    sigma = jax.nn.sigmoid(gate)
    activated = gate * sigma
    slope = sigma * (1.0 + gate * (1.0 - sigma))
    hidden = (activated * upper).astype(jnp.bfloat16)
    x_proj = jnp.einsum(
        "sjcd,dr->sjcr", x_rows, projector, preferred_element_type=jnp.float32
    ).astype(jnp.bfloat16)
    x_rows, upper, activated, slope, hidden, x_proj = (
        x_rows,
        upper,
        activated,
        slope,
        hidden,
        x_proj,
    )
    dy_recv = lax.all_to_all(dy_send, EXPERT, split_axis=0, concat_axis=0, tiled=True)
    dy_rows = dy_recv.reshape(block_shape)
    hidden_grad = jnp.einsum(
        "sjcd,jfd->sjcf", dy_rows, down_weight, preferred_element_type=jnp.float32
    )
    up_grad = (hidden_grad * activated).astype(jnp.bfloat16)
    gate_grad = (hidden_grad * upper * slope).astype(jnp.bfloat16)
    row_grads = jnp.einsum(
        "sjcf,jdf->sjcd", gate_grad, gate_weight, preferred_element_type=jnp.float32
    )
    row_grads = row_grads + jnp.einsum(
        "sjcf,jdf->sjcd", up_grad, up_weight, preferred_element_type=jnp.float32
    )
    row_grads = row_grads.astype(jnp.bfloat16).reshape(
        group_count, local_count * slot_cap, model_width
    )
    returned = lax.all_to_all(row_grads, EXPERT, split_axis=0, concat_axis=0, tiled=True).reshape(
        slot_total, model_width
    )
    returned = jnp.concatenate([returned, jnp.zeros((1, model_width), jnp.bfloat16)], 0)
    token_grads = jnp.sum(
        returned[target].reshape(tok_count, route_top, model_width).astype(jnp.float32), axis=1
    ).astype(jnp.bfloat16)
    dy_proj = jnp.einsum(
        "sjcd,dr->sjcr", dy_rows, projector, preferred_element_type=jnp.float32
    ).astype(jnp.bfloat16)
    partial_grads = jnp.stack(
        [
            jnp.einsum("sjcf,sjcr->jfr", gate_grad, x_proj, preferred_element_type=jnp.float32),
            jnp.einsum("sjcf,sjcr->jfr", up_grad, x_proj, preferred_element_type=jnp.float32),
            jnp.einsum("sjcf,sjcr->jfr", hidden, dy_proj, preferred_element_type=jnp.float32),
        ],
        1,
    )
    projected_grads = taken_together(partial_grads.astype(jnp.bfloat16), "replica").astype(
        jnp.float32
    )
    grads_low = projected_grads.astype(jnp.bfloat16)
    mixed = jnp.einsum(
        "sjcf,jfr->sjcr", gate_grad, grads_low[:, 0], preferred_element_type=jnp.float32
    )
    mixed = (
        mixed
        + jnp.einsum("sjcf,jfr->sjcr", up_grad, grads_low[:, 1], preferred_element_type=jnp.float32)
    ).astype(jnp.bfloat16)
    down_mix = jnp.einsum(
        "sjcf,jfr->sjcr", hidden, grads_low[:, 2], preferred_element_type=jnp.float32
    ).astype(jnp.bfloat16)
    power = jnp.einsum("sjcd,sjcr->dr", x_rows, mixed, preferred_element_type=jnp.float32)
    power = power + jnp.einsum(
        "sjcd,sjcr->dr", dy_rows, down_mix, preferred_element_type=jnp.float32
    )
    panel_rows = model_width // group_count
    power_sum = nested_sum(
        power.astype(jnp.bfloat16), (("expert_0", "expert_1"), ("expert_2", "replica"))
    )
    gram_total = jnp.dot(
        power_sum.T, power_sum, precision=lax.Precision.HIGHEST, preferred_element_type=jnp.float32
    )
    own_panel = lax.dynamic_slice_in_dim(
        power_sum, lax.axis_index(EXPERT) * panel_rows, panel_rows, 0
    )
    lower = jnp.linalg.cholesky(gram_total)
    new_basis = (
        math.sqrt(model_width) * jax.scipy.linalg.solve_triangular(lower, own_panel.T, lower=True).T
    )
    return (token_grads, projected_grads, new_basis)


def solution(mesh):
    finer = Mesh(
        mesh.devices.reshape(8, 4, 2, mesh.shape["replica"]),
        ("expert_0", "expert_1", "expert_2", "replica"),
    )
    placed = (
        P(EXPERT_REPLICA, None),
        P(EXPERT_REPLICA, None),
        P(EXPERT_REPLICA, None),
        P(EXPERT_REPLICA, None),
        P(EXPERT_REPLICA, None),
        P(EXPERT_REPLICA, None),
        P(EXPERT, None, None),
        P(EXPERT, None, None),
        P(EXPERT, None, None),
        P(EXPERT, None),
    )
    return jax.shard_map(
        body,
        mesh=finer,
        in_specs=placed,
        out_specs=(P(EXPERT_REPLICA, None), P(EXPERT, None, None, None), P(EXPERT, None)),
        check_vma=False,
    )
```

profile of v0, /device:TPU:2, one launch (start us, length us, event | category | flops | bytes accessed | tf_op | source)
XLA Modules:
  0.0 528.2 jit_solution(2570155433327698044)
XLA Ops:
  0.6 0.9 convert_element_type.89
  1.6 0.9 broadcast_in_dim.34
  2.4 11.7 %all-to-all-start.3 = ((bf16[32,32,256]{2,1,0:T(8,128)(2,1)}), bf16[32,32,256]{2,1,0:T(8,128)(2,1)}, u32[]{:S(2)}, u32[]{:S(2)}) async-start(bf16[32,32,256]{2,1,0:T(8,128)(2,1)} %broadcast_in_dim.34), calls=%async_computation.3 | async-start | bytes 1048576 | tf_op jit(solution)/shard_map/all_to_all | solution.py:15
  14.1 0.7 add_select_fusion.2
  15.0 1.9 concatenate.17
  16.9 0.6 compare_select_fusion
  17.5 4.3 scatter_custom_fusion
  21.9 10.0 %gather_fusion.2 = bf16[1024,2048]{1,0:T(8,128)(2,1)} fusion(bf16[129,2048]{1,0:T(8,128)(2,1)} %concatenate.17, s32[1024]{0:T(1024)S(1)} %get-tuple-element.36), kind=kCustom, calls=%fused_computation.2 | custom fusion | bytes 8392704 | tf_op jit(solution)/shard_map/gather | solution.py:95
  31.9 1.2 broadcast_in_dim.35
  33.0 5.4 %all_to_all.50 = bf16[2,32,32,256]{3,2,1,0:T(8,128)(2,1)} all-to-all(bf16[2,32,32,256]{3,2,1,0:T(8,128)(2,1)S(1)} %broadcast_in_dim.35), channel_id=1, replica_groups=mesh['expert_0'=8,'expert_1'=4,'expert_2'=2,'replica'=4] {'expert_2'}, dimensions={0} | all-to-all | bytes 2097152 | tf_op jit(solution)/shard_map/all_to_all | solution.py:15
  38.4 10.4 %all-to-all-start.1 = ((bf16[64,16,2048]{2,1,0:T(8,128)(2,1)}), bf16[64,16,2048]{2,1,0:T(8,128)(2,1)}, u32[]{:S(2)}, u32[]{:S(2)}) async-start(bf16[64,16,2048]{2,1,0:T(8,128)(2,1)} %bitcast.211), calls=%async_computation.1 | async-start | bytes 8388608 | tf_op jit(solution)/shard_map/all_to_all | solution.py:105
  48.8 1.9 concatenate.15
  50.7 10.0 %gather_fusion = bf16[1024,2048]{1,0:T(8,128)(2,1)} fusion(bf16[129,2048]{1,0:T(8,128)(2,1)} %concatenate.15, s32[1024]{0:T(1024)S(1)} %get-tuple-element.36), kind=kCustom, calls=%fused_computation | custom fusion | bytes 8392704 | tf_op jit(solution)/shard_map/gather | solution.py:96
  60.9 6.2 %gather_fusion.1 = f32[1024]{0:T(1024)S(1)} fusion(f32[1025]{0:T(1024)S(1)} %pad_maximum_fusion.1, s32[1024]{0:T(1024)S(1)} %get-tuple-element.35), kind=kCustom, calls=%fused_computation.1 | custom fusion | bytes 12288 | tf_op jit(solution)/shard_map/gather | solution.py:96
  67.1 4.9 fusion
  72.0 72.9 %all-to-all-done.1 = bf16[64,16,2048]{2,1,0:T(8,128)(2,1)} async-done(((bf16[64,16,2048]{2,1,0:T(8,128)(2,1)}), bf16[64,16,2048]{2,1,0:T(8,128)(2,1)}, u32[]{:S(2)}, u32[]{:S(2)}) %all-to-all-start.1) | async-done | bytes 4194336 | tf_op jit(solution)/shard_map/all_to_all | solution.py:105
  144.9 6.4 %all-to-all-start = ((bf16[64,16,2048]{2,1,0:T(8,128)(2,1)}), bf16[64,16,2048]{2,1,0:T(8,128)(2,1)}, u32[]{:S(2)}, u32[]{:S(2)}) async-start(bf16[64,16,2048]{2,1,0:T(8,128)(2,1)} %fusion), calls=%async_computation | async-start | bytes 8388608 | tf_op jit(solution)/shard_map/all_to_all | solution.py:124
  151.2 1.5 fusion.48
  152.9 1.0 copy-done.7
  153.9 4.5 convolution_convert_fusion.2
  158.4 5.7 %fusion.8 = f32[2,64,8,384]{3,2,1,0:T(8,128)} fusion(bf16[2,2048,384]{2,1,0:T(8,128)(2,1)S(1)} %copy-done.5, bf16[64,16,2048]{2,1,0:T(8,128)(2,1)} %all-to-all-done.1), kind=kOutput, calls=%fused_computation.20 | convolution fusion | flops 1610612736 | bytes 8912896 | tf_op jit(solution)/shard_map/sjcd,jdf->sjcf/dot_general | solution.py:107
  164.1 83.2 %all-to-all-done = bf16[64,16,2048]{2,1,0:T(8,128)(2,1)} async-done(((bf16[64,16,2048]{2,1,0:T(8,128)(2,1)}), bf16[64,16,2048]{2,1,0:T(8,128)(2,1)}, u32[]{:S(2)}, u32[]{:S(2)}) %all-to-all-start) | async-done | bytes 4194336 | tf_op jit(solution)/shard_map/all_to_all | solution.py:124
  247.2 5.6 %fusion.3 = f32[2,64,8,384]{3,2,1,0:T(8,128)S(1)} fusion(bf16[2,384,2048]{2,1,0:T(8,128)(2,1)} %param.18, bf16[64,16,2048]{2,1,0:T(8,128)(2,1)} %all-to-all-done), kind=kOutput, calls=%fused_computation.15 | convolution fusion | flops 1610612736 | bytes 8912896 | tf_op jit(solution)/shard_map/sjcd,jfd->sjcf/dot_general | solution.py:126
  252.9 5.1 fusion.37
  258.9 0.8 copy-done.8
  259.8 3.4 convolution_convert_fusion.1
  264.4 56.7 %all_to_all.51 = bf16[4,2,3,384,256]{4,3,2,1,0:T(8,128)(2,1)S(1)} all-to-all(bf16[4,2,3,384,256]{4,3,2,1,0:T(8,128)(2,1)S(1)} %broadcast_in_dim.36), channel_id=1, replica_groups=mesh['expert_0'=8,'expert_1'=4,'expert_2'=2,'replica'=4] {'replica'}, dimensions={0} | all-to-all | bytes 9437184 | tf_op jit(solution)/shard_map/all_to_all | solution.py:15
  321.0 0.8 convert_reduce_fusion
  323.2 4.0 fusion.18
  327.3 4.1 fusion.27
  331.5 18.4 %all_to_all.52 = bf16[8,32,8,256]{3,2,1,0:T(8,128)(2,1)} all-to-all(bf16[8,32,8,256]{3,2,1,0:T(8,128)(2,1)S(1)} %bitcast.214), channel_id=1, replica_groups=mesh['expert_0'=8,'expert_1'=4,'expert_2'=2,'replica'=4] {'expert_2','re..., dimensions={0} | all-to-all | bytes 2097152 | tf_op jit(solution)/shard_map/all_to_all | solution.py:46
  349.9 1.4 reduce_sum.47
  351.2 16.2 %all_to_all.53 = bf16[32,8,256]{2,1,0:T(8,128)(2,1)S(1)} all-to-all(bf16[32,8,256]{2,1,0:T(8,128)(2,1)S(1)} %reduce_sum.47), channel_id=1, replica_groups=mesh['expert_0'=8,'expert_1'=4,'expert_2'=2,'replica'=4] {'expert_0','ex..., dimensions={0} | all-to-all | bytes 262144 | tf_op jit(solution)/shard_map/all_to_all | solution.py:54
  367.5 13.9 %all_to_all.54 = bf16[32,8,256]{2,1,0:T(8,128)(2,1)S(1)} all-to-all(bf16[32,8,256]{2,1,0:T(8,128)(2,1)S(1)} %broadcast_in_dim.37), channel_id=1, replica_groups=mesh['expert_0'=8,'expert_1'=4,'expert_2'=2,'replica'=4] {'expert_0','ex..., dimensions={0} | all-to-all | bytes 262144 | tf_op jit(solution)/shard_map/all_to_all | solution.py:15
  381.5 1.1 broadcast_in_dim.38
  382.6 4.3 all-to-all-start.9
  386.9 4.6 fusion.12
  391.5 2.5 fusion.5
  393.9 2.2 copy.144
  396.2 6.0 %all-to-all-done.9 = bf16[8,32,8,256]{3,1,2,0:T(8,128)(2,1)} async-done(((bf16[8,32,8,256]{3,1,2,0:T(8,128)(2,1)}), bf16[8,32,8,256]{3,1,2,0:T(8,128)(2,1)}, u32[]{:S(2)}, u32[]{:S(2)}) %all-to-all-start.9) | async-done | bytes 1048608 | tf_op jit(solution)/shard_map/all_to_all | solution.py:15
  402.1 7.4 %all-to-all-start.2 = ((bf16[64,16,2048]{2,1,0:T(8,128)(2,1)}), bf16[64,16,2048]{2,1,0:T(8,128)(2,1)}, u32[]{:S(2)}, u32[]{:S(2)}) async-start(bf16[64,16,2048]{2,1,0:T(8,128)(2,1)} %bitcast.213), calls=%async_computation.2 | async-start | bytes 8388608 | tf_op jit(solution)/shard_map/all_to_all | solution.py:140
  409.6 2.1 convolution_bitcast_fusion.3
  411.7 0.8 copy.83
  412.6 1.0 fusion.58
  413.6 0.7 copy-done.9
  414.3 11.7 %cholesky.50 = f32[128,128]{1,0:T(8,128)S(1)} custom-call(f32[128,128]{1,0:T(8,128)S(1)} %cholesky.118), custom_call_target="Cholesky" | custom-call | tf_op jit(solution)/shard_map/jit(cholesky)/cholesky | solution.py:186
  426.0 9.8 %custom-call.15 = f32[1,128,128]{1,2,0:T(8,128)S(1)} custom-call(f32[1,128,128]{2,1,0:T(8,128)S(1)} %get-tuple-element.32), custom_call_target="InvertDiagBlocksLowerTriangular" | custom-call | tf_op jit(solution)/shard_map/jit(cholesky)/cholesky | solution.py:186
  435.8 1.0 constant_dynamic-update-slice_fusion.1
  436.9 1.1 convolution_subtract_fusion
  438.0 11.7 %cholesky.105 = f32[128,128]{1,0:T(8,128)S(1)} custom-call(f32[128,128]{1,0:T(8,128)S(1)} %convolution_subtract_fusion), custom_call_target="Cholesky" | custom-call | tf_op jit(solution)/shard_map/jit(cholesky)/cholesky | solution.py:186
  449.8 0.6 compare_reduce_fusion
  451.6 1.0 select_select_fusion
  452.7 5.2 while.1
  452.7 0.6 fusion.97
  453.3 2.0 bitcast_dynamic-update-slice_fusion.2
  455.3 0.6 fusion.97
  455.9 2.0 bitcast_dynamic-update-slice_fusion.2
  457.9 20.7 %custom-call.16 = f32[2,128,128]{1,2,0:T(8,128)S(1)} custom-call(f32[2,128,128]{2,1,0:T(8,128)} %get-tuple-element.10), custom_call_target="InvertDiagBlocksLowerTriangular" | custom-call | tf_op jit(solution)/shard_map/jit(_solve_triangular)/triangular_solve | solution.py:188
  478.6 1.8 copy.84
  481.0 0.6 fusion.65
  481.6 23.9 %all-to-all-done.2 = bf16[64,16,2048]{2,1,0:T(8,128)(2,1)} async-done(((bf16[64,16,2048]{2,1,0:T(8,128)(2,1)}), bf16[64,16,2048]{2,1,0:T(8,128)(2,1)}, u32[]{:S(2)}, u32[]{:S(2)}) %all-to-all-start.2) | async-done | bytes 4194336 | tf_op jit(solution)/shard_map/all_to_all | solution.py:140
  505.6 4.7 concatenate.18
  510.3 11.6 %gather_fusion.3 = bf16[1024,2048]{1,0:T(8,128)(2,1)} fusion(bf16[1025,2048]{1,0:T(8,128)(2,1)} %concatenate.18, s32[1024]{0:T(1024)S(1)} %broadcast_clamp_fusion), kind=kCustom, calls=%fused_computation.3 | custom fusion | bytes 8392704 | tf_op jit(solution)/shard_map/gather | solution.py:145
  521.9 5.9 %bitcast_reduce_fusion = bf16[128,2048]{1,0:T(8,128)(2,1)} fusion(bf16[1024,2048]{1,0:T(8,128)(2,1)} %gather_fusion.3), kind=kLoop, calls=%fused_computation.11 | loop fusion | flops 1835008 | bytes 4718592 | tf_op jit(solution)/shard_map/reduce_sum | solution.py:144
  (62 shorter events, 4.9 us)
Async XLA Ops:
  0.6 252.2 %copy-start = (bf16[2,2048,384]{2,1,0:T(8,128)(2,1)S(1)}, bf16[2,2048,384]{2,1,0:T(8,128)(2,1)}, u32[]{:S(2)}) copy-start(bf16[2,2048,384]{2,1,0:T(8,128)(2,1)} %param.17) | copy-start | bytes 9437188
  2.4 29.4 %all-to-all-start.3 = ((bf16[32,32,256]{2,1,0:T(8,128)(2,1)}), bf16[32,32,256]{2,1,0:T(8,128)(2,1)}, u32[]{:S(2)}, u32[]{:S(2)}) async-start(bf16[32,32,256]{2,1,0:T(8,128)(2,1)} %broadcast_in_dim.34), calls=%async_computation.3 | async-start | bytes 1048576 | tf_op jit(solution)/shard_map/all_to_all | solution.py:15
  38.4 106.5 %all-to-all-start.1 = ((bf16[64,16,2048]{2,1,0:T(8,128)(2,1)}), bf16[64,16,2048]{2,1,0:T(8,128)(2,1)}, u32[]{:S(2)}, u32[]{:S(2)}) async-start(bf16[64,16,2048]{2,1,0:T(8,128)(2,1)} %bitcast.211), calls=%async_computation.1 | async-start | bytes 8388608 | tf_op jit(solution)/shard_map/all_to_all | solution.py:105
  50.7 10.0 %copy-start.11 = (f32[128,8]{0,1:T(8,128)S(1)}, f32[128,8]{0,1:T(8,128)}, u32[]{:S(2)}) copy-start(f32[128,8]{0,1:T(8,128)} %param.12) | copy-start | bytes 12292
  144.9 102.4 %all-to-all-start = ((bf16[64,16,2048]{2,1,0:T(8,128)(2,1)}), bf16[64,16,2048]{2,1,0:T(8,128)(2,1)}, u32[]{:S(2)}, u32[]{:S(2)}) async-start(bf16[64,16,2048]{2,1,0:T(8,128)(2,1)} %fusion), calls=%async_computation | async-start | bytes 8388608 | tf_op jit(solution)/shard_map/all_to_all | solution.py:124
  152.8 1.0 copy-start.7
  152.9 5.6 %copy-start.5 = (bf16[2,2048,384]{2,1,0:T(8,128)(2,1)S(1)}, bf16[2,2048,384]{2,1,0:T(8,128)(2,1)}, u32[]{:S(2)}) copy-start(bf16[2,2048,384]{2,1,0:T(8,128)(2,1)} %param.16) | copy-start | bytes 9437188
  247.2 5.6 %copy-start.12 = (f32[2,64,8,384]{3,2,1,0:T(8,128)S(1)}, f32[2,64,8,384]{3,2,1,0:T(8,128)}, u32[]{:S(2)}) copy-start(f32[2,64,8,384]{3,2,1,0:T(8,128)} %fusion.8) | copy-start | bytes 4718596
  252.9 5.2 copy-start.13
  258.0 63.9 %copy-start.4 = (bf16[64,2,8,384]{3,2,0,1:T(8,128)(2,1)}, bf16[64,2,8,384]{3,2,0,1:T(8,128)(2,1)S(1)}, u32[]{:S(2)}) copy-start(bf16[64,2,8,384]{3,2,0,1:T(8,128)(2,1)S(1)} %get-tuple-element.25) | copy-start | bytes 2359300
  258.0 64.8 %copy-start.2 = (bf16[64,2,8,384]{3,2,0,1:T(8,128)(2,1)}, bf16[64,2,8,384]{3,2,0,1:T(8,128)(2,1)S(1)}, u32[]{:S(2)}) copy-start(bf16[64,2,8,384]{3,2,0,1:T(8,128)(2,1)S(1)} %get-tuple-element.26) | copy-start | bytes 2359300
  258.5 1.3 copy-start.8
  321.9 5.4 %copy-start.1 = (f32[2,3,384,256]{3,2,1,0:T(8,128)}, f32[2,3,384,256]{3,2,1,0:T(8,128)S(1)}, u32[]{:S(2)}) copy-start(f32[2,3,384,256]{3,2,1,0:T(8,128)S(1)} %convert_reduce_fusion) | copy-start | bytes 7077892
  382.6 19.5 %all-to-all-start.9 = ((bf16[8,32,8,256]{3,1,2,0:T(8,128)(2,1)}), bf16[8,32,8,256]{3,1,2,0:T(8,128)(2,1)}, u32[]{:S(2)}, u32[]{:S(2)}) async-start(bf16[8,32,8,256]{3,1,2,0:T(8,128)(2,1)} %broadcast_in_dim.38), calls=%async_computation.9 | async-start | bytes 2097152 | tf_op jit(solution)/shard_map/all_to_all | solution.py:15
  386.9 4.6 copy-start.3
  402.1 7.5 %copy-start.10 = (s32[1024,1]{0,1:T(1,128)S(1)}, s32[1024,1]{0,1:T(1,128)}, u32[]{:S(2)}) copy-start(s32[1024,1]{0,1:T(1,128)} %get-tuple-element.33) | copy-start | bytes 12292
  402.1 103.4 %all-to-all-start.2 = ((bf16[64,16,2048]{2,1,0:T(8,128)(2,1)}), bf16[64,16,2048]{2,1,0:T(8,128)(2,1)}, u32[]{:S(2)}, u32[]{:S(2)}) async-start(bf16[64,16,2048]{2,1,0:T(8,128)(2,1)} %bitcast.213), calls=%async_computation.2 | async-start | bytes 8388608 | tf_op jit(solution)/shard_map/all_to_all | solution.py:140
  413.5 0.7 copy-start.9
  449.8 1.9 copy-start.6
where the time goes:
time: 535 us; the launch traced here: 528 us
  waiting for transfers between devices  186 us (35%)
  blocking collectives  111 us (21%)
  other arithmetic  74.1 us (14%)
  local copies, waits for them, and re-layouts  67.7 us (13%)
  matrix products  46.9 us (9%)
  starting transfers between devices  40.1 us (7%)
    all_to_all x1, waiting for transfers between devices, body(): lax.all_to_all(dy_send, EXPERT, split_axis=0, concat_axis=0, tiled=True)  83.2 us
    all_to_all x3, blocking collectives, from_everyone(): return lax.all_to_all(copies, axis, split_axis=0, concat_axis=0, tiled=True)  76 us
    all_to_all x1, waiting for transfers between devices, body(): lax.all_to_all(x_send, EXPERT, split_axis=0, concat_axis=0, tiled=True)  72.9 us
    another operation x6, other arithmetic, body(): lower = jnp.linalg.cholesky(gram_total)  33.9 us
    all_to_all x1, waiting for transfers between devices, body(): lax.all_to_all(row_grads, EXPERT, split_axis=0, concat_axis=0, tiled=True)  23.9 us
    another operation x3, other arithmetic, body(): jax.scipy.linalg.solve_triangular(lower, own_panel.T, lower=True)  21.7 us
    all_to_all x1, blocking collectives, sent_and_summed(): lax.all_to_all(pieces, axis, split_axis=0, concat_axis=0, tiled=True)  18.4 us
    all_to_all x1, blocking collectives, sum_by_axis(): lax.all_to_all(own.astype(jnp.bfloat16), far, 0, 0, tiled=True)  16.2 us
  transfers between devices with their start and end apart: 5, of which 4 were waited for; matrix products, arithmetic and copies ran while one was open for 25% of the time, Pallas kernels for 0%

commit v1 on v0

v1 whole, which is shorter than its diff:
```python
import math

import jax
import jax.numpy as jnp
from jax import lax
from jax.experimental import pallas as pl
from jax.experimental.pallas import tpu as pltpu
from jax.sharding import Mesh
from jax.sharding import PartitionSpec as P

Z, X, C, Y = "expert_0", "expert_1", "expert_2", "replica"
EXPERT = (Z, X, C)
EXPERT_REPLICA = (Z, X, C, Y)
PLANE = (X, C)
PAIR = 2
RADIX = 256
DROPPED = 255 * RADIX
SHIFT = float(1 << 17)
SIDE = 128
BLOCK = 64


f32, bf16 = jnp.float32, jnp.bfloat16


def dot(a, b, over=((1,), (0,)), precision=None):
    return lax.dot_general(a, b, (over, ((), ())), precision=precision, preferred_element_type=f32)


def cost(flops, nbytes):
    return pl.CostEstimate(flops=int(flops), bytes_accessed=int(nbytes), transcendentals=0)


def from_everyone(array, axis):
    copies = jnp.broadcast_to(array, (lax.axis_size(axis), *array.shape))
    return lax.all_to_all(copies, axis, split_axis=0, concat_axis=0, tiled=True)


def sent_and_summed(lines, axis):
    devices = lax.axis_size(axis)
    pieces = lines.reshape(devices, -1, lines.shape[-1])
    arrived = lax.all_to_all(pieces, axis, split_axis=0, concat_axis=0, tiled=True)
    return arrived.astype(f32).sum(axis=0).astype(bf16)


def gathered(lines, axis):
    return from_everyone(lines, axis).reshape(-1, lines.shape[-1])


def packed_body(cap, tokens, expert_ids, slot_ids, kept_mask, route_weights, out):
    width = tokens.shape[1]
    target = jnp.where(kept_mask[...] > 0, expert_ids[...] * cap + slot_ids[...], DROPPED)
    weight = route_weights[...]
    first = weight.astype(bf16)
    rest = weight - first.astype(f32)
    second = rest.astype(bf16)
    third = (rest - second.astype(f32)).astype(bf16)
    digits = [(target // RADIX).astype(f32), (target % RADIX).astype(f32)]
    parts = digits + [first.astype(f32), second.astype(f32), third.astype(f32)]
    top = target.shape[1]
    spare = jnp.zeros((target.shape[0], SIDE - len(parts) * top), f32)
    out[:, :width] = tokens[...]
    out[:, width:] = jnp.concatenate(parts + [spare], 1).astype(bf16)


def packed(tokens, half, cap, *routing):
    count, top = routing[0].shape
    small = pl.BlockSpec((count, top), lambda i: (0, 0))
    return pl.pallas_call(
        lambda *refs: packed_body(cap, *refs),
        out_shape=jax.ShapeDtypeStruct((count, half + SIDE), bf16),
        grid=(1,),
        in_specs=[pl.BlockSpec((count, half), lambda i: (0, 0))] + [small] * len(routing),
        out_specs=pl.BlockSpec((count, half + SIDE), lambda i: (0, 0)),
        cost_estimate=cost(1e6, 6e5),
        name="packed",
    )(tokens, *routing)


def want_slots(shape, dim, base, block_of):
    slot = lax.broadcasted_iota(jnp.int32, shape, dim)
    place, source = slot & 7, (slot >> 3) & 1
    return (base + block_of(slot >> 4) * 8 + place).astype(f32) + SHIFT * source.astype(f32)


def keys_of(routes, top, dim):
    for k in range(top):
        take = (lambda n: routes[n : n + 1, :]) if dim == 1 else (lambda n: routes[:, n : n + 1])
        key = take(k) * RADIX + take(top + k)
        token = lax.broadcasted_iota(jnp.int32, key.shape, dim)
        half = routes.shape[dim] // PAIR
        yield k, key + SHIFT * (token // half).astype(f32)


def pick_body(top, scaled, base_ref, routes_ref, rows_ref, out_ref):
    slots = rows_ref.shape[0]
    routes = routes_ref[...].astype(f32).T
    want = want_slots((slots, slots), 0, base_ref[0], lambda block: block)
    chosen = jnp.zeros((slots, slots), f32)
    scale = jnp.zeros((slots, slots), f32)
    for k, key in keys_of(routes, top, 1):
        hit = key == want
        chosen = jnp.where(hit, 1.0, chosen)
        if scaled:
            part = lambda n: routes[n * top + k : n * top + k + 1, :]
            scale = jnp.where(hit, part(2) + part(3) + part(4), scale)
    picked = dot(chosen.astype(bf16), rows_ref[...])
    if scaled:
        picked = picked * jnp.sum(scale, axis=1, keepdims=True)
    out_ref[...] = picked.astype(bf16).reshape(out_ref.shape)


def pick(base, routed, rows, width, top, scaled, devices, experts, cap):
    slots = devices * experts * cap * PAIR
    steps = rows.shape[0] // slots
    return pl.pallas_call(
        lambda *refs: pick_body(top, scaled, *refs),
        out_shape=jax.ShapeDtypeStruct((devices, experts, steps * PAIR * cap, width), bf16),
        grid_spec=pltpu.PrefetchScalarGridSpec(
            num_scalar_prefetch=1,
            grid=(steps,),
            in_specs=[
                pl.BlockSpec((slots, SIDE), lambda i, b: (i, width // SIDE)),
                pl.BlockSpec((slots, width), lambda i, b: (i, 0)),
            ],
            out_specs=pl.BlockSpec(
                (devices, experts, PAIR * cap, width), lambda i, b: (0, 0, i, 0)
            ),
        ),
        cost_estimate=cost(2 * slots * slots * width * steps, 4 * slots * width * steps),
        name="pick_scaled" if scaled else "pick",
    )(base, routed, rows)


def give_back_body(top, base_ref, routes_ref, *refs):
    *row_refs, out_ref = refs
    slots = out_ref.shape[0]
    devices = len(row_refs)
    routes = routes_ref[...].astype(f32)
    here = base_ref[1]

    def block_of(block):
        return ((here - (block >> 1)) & (devices - 1)) * 2 + (block & 1)

    want = want_slots((slots, slots), 1, base_ref[0], block_of)
    chosen = jnp.zeros((slots, slots), f32)
    for _, key in keys_of(routes, top, 0):
        chosen = jnp.where(key == want, 1.0, chosen)
    width = out_ref.shape[1]
    rows = jnp.concatenate([r[...].reshape(slots // devices, width) for r in row_refs], 0)
    out_ref[...] = dot(chosen.astype(bf16), rows).astype(bf16)


def give_back(base, routed, pieces, top, cap):
    experts, all_rows, width = pieces[0].shape
    steps = all_rows // (PAIR * cap)
    slots = len(pieces) * experts * PAIR * cap
    return pl.pallas_call(
        lambda *refs: give_back_body(top, *refs),
        out_shape=jax.ShapeDtypeStruct((steps * slots, width), bf16),
        grid_spec=pltpu.PrefetchScalarGridSpec(
            num_scalar_prefetch=1,
            grid=(steps,),
            in_specs=[pl.BlockSpec((slots, SIDE), lambda i, b: (i, width // SIDE))]
            + [pl.BlockSpec((experts, PAIR * cap, width), lambda i, b: (0, i, 0))] * len(pieces),
            out_specs=pl.BlockSpec((slots, width), lambda i, b: (i, 0)),
        ),
        cost_estimate=cost(2 * slots * slots * width * steps, 4 * slots * width * steps),
        name="give_back",
    )(base, routed, *pieces)


def flat(ref):
    value = ref[...]
    return value.reshape(-1, value.shape[-1])


def forward_body(x0, x1, gate_w, up_w, proj, act, slope_up, hidden, x_proj):
    half = x0.shape[-1]
    rows = (flat(x0), flat(x1))

    def times(weight):
        return dot(rows[0], weight[:half]) + dot(rows[1], weight[half:])

    gate, upper = times(gate_w[0]), times(up_w[0])
    sigma = jax.nn.sigmoid(gate)
    activated = gate * sigma
    act[0] = activated
    slope_up[0] = upper * (sigma * (1.0 + gate * (1.0 - sigma)))
    hidden[0] = (activated * upper).astype(bf16)
    x_proj[0] = times(proj).astype(bf16)


def forward(x0, x1, gate_w, up_w, proj):
    plane, experts, depth, half = x0.shape
    width, hid = gate_w.shape[1:]
    rank = proj.shape[1]
    rows = plane * depth
    part = plane // 2
    row_spec = pl.BlockSpec((part, 1, depth, half), lambda j, s: (s, j, 0, 0))
    weight = pl.BlockSpec((1, width, hid), lambda j, s: (j, 0, 0))
    out = lambda n: pl.BlockSpec((1, part * depth, n), lambda j, s: (j, s, 0))
    shape = lambda n, t: jax.ShapeDtypeStruct((experts, rows, n), t)
    return pl.pallas_call(
        forward_body,
        out_shape=(shape(hid, f32), shape(hid, f32), shape(hid, bf16), shape(rank, bf16)),
        grid=(experts, 2),
        in_specs=[row_spec] * 2 + [weight] * 2 + [pl.BlockSpec((width, rank), lambda j, s: (0, 0))],
        out_specs=(out(hid), out(hid), out(hid), out(rank)),
        cost_estimate=cost(2 * experts * rows * width * (2 * hid + rank), 16e6),
        name="forward",
    )(x0, x1, gate_w, up_w, proj)


def first_half_body(dy, down_w, proj, hidden_grad, dy_proj):
    rows = flat(dy)
    hidden_grad[0] = dot(rows, down_w[0], ((1,), (1,)))
    dy_proj[0] = dot(rows, proj[...])


def first_half(dy, down_w, proj):
    plane, experts, depth, half = dy.shape
    hid, rank = down_w.shape[1], proj.shape[1]
    rows = plane * depth
    out = lambda n: pl.BlockSpec((1, rows, n), lambda j: (j, 0, 0))
    return pl.pallas_call(
        first_half_body,
        out_shape=tuple(jax.ShapeDtypeStruct((experts, rows, n), f32) for n in (hid, rank)),
        grid=(experts,),
        in_specs=[
            pl.BlockSpec((plane, 1, depth, half), lambda j: (0, j, 0, 0)),
            pl.BlockSpec((1, hid, half), lambda j: (j, 0, 0)),
            pl.BlockSpec((half, rank), lambda j: (0, 0)),
        ],
        out_specs=(out(hid), out(rank)),
        cost_estimate=cost(2 * experts * rows * half * (hid + rank), 8e6),
        name="first_half",
    )(dy, down_w, proj)


def backward_body(
    dy, down_w, proj, hidden_part, proj_part, act, slope_up, hidden, x_proj, gate_grad, up_grad, grads
):
    rows = flat(dy)
    hidden_grad = hidden_part[0] + dot(rows, down_w[0], ((1,), (1,)))
    dy_proj = (proj_part[0] + dot(rows, proj[...])).astype(bf16)
    of_up = (hidden_grad * act[0]).astype(bf16)
    of_gate = (hidden_grad * slope_up[0]).astype(bf16)
    up_grad[0] = of_up
    gate_grad[0] = of_gate
    over = ((0,), (0,))
    grads[0, 0] = dot(of_gate, x_proj[0], over).astype(bf16)
    grads[0, 1] = dot(of_up, x_proj[0], over).astype(bf16)
    grads[0, 2] = dot(hidden[0], dy_proj, over).astype(bf16)


def backward(dy, down_w, proj, hidden_part, proj_part, act, slope_up, hidden, x_proj):
    plane, experts, depth, half = dy.shape
    hid, rank = down_w.shape[1], proj.shape[1]
    rows = plane * depth
    mat = lambda n: pl.BlockSpec((1, rows, n), lambda j: (j, 0, 0))
    shape = jax.ShapeDtypeStruct((experts, rows, hid), bf16)
    return pl.pallas_call(
        backward_body,
        out_shape=(shape, shape, jax.ShapeDtypeStruct((experts, 3, hid, rank), bf16)),
        grid=(experts,),
        in_specs=[
            pl.BlockSpec((plane, 1, depth, half), lambda j: (0, j, 0, 0)),
            pl.BlockSpec((1, hid, half), lambda j: (j, 0, 1)),
            pl.BlockSpec((half, rank), lambda j: (1, 0)),
            mat(hid), mat(rank), mat(hid), mat(hid), mat(hid), mat(rank),
        ],
        out_specs=(mat(hid), mat(hid), pl.BlockSpec((1, 3, hid, rank), lambda j: (j, 0, 0, 0))),
        cost_estimate=cost(2 * experts * rows * (half * (hid + rank) + 3 * hid * rank), 12e6),
        name="backward",
    )(dy, down_w, proj, hidden_part, proj_part, act, slope_up, hidden, x_proj)


def row_grads_body(gate_grad, up_grad, gate_w, up_w, out0, out1):
    half = out0.shape[-1]
    over = ((1,), (1,))
    for n, out in enumerate((out0, out1)):
        part = slice(n * half, (n + 1) * half)
        value = dot(gate_grad[0], gate_w[0, part], over) + dot(up_grad[0], up_w[0, part], over)
        out[...] = value.astype(bf16).reshape(out.shape)


def row_grads_of(gate_grad, up_grad, gate_w, up_w, plane):
    experts, rows, hid = gate_grad.shape
    width = gate_w.shape[1]
    depth, part = rows // plane, plane // 2
    mat = pl.BlockSpec((1, rows // 2, hid), lambda j, s: (j, s, 0))
    weight = pl.BlockSpec((1, width, hid), lambda j, s: (j, 0, 0))
    shape = jax.ShapeDtypeStruct((plane, experts, depth, width // 2), bf16)
    return pl.pallas_call(
        row_grads_body,
        out_shape=(shape, shape),
        grid=(experts, 2),
        in_specs=[mat, mat, weight, weight],
        out_specs=[pl.BlockSpec((part, 1, depth, width // 2), lambda j, s: (s, j, 0, 0))] * 2,
        cost_estimate=cost(4 * experts * rows * width * hid, 12e6),
        name="row_grads",
    )(gate_grad, up_grad, gate_w, up_w)


def weight_grads_body(x0, x1, dy0, dy1, gate_grad, up_grad, hidden, out):
    half, hid = x0.shape[-1], hidden.shape[-1]
    over = ((0,), (0,))
    for n, (x, dy) in enumerate(((x0, dy0), (x1, dy1))):
        part = pl.ds(n * half, half)
        out[part, 0:hid] = dot(flat(x), gate_grad[0], over).astype(bf16)
        out[part, hid : 2 * hid] = dot(flat(x), up_grad[0], over).astype(bf16)
        out[part, 2 * hid : 3 * hid] = dot(flat(dy), hidden[0], over).astype(bf16)


def weight_grads(x0, x1, dy0, dy1, gate_grad, up_grad, hidden):
    plane, experts, depth, half = x0.shape
    rows, hid = plane * depth, hidden.shape[2]
    row_spec = pl.BlockSpec((plane, 1, depth, half), lambda j: (0, j, 0, 0))
    mat = pl.BlockSpec((1, rows, hid), lambda j: (j, 0, 0))
    return pl.pallas_call(
        weight_grads_body,
        out_shape=jax.ShapeDtypeStruct((2 * half, 3 * hid * experts), bf16),
        grid=(experts,),
        in_specs=[row_spec] * 4 + [mat] * 3,
        out_specs=pl.BlockSpec((2 * half, 3 * hid), lambda j: (0, j)),
        cost_estimate=cost(12 * experts * rows * half * hid, 24e6),
        name="weight_grads",
    )(x0, x1, dy0, dy1, gate_grad, up_grad, hidden)


def inverse_factor(square):
    size = square.shape[0]
    row = lax.broadcasted_iota(jnp.int32, (size, 2 * size), 0)
    lane = lax.broadcasted_iota(jnp.int32, (size, 2 * size), 1)
    work = jnp.concatenate([square, jnp.zeros_like(square)], 1)
    work = jnp.where(lane == row + size, 1.0, work)
    groups = [work[g : g + 8] for g in range(0, size, 8)]
    scales = [jnp.zeros((8, 2 * size), f32) for _ in groups]
    inner = lax.broadcasted_iota(jnp.int32, (8, 2 * size), 0)
    for j in range(size):
        g, at = divmod(j, 8)
        spread = [jnp.broadcast_to(w[:, j : j + 1], (8, 2 * size)) for w in groups[g:]]
        pivot = spread[0][at : at + 1]
        line = groups[g][at : at + 1]
        scales[g] = jnp.where(inner == at, lax.rsqrt(pivot), scales[g])
        line = line / pivot
        factor = jnp.where(inner > at, spread[0], 0.0)
        groups[g] = groups[g] - factor * line
        for n in range(g + 1, len(groups)):
            groups[n] = groups[n] - spread[n - g] * line
    return jnp.concatenate([w * s for w, s in zip(groups, scales)], 0)


def new_basis_body(scale, index_ref, power, own, out, gram, side, solved):
    size = power.shape[1]
    exact = lax.Precision.HIGHEST
    over = ((0,), (0,))
    gram[...] = dot(power[...], power[...], over)
    panel = own[...].astype(f32)
    spare = jnp.zeros((SIDE - panel.shape[0], size), f32)
    side[...] = jnp.concatenate([panel, spare], 0).T

    def step(k, _):
        head = gram[0:BLOCK]
        factor = inverse_factor(head[:, 0:BLOCK])
        none = jnp.zeros_like(head)
        lines = dot(factor, jnp.concatenate([none, head], 0), precision=exact)
        head = side[0:BLOCK]
        answer = dot(factor, jnp.concatenate([jnp.zeros_like(head), head], 0), precision=exact)
        solved[pl.ds(pl.multiple_of(k * BLOCK, BLOCK), BLOCK)] = answer
        lower = lines[:, BLOCK:]
        rest = gram[BLOCK:] - dot(lower, lines, over, exact)
        rest = jnp.concatenate([rest[:, BLOCK:], jnp.zeros((size - BLOCK, BLOCK), f32)], 1)
        gram[0 : size - BLOCK] = rest
        side[0 : size - BLOCK] = side[BLOCK:] - dot(lower, answer, over, exact)
        return 0

    lax.fori_loop(0, size // BLOCK, step, 0)
    out[...] = scale * solved[...].T[: out.shape[0]]


def new_basis_of(power, index, panel_rows):
    width, rank = power.shape
    return pl.pallas_call(
        lambda *refs: new_basis_body(math.sqrt(width), *refs),
        out_shape=jax.ShapeDtypeStruct((panel_rows, rank), f32),
        grid_spec=pltpu.PrefetchScalarGridSpec(
            num_scalar_prefetch=1,
            grid=(1,),
            in_specs=[
                pl.BlockSpec((width, rank), lambda i, n: (0, 0)),
                pl.BlockSpec((panel_rows, rank), lambda i, n: (n[0], 0)),
            ],
            out_specs=pl.BlockSpec((panel_rows, rank), lambda i, n: (0, 0)),
            scratch_shapes=[
                pltpu.VMEM((rank, rank), f32),
                pltpu.VMEM((rank, SIDE), f32),
                pltpu.VMEM((rank, SIDE), f32),
            ],
        ),
        cost_estimate=cost(3e10, 2e6),
        name="new_basis",
    )(index, power, power)


def layer(
    tokens,
    cotangent,
    route_weights,
    expert_ids,
    slot_ids,
    kept_mask,
    gate_weight,
    up_weight,
    down_weight,
    projector_basis,
):
    tok_count, model_width = tokens.shape
    half = model_width // 2
    top = expert_ids.shape[1]
    experts = gate_weight.shape[0]
    group_count = lax.axis_size(EXPERT)
    plane = lax.axis_size(PLANE)
    cap = tok_count * top // (experts * group_count)
    here = lax.axis_index(PLANE)
    base = jnp.stack([lax.axis_index(Z) * (plane * experts * cap), here]).astype(jnp.int32)

    first_rows = packed(tokens, half, cap, expert_ids, slot_ids, kept_mask, route_weights)

    def along_z(value):
        return lax.all_gather(value, Z, axis=0, tiled=True)

    def after(value, *earlier):
        return lax.optimization_barrier((value, *earlier))

    projector = (projector_basis * (1.0 / math.sqrt(model_width))).astype(bf16)
    projector = gathered(projector, (Z, X))
    pieces = from_everyone(projector, C)
    pieces = pieces.reshape(lax.axis_size(C), -1, *projector_basis.shape).swapaxes(0, 1)
    projector = pieces.reshape(model_width, -1)

    x0_all = along_z(first_rows)
    x1_in, x0_all, projector = after(tokens[:, half:], x0_all, projector)
    x1_all = along_z(x1_in)
    dy0_in, x1_all = after(cotangent[:, :half], x1_all)
    dy0_all = along_z(dy0_in)
    dy1_in, dy0_all = after(cotangent[:, half:], dy0_all)
    dy1_all = along_z(dy1_in)

    def sent(rows, scaled):
        picked = pick(base, x0_all, rows, half, top, scaled, plane, experts, cap)
        return lax.all_to_all(picked, PLANE, split_axis=0, concat_axis=0, tiled=True)

    x0, x1 = sent(x0_all, False), sent(x1_all, False)
    dy0, dy1 = sent(dy0_all, True), sent(dy1_all, True)

    act, slope_up, hidden, x_proj = forward(x0, x1, gate_weight, up_weight, projector)
    hidden_part, proj_part = first_half(dy0, down_weight, projector)
    gate_grad, up_grad, partial = backward(
        dy1, down_weight, projector, hidden_part, proj_part, act, slope_up, hidden, x_proj
    )

    own_grads = sent_and_summed(partial.reshape(-1, partial.shape[-1]), Y)
    grads_low = gathered(own_grads, Y)
    projected_grads = grads_low.astype(f32).reshape(partial.shape)

    returned = []
    halves = row_grads_of(gate_grad, up_grad, gate_weight, up_weight, plane)
    for rows in halves:
        pieces = []
        for d in range(plane):
            piece = lax.dynamic_index_in_dim(rows, (here + d) % plane, 0, keepdims=False)
            if d:
                piece = lax.ppermute(piece, PLANE, [(i, (i + d) % plane) for i in range(plane)])
            pieces.append(piece)
        returned.append(pieces)

    late_gate_grad, _ = after(gate_grad, own_grads)
    own_weight_grads = weight_grads(x0, x1, dy0, dy1, late_gate_grad, up_grad, hidden)
    near, far = (C, Y), (Z, X)
    power = dot(own_weight_grads, grads_low).astype(bf16)
    first_base, power = after(base, power)
    power = sent_and_summed(power, near)
    second_base, power = after(base, power)
    power = sent_and_summed(power, far)
    power = gathered(gathered(power, far), near)

    token_parts = []
    for when, pieces in zip((first_base, second_base), returned):
        token_parts.append(give_back(when, x0_all, pieces, top, cap))
    token_grads = jnp.concatenate(
        [lax.psum_scatter(part, Z, scatter_dimension=0, tiled=True) for part in token_parts], 1
    )

    index = lax.axis_index(EXPERT).astype(jnp.int32).reshape(1)
    new_basis = new_basis_of(power, index, model_width // group_count)
    return (token_grads, projected_grads, new_basis)


def solution(mesh):
    finer = Mesh(mesh.devices.reshape(8, 4, 2, mesh.shape["replica"]), EXPERT_REPLICA)
    rows = P(EXPERT_REPLICA, None)
    placed = (rows,) * 6 + (P(EXPERT, None, None),) * 3 + (P(EXPERT, None),)
    return jax.shard_map(
        layer,
        mesh=finer,
        in_specs=placed,
        out_specs=(rows, P(EXPERT, None, None, None), P(EXPERT, None)),
        check_vma=False,
    )
```

time: 535 us -> 450 us (0.84)
  Pallas kernels: 0 us -> 106 us
  blocking collectives: 111 us -> 19.4 us
  other arithmetic: 74.1 us -> 6.06 us
  local copies, waits for them, and re-layouts: 67.7 us -> 21.4 us
  matrix products: 46.9 us -> 7.27 us
  starting transfers between devices: 40.1 us -> 79.7 us
  between operations: 2.82 us -> 14.3 us
  waiting for transfers between devices: 186 us -> 192 us
    all_to_all x3 -> x7, waiting for transfers between devices: 180 us -> 67.2 us  [the longest x4 51 us: sent(): lax.all_to_all(picked, PLANE, split_axis=0, concat_axis=0, tiled=True)]
    pallas_call x0 -> x13, Pallas kernels: none -> 106 us  [the longest x1 26.7 us: new_basis_of(): pl.pallas_call(lambda *refs: new_basis_body(math.sqrt(width), *refs), out...]
    all_gather x0 -> x4, waiting for transfers between devices: none -> 82.4 us  [along_z(): return lax.all_gather(value, Z, axis=0, tiled=True)]
    all_to_all x3 -> x2, blocking collectives: 76 us -> 19.4 us  [from_everyone(): return lax.all_to_all(copies, axis, split_axis=0, concat_axis=0, tiled=True)]
    another operation x10 -> x1, other arithmetic: 55.8 us -> 0.65 us  [layer(): jnp.stack([lax.axis_index(Z) * (plane * experts * cap), here])]
    gather x4 -> x0, local copies, waits for them, and re-layouts: 37.7 us -> none  [the longest x1 11.6 us: body(): returned[target].reshape(tok_count, route_top, model_width)]
    dot_general x16 -> x1, matrix products: 44.2 us -> 7.27 us  [dot(): lax.dot_general(a, b, (over, ((), ())), precision=precision, preferred_el...]
    all_to_all x2 -> x0, blocking collectives: 34.6 us -> none  [the longest x1 18.4 us: sent_and_summed(): lax.all_to_all(pieces, axis, split_axis=0, concat_axis=0, tiled=True)]
  transfers between devices with their start and end apart: 5 -> 30, of which waited for: 4 -> 12; matrix products, arithmetic and copies ran while one was open for 25% -> 5% of each run, Pallas kernels for 0% -> 21%
where the time goes in v1:
time: 450 us; the launch traced here: 446 us
  waiting for transfers between devices  192 us (43%)
  Pallas kernels  106 us (24%)
  starting transfers between devices  79.7 us (18%)
  local copies, waits for them, and re-layouts  21.4 us (5%)
  blocking collectives  19.4 us (4%)
  between operations  14.3 us (3%)
  matrix products  7.27 us (2%)
  other arithmetic  6.06 us (1%)
    all_gather x4, waiting for transfers between devices, along_z(): return lax.all_gather(value, Z, axis=0, tiled=True)  82.4 us
    all_to_all x4, waiting for transfers between devices, sent(): lax.all_to_all(picked, PLANE, split_axis=0, concat_axis=0, tiled=True)  51 us
    all_to_all x3, waiting for transfers between devices, from_everyone(): return lax.all_to_all(copies, axis, split_axis=0, concat_axis=0, tiled=True)  35.2 us
    pallas_call x1, Pallas kernels, new_basis_of(): pl.pallas_call(lambda *refs: new_basis_body(math.sqrt(width), *refs), out...  26.7 us
    ppermute x14, starting transfers between devices, layer(): lax.ppermute(piece, PLANE, [(i, (i + d) % plane) for i in range(plane)])  23.5 us
    pallas_call x4, Pallas kernels, pick(): pl.pallas_call(lambda *refs: pick_body(top, scaled, *refs), out_shape=jax...  21.9 us
    all_to_all x3, starting transfers between devices, from_everyone(): return lax.all_to_all(copies, axis, split_axis=0, concat_axis=0, tiled=True)  20.9 us
    all_to_all x4, starting transfers between devices, sent(): lax.all_to_all(picked, PLANE, split_axis=0, concat_axis=0, tiled=True)  20.2 us
  transfers between devices with their start and end apart: 30, of which 12 were waited for; matrix products, arithmetic and copies ran while one was open for 5% of the time, Pallas kernels for 21%

profile of v1, /device:TPU:2, one launch (start us, length us, event | category | flops | bytes accessed | tf_op | source)
XLA Modules:
  0.0 445.9 jit_solution(10524391056029657513)
XLA Ops:
  7.2 1.5 copy.22.refs_1_
  8.7 1.4 copy.23.refs_2_
  10.1 1.4 copy.24.refs_3_
  11.5 1.4 copy.25.refs_4_
  12.9 1.9 packed.1
  14.8 0.8 multiply_convert_fusion
  15.6 0.9 broadcast_in_dim.15
  16.5 11.6 %all-to-all-start = ((bf16[32,32,256]{2,1,0:T(8,128)(2,1)}), bf16[32,32,256]{2,1,0:T(8,128)(2,1)S(1)}, u32[]{:S(2)}, u32[]{:S(2)}) async-start(bf16[32,32,256]{2,1,0:T(8,128)(2,1)} %broadcast_in_dim.15), calls=%async_computation | async-start | bytes 1048576 | tf_op jit(solution)/shard_map/all_to_all | solution.py:36
  28.1 0.7 slice.9
  28.8 21.6 %all-to-all-done = bf16[32,32,256]{2,1,0:T(8,128)(2,1)S(1)} async-done(((bf16[32,32,256]{2,1,0:T(8,128)(2,1)}), bf16[32,32,256]{2,1,0:T(8,128)(2,1)S(1)}, u32[]{:S(2)}, u32[]{:S(2)}) %all-to-all-start) | async-done | bytes 524320 | tf_op jit(solution)/shard_map/all_to_all | solution.py:36
  50.5 4.7 %all_to_all.60 = bf16[2,1024,256]{2,1,0:T(8,128)(2,1)S(1)} all-to-all(bf16[2,1024,256]{2,1,0:T(8,128)(2,1)S(1)} %broadcast_in_dim.16), channel_id=1, replica_groups=mesh['expert_0'=8,'expert_1'=4,'expert_2'=2,'replica'=4] {'expert_2'}, dimensions={0} | all-to-all | bytes 2097152 | tf_op jit(solution)/shard_map/all_to_all | solution.py:36
  55.2 1.0 copy.26
  56.3 11.7 %all-gather.5.cloned.1.call-done.refs_1_.refs_2_ = bf16[1024,1152]{1,0:T(8,128)(2,1)} async-done(((bf16[128,1152]{1,0:T(8,128)(2,1)}), bf16[1024,1152]{1,0:T(8,128)(2,1)}) %all-gather.5.cloned.1.call-update) | async-done | bytes 2359312 | tf_op jit(solution)/shard_map/all_gather | solution.py:432
  68.1 0.8 fusion
  68.9 40.2 %all-gather.7.cloned.1.call-done.refs_2_ = bf16[1024,1024]{1,0:T(8,128)(2,1)} async-done(((bf16[128,1024]{1,0:T(8,128)(2,1)}), bf16[1024,1024]{1,0:T(8,128)(2,1)}) %all-gather.7.cloned.1.call-update) | async-done | bytes 2097168 | tf_op jit(solution)/shard_map/all_gather | solution.py:432
  109.8 5.4 %pick.2 = bf16[8,2,64,1024]{3,2,1,0:T(8,128)(2,1)} custom-call(s32[2]{0:T(128)} %pad_add_fusion.refs_0_, bf16[1024,1152]{1,0:T(8,128)(2,1)} %all-gather.5.cloned.1.call-done.refs_1_.refs_2_, bf16[1024,1152]{1,0:T(8,128)(2,1)} %all-gather.5.cloned.1.call-done.refs_1_.refs_2_), custom_call_target="tpu_custom_call" | custom-call | flops 536870912 | bytes 4194304 | tf_op jit(solution)/shard_map/pick/pallas_call | solution.py:116
  115.1 4.8 %all-to-all-start.2 = ((bf16[8,2,64,1024]{3,2,1,0:T(8,128)(2,1)}), bf16[8,2,64,1024]{3,2,1,0:T(8,128)(2,1)S(1)}, u32[]{:S(2)}, u32[]{:S(2)}) async-start(bf16[8,2,64,1024]{3,2,1,0:T(8,128)(2,1)} %pick.2), calls=%async_computation.2 | async-start | bytes 4194304 | tf_op jit(solution)/shard_map/all_to_all | solution.py:453
  119.9 30.5 %all-gather.9.cloned.1.call-done.refs_2_ = bf16[1024,1024]{1,0:T(8,128)(2,1)} async-done(((bf16[128,1024]{1,0:T(8,128)(2,1)}), bf16[1024,1024]{1,0:T(8,128)(2,1)}) %all-gather.9.cloned.1.call-update) | async-done | bytes 2097168 | tf_op jit(solution)/shard_map/all_gather | solution.py:432
  150.5 5.4 %pick.3 = bf16[8,2,64,1024]{3,2,1,0:T(8,128)(2,1)} custom-call(s32[2]{0:T(128)} %pad_add_fusion.refs_0_, bf16[1024,1152]{1,0:T(8,128)(2,1)} %all-gather.5.cloned.1.call-done.refs_1_.refs_2_, bf16[1024,1024]{1,0:T(8,128)(2,1)} %all-gather.7.cloned.1.call-done.refs_2_), custom_call_target="tpu_custom_call" | custom-call | flops 536870912 | bytes 4194304 | tf_op jit(solution)/shard_map/pick/pallas_call | solution.py:116
  155.9 1.3 copy-done.1
  157.2 4.8 %all-to-all-start.3 = ((bf16[8,2,64,1024]{3,2,1,0:T(8,128)(2,1)}), bf16[8,2,64,1024]{3,2,1,0:T(8,128)(2,1)}, u32[]{:S(2)}, u32[]{:S(2)}) async-start(bf16[8,2,64,1024]{3,2,1,0:T(8,128)(2,1)} %pick.3), calls=%async_computation.3 | async-start | bytes 4194304 | tf_op jit(solution)/shard_map/all_to_all | solution.py:453
  162.0 5.6 %pick_scaled.2 = bf16[8,2,64,1024]{3,2,1,0:T(8,128)(2,1)} custom-call(s32[2]{0:T(128)} %pad_add_fusion.refs_0_, bf16[1024,1152]{1,0:T(8,128)(2,1)} %all-gather.5.cloned.1.call-done.refs_1_.refs_2_, bf16[1024,1024]{1,0:T(8,128)(2,1)} %all-gather.9.cloned.1.call-done.refs_2_), custom_call_target="tpu_custom_call" | custom-call | flops 536870912 | bytes 4194304 | tf_op jit(solution)/shard_map/pick_scaled/pallas_call | solution.py:116
  167.6 20.3 %all-to-all-done.3.x1 = bf16[8,2,64,1024]{3,2,1,0:T(8,128)(2,1)} async-done(((bf16[8,2,64,1024]{3,2,1,0:T(8,128)(2,1)}), bf16[8,2,64,1024]{3,2,1,0:T(8,128)(2,1)}, u32[]{:S(2)}, u32[]{:S(2)}) %all-to-all-start.3) | async-done | bytes 2097184 | tf_op jit(solution)/shard_map/all_to_all | solution.py:453
  187.8 5.0 %all-to-all-start.4 = ((bf16[8,2,64,1024]{3,2,1,0:T(8,128)(2,1)}), bf16[8,2,64,1024]{3,2,1,0:T(8,128)(2,1)S(1)}, u32[]{:S(2)}, u32[]{:S(2)}) async-start(bf16[8,2,64,1024]{3,2,1,0:T(8,128)(2,1)} %pick_scaled.2), calls=%async_computation.4 | async-start | bytes 4194304 | tf_op jit(solution)/shard_map/all_to_all | solution.py:453
  192.8 5.6 %pick_scaled.3 = bf16[8,2,64,1024]{3,2,1,0:T(8,128)(2,1)} custom-call(s32[2]{0:T(128)} %pad_add_fusion.refs_0_, bf16[1024,1152]{1,0:T(8,128)(2,1)} %all-gather.5.cloned.1.call-done.refs_1_.refs_2_, bf16[1024,1024]{1,0:T(8,128)(2,1)} %all-gather.11.cloned.1.call-done.refs_2_), custom_call_target="tpu_custom_call" | custom-call | flops 536870912 | bytes 4194304 | tf_op jit(solution)/shard_map/pick_scaled/pallas_call | solution.py:116
  198.4 20.2 %all-to-all-done.4.dy.dy0 = bf16[8,2,64,1024]{3,2,1,0:T(8,128)(2,1)S(1)} async-done(((bf16[8,2,64,1024]{3,2,1,0:T(8,128)(2,1)}), bf16[8,2,64,1024]{3,2,1,0:T(8,128)(2,1)S(1)}, u32[]{:S(2)}, u32[]{:S(2)}) %all-to-all-start.4) | async-done | bytes 2097184 | tf_op jit(solution)/shard_map/all_to_all | solution.py:453
  218.5 1.3 copy-done
  219.9 5.7 %all-to-all-start.5 = ((bf16[8,2,64,1024]{3,2,1,0:T(8,128)(2,1)}), bf16[8,2,64,1024]{3,2,1,0:T(8,128)(2,1)}, u32[]{:S(2)}, u32[]{:S(2)}) async-start(bf16[8,2,64,1024]{3,2,1,0:T(8,128)(2,1)} %pick_scaled.3), calls=%async_computation.5 | async-start | bytes 4194304 | tf_op jit(solution)/shard_map/all_to_all | solution.py:453
  225.5 10.7 %forward.1 = (f32[2,512,384]{2,1,0:T(8,128)}, f32[2,512,384]{2,1,0:T(8,128)}, bf16[2,512,384]{2,1,0:T(8,128)(2,1)}, bf16[2,512,256]{2,1,0:T(8,128)(2,1)}) custom-call(bf16[8,2,64,1024]{3,2,1,0:T(8,128)(2,1)} %copy-done.1, bf16[8,2,64,1024]{3,2,1,0:T(8,128)(2,1)} %all-to-all-done.3.x1, bf16[2,2048,384]{2,1,0:T(8,128)(2,1)} %gate_w.3, ...), custom_call_target="tpu_custom_call" | custom-call | flops 4294967296 | bytes 16000000 | tf_op jit(solution)/shard_map/forward/pallas_call | solution.py:204
  236.2 4.6 %first_half.1 = (f32[2,512,384]{2,1,0:T(8,128)}, f32[2,512,256]{2,1,0:T(8,128)}) custom-call(bf16[8,2,64,1024]{3,2,1,0:T(8,128)(2,1)} %copy-done, bf16[2,384,2048]{2,1,0:T(8,128)(2,1)} %down_w.3, bf16[2048,256]{1,0:T(8,128)(2,1)} %bitcast.51), custom_call_target="tpu_custom_call" | custom-call | flops 1342177280 | bytes 8000000 | tf_op jit(solution)/shard_map/first_half/pallas_call | solution.py:226
  240.8 10.6 %all-to-all-done.5.dy.dy1 = bf16[8,2,64,1024]{3,2,1,0:T(8,128)(2,1)} async-done(((bf16[8,2,64,1024]{3,2,1,0:T(8,128)(2,1)}), bf16[8,2,64,1024]{3,2,1,0:T(8,128)(2,1)}, u32[]{:S(2)}, u32[]{:S(2)}) %all-to-all-start.5) | async-done | bytes 2097184 | tf_op jit(solution)/shard_map/all_to_all | solution.py:453
  251.4 6.6 %backward.1 = (bf16[2,512,384]{2,1,0:T(8,128)(2,1)}, bf16[2,512,384]{2,1,0:T(8,128)(2,1)}, bf16[2,3,384,256]{3,2,1,0:T(8,128)(2,1)}) custom-call(bf16[8,2,64,1024]{3,2,1,0:T(8,128)(2,1)} %all-to-all-done.5.dy.dy1, bf16[2,384,2048]{2,1,0:T(8,128)(2,1)} %down_w.3, bf16[2048,256]{1,0:T(8,128)(2,1)} %bitcast.52, f32[2,512,384]{2,1,0:T(8,128)} %get-tuple-element.33.hidden_part, ...), custom_call_target="tpu_custom_call" | custom-call | flops 1946157056 | bytes 12000000 | tf_op jit(solution)/shard_map/backward/pallas_call | solution.py:263
  258.0 4.3 all-to-all-start.6
  262.3 16.2 %all-to-all-done.6 = bf16[4,576,256]{2,1,0:T(8,128)(2,1)S(1)} async-done(((bf16[4,576,256]{2,1,0:T(8,128)(2,1)}), bf16[4,576,256]{2,1,0:T(8,128)(2,1)S(1)}, u32[]{:S(2)}, u32[]{:S(2)}) %all-to-all-start.6) | async-done | bytes 1179680 | tf_op jit(solution)/shard_map/all_to_all | solution.py:42
  278.8 1.1 broadcast_in_dim.17
  279.9 3.5 all-to-all-start.7
  283.5 9.8 %row_grads.1 = (bf16[8,2,64,1024]{3,2,1,0:T(8,128)(2,1)}, bf16[8,2,64,1024]{3,2,1,0:T(8,128)(2,1)}) custom-call(bf16[2,512,384]{2,1,0:T(8,128)(2,1)} %get-tuple-element.41.gate_grad, bf16[2,512,384]{2,1,0:T(8,128)(2,1)} %get-tuple-element.42.up_grad, bf16[2,2048,384]{2,1,0:T(8,128)(2,1)} %gate_w.3, bf16[2,2048,384]{2,1,0:T(8,128)(2,1)} %up_w.3), custom_call_target="tpu_custom_call" | custom-call | flops 3221225472 | bytes 12000000 | tf_op jit(solution)/shard_map/row_grads/pallas_call | solution.py:295
  293.3 2.5 dynamic-slice_bitcast_fusion.8
  295.9 3.4 collective-permute-start.2
  299.6 2.7 collective-permute-start.4
  302.3 11.7 %weight_grads.1 = bf16[2048,2304]{1,0:T(8,128)(2,1)} custom-call(bf16[8,2,64,1024]{3,2,1,0:T(8,128)(2,1)} %copy-done.1, bf16[8,2,64,1024]{3,2,1,0:T(8,128)(2,1)} %all-to-all-done.3.x1, bf16[8,2,64,1024]{3,2,1,0:T(8,128)(2,1)} %copy-done, bf16[8,2,64,1024]{3,2,1,0:T(8,128)(2,1)} %all-to-all-done.5.dy.dy1, bf16[2,512,384]{2,1,0:T(8,128)(2,1)} %get-tuple-element.41.gate_grad, ...), custom_call_target="tpu_custom_call" | custom-call | flops 4831838208 | bytes 24000000 | tf_op jit(solution)/shard_map/weight_grads/pallas_call | solution.py:321
  314.6 0.9 collective-permute-start.6
  315.6 7.3 %convolution_convert_fusion = bf16[2048,256]{1,0:T(8,128)(2,1)} fusion(bf16[2048,2304]{1,0:T(8,128)(2,1)} %weight_grads.1, bf16[2304,256]{1,0:T(8,128)(2,1)S(1)} %bitcast.53), kind=kOutput, calls=%fused_computation | convolution fusion | flops 2416443392 | bytes 11665408 | tf_op jit(solution)/shard_map/dot_general | solution.py:27
  322.9 1.2 collective-permute-done.6.refs_9_
  324.1 0.7 copy-done.10
  324.8 6.1 %give_back.2 = bf16[1024,1024]{1,0:T(8,128)(2,1)} custom-call(s32[2]{0:T(128)} %pad_add_fusion.refs_0_, bf16[1024,1152]{1,0:T(8,128)(2,1)} %all-gather.5.cloned.1.call-done.refs_1_.refs_2_, bf16[2,64,1024]{2,1,0:T(8,128)(2,1)} %get-tuple-element.56.refs_2_, bf16[2,64,1024]{2,1,0:T(8,128)(2,1)} %copy-done.6, bf16[2,64,1024]{2,1,0:T(8,128)(2,1)} %copy-done.8, ...), custom_call_target="tpu_custom_call" | custom-call | flops 536870912 | bytes 4194304 | tf_op jit(solution)/shard_map/give_back/pallas_call | solution.py:158
  330.9 4.9 %all-to-all-start.8 = ((bf16[8,256,256]{2,1,0:T(8,128)(2,1)}), bf16[8,256,256]{2,1,0:T(8,128)(2,1)S(1)}, u32[]{:S(2)}, u32[]{:S(2)}) async-start(bf16[8,256,256]{2,1,0:T(8,128)(2,1)} %bitcast.16), calls=%async_computation.9 | async-start | bytes 2097152 | tf_op jit(solution)/shard_map/all_to_all | solution.py:42
  335.8 2.5 dynamic-slice_bitcast_fusion
  339.2 2.9 collective-permute-start.9
  342.6 3.0 collective-permute-start.11
  346.0 2.8 collective-permute-start.12
  349.5 5.4 %collective-permute-start.13 = (bf16[2,64,1024]{2,1,0:T(8,128)(2,1)S(1)}, bf16[2,64,1024]{2,1,0:T(8,128)(2,1)}, u32[]{:S(2)}, u32[]{:S(2)}) collective-permute-start(bf16[2,64,1024]{2,1,0:T(8,128)(2,1)S(1)} %get-tuple-element.57), channel_id=1, source_target_pairs={{0,28},{4,0},{8,4},{12,8},{16,12},{20,16},{24,20},{28,24},{1,29},{... | collective-permute-start | bytes 786440 | tf_op jit(solution)/shard_map/ppermute | solution.py:475
  354.9 0.8 reduce_sum.37
  355.7 5.5 %all-to-all-start.9 = ((bf16[32,8,256]{2,1,0:T(8,128)(2,1)}), bf16[32,8,256]{2,1,0:T(8,128)(2,1)S(1)}, u32[]{:S(2)}, u32[]{:S(2)}) async-start(bf16[32,8,256]{2,1,0:T(8,128)(2,1)} %bitcast.27), calls=%async_computation.11 | async-start | bytes 262144 | tf_op jit(solution)/shard_map/all_to_all | solution.py:42
  361.5 5.0 %collective-permute-done.13.refs_9_ = bf16[2,64,1024]{2,1,0:T(8,128)(2,1)} collective-permute-done((bf16[2,64,1024]{2,1,0:T(8,128)(2,1)S(1)}, bf16[2,64,1024]{2,1,0:T(8,128)(2,1)}, u32[]{:S(2)}, u32[]{:S(2)}) %collective-permute-start.13) | collective-permute-done | bytes 262176 | tf_op jit(solution)/shard_map/ppermute | solution.py:475
  366.5 6.1 %give_back.3 = bf16[1024,1024]{1,0:T(8,128)(2,1)} custom-call(s32[2]{0:T(128)} %pad_add_fusion.refs_0_, bf16[1024,1152]{1,0:T(8,128)(2,1)} %all-gather.5.cloned.1.call-done.refs_1_.refs_2_, bf16[2,64,1024]{2,1,0:T(8,128)(2,1)} %get-tuple-element.64.refs_2_, bf16[2,64,1024]{2,1,0:T(8,128)(2,1)} %copy-done.5, bf16[2,64,1024]{2,1,0:T(8,128)(2,1)} %copy-done.7, ...), custom_call_target="tpu_custom_call" | custom-call | flops 536870912 | bytes 4194304 | tf_op jit(solution)/shard_map/give_back/pallas_call | solution.py:158
  372.7 14.7 %all_to_all.61 = bf16[32,8,256]{2,1,0:T(8,128)(2,1)S(1)} all-to-all(bf16[32,8,256]{2,1,0:T(8,128)(2,1)S(1)} %broadcast_in_dim.18), channel_id=1, replica_groups=mesh['expert_0'=8,'expert_1'=4,'expert_2'=2,'replica'=4] {'expert_0','ex..., dimensions={0} | all-to-all | bytes 262144 | tf_op jit(solution)/shard_map/all_to_all | solution.py:36
  387.4 1.1 broadcast_in_dim.19
  388.5 5.8 %all-to-all-start.11 = ((bf16[8,256,256]{2,1,0:T(8,128)(2,1)}), bf16[8,256,256]{2,1,0:T(8,128)(2,1)S(1)}, u32[]{:S(2)}, u32[]{:S(2)}) async-start(bf16[8,256,256]{2,1,0:T(8,128)(2,1)} %broadcast_in_dim.19), calls=%async_computation.13 | async-start | bytes 2097152 | tf_op jit(solution)/shard_map/all_to_all | solution.py:36
  394.2 1.6 convert.4
  395.8 13.6 %all-to-all-done.11 = bf16[8,256,256]{2,1,0:T(8,128)(2,1)S(1)} async-done(((bf16[8,256,256]{2,1,0:T(8,128)(2,1)}), bf16[8,256,256]{2,1,0:T(8,128)(2,1)S(1)}, u32[]{:S(2)}, u32[]{:S(2)}) %all-to-all-start.11) | async-done | bytes 1048608 | tf_op jit(solution)/shard_map/all_to_all | solution.py:36
  409.5 1.0 copy-done.3
  410.5 26.7 %new_basis.1 = f32[32,256]{1,0:T(8,128)} custom-call(s32[1]{0:T(128)} %bitcast.26.refs_0_, bf16[2048,256]{1,0:T(8,128)(2,1)} %bitcast.58, bf16[2048,256]{1,0:T(8,128)(2,1)} %bitcast.59), custom_call_target="tpu_custom_call" | custom-call | flops 30000001024 | bytes 2000000 | tf_op jit(solution)/shard_map/new_basis/pallas_call | solution.py:385
  437.2 1.9 pad_maximum_fusion
  (61 shorter events, 5.2 us)
Async XLA Ops:
  7.2 21.0 %copy-start.2 = (bf16[128,2048]{1,0:T(8,128)(2,1)S(1)}, bf16[128,2048]{1,0:T(8,128)(2,1)}, u32[]{:S(2)}) copy-start(bf16[128,2048]{1,0:T(8,128)(2,1)} %refs_0_.1) | copy-start | bytes 1572868
  7.2 60.8 %all-gather.5.cloned.1.call-start = ((), (), s32[]{:S(2)}) async-start(), calls=%async_computation.14 | async-start | bytes 2654208 | tf_op jit(solution)/shard_map/all_gather | solution.py:432
  16.5 34.0 %all-to-all-start = ((bf16[32,32,256]{2,1,0:T(8,128)(2,1)}), bf16[32,32,256]{2,1,0:T(8,128)(2,1)S(1)}, u32[]{:S(2)}, u32[]{:S(2)}) async-start(bf16[32,32,256]{2,1,0:T(8,128)(2,1)} %broadcast_in_dim.15), calls=%async_computation | async-start | bytes 1048576 | tf_op jit(solution)/shard_map/all_to_all | solution.py:36
  28.1 81.0 %all-gather.7.cloned.1.call-start = ((), (), s32[]{:S(2)}) async-start(), calls=%async_computation.15 | async-start | bytes 2359296 | tf_op jit(solution)/shard_map/all_gather | solution.py:432
  50.5 17.6 %copy-start.4 = (bf16[128,2048]{1,0:T(8,128)(2,1)S(1)}, bf16[128,2048]{1,0:T(8,128)(2,1)}, u32[]{:S(2)}) copy-start(bf16[128,2048]{1,0:T(8,128)(2,1)} %param.11) | copy-start | bytes 1572868
  68.0 82.4 %all-gather.9.cloned.1.call-start = ((), (), s32[]{:S(2)}) async-start(), calls=%async_computation.16 | async-start | bytes 2359296 | tf_op jit(solution)/shard_map/all_gather | solution.py:432
  115.1 40.7 %all-to-all-start.2 = ((bf16[8,2,64,1024]{3,2,1,0:T(8,128)(2,1)}), bf16[8,2,64,1024]{3,2,1,0:T(8,128)(2,1)S(1)}, u32[]{:S(2)}, u32[]{:S(2)}) async-start(bf16[8,2,64,1024]{3,2,1,0:T(8,128)(2,1)} %pick.2), calls=%async_computation.2 | async-start | bytes 4194304 | tf_op jit(solution)/shard_map/all_to_all | solution.py:453
  119.9 72.9 %all-gather.11.cloned.1.call-start = ((), (), s32[]{:S(2)}) async-start(), calls=%async_computation.17 | async-start | bytes 2359296 | tf_op jit(solution)/shard_map/all_gather | solution.py:432
  155.9 1.3 copy-start.1
  157.2 30.7 %all-to-all-start.3 = ((bf16[8,2,64,1024]{3,2,1,0:T(8,128)(2,1)}), bf16[8,2,64,1024]{3,2,1,0:T(8,128)(2,1)}, u32[]{:S(2)}, u32[]{:S(2)}) async-start(bf16[8,2,64,1024]{3,2,1,0:T(8,128)(2,1)} %pick.3), calls=%async_computation.3 | async-start | bytes 4194304 | tf_op jit(solution)/shard_map/all_to_all | solution.py:453
  187.8 30.7 %all-to-all-start.4 = ((bf16[8,2,64,1024]{3,2,1,0:T(8,128)(2,1)}), bf16[8,2,64,1024]{3,2,1,0:T(8,128)(2,1)S(1)}, u32[]{:S(2)}, u32[]{:S(2)}) async-start(bf16[8,2,64,1024]{3,2,1,0:T(8,128)(2,1)} %pick_scaled.2), calls=%async_computation.4 | async-start | bytes 4194304 | tf_op jit(solution)/shard_map/all_to_all | solution.py:453
  218.5 1.3 copy-start
  219.9 31.5 %all-to-all-start.5 = ((bf16[8,2,64,1024]{3,2,1,0:T(8,128)(2,1)}), bf16[8,2,64,1024]{3,2,1,0:T(8,128)(2,1)}, u32[]{:S(2)}, u32[]{:S(2)}) async-start(bf16[8,2,64,1024]{3,2,1,0:T(8,128)(2,1)} %pick_scaled.3), calls=%async_computation.5 | async-start | bytes 4194304 | tf_op jit(solution)/shard_map/all_to_all | solution.py:453
  258.0 20.5 %all-to-all-start.6 = ((bf16[4,576,256]{2,1,0:T(8,128)(2,1)}), bf16[4,576,256]{2,1,0:T(8,128)(2,1)S(1)}, u32[]{:S(2)}, u32[]{:S(2)}) async-start(bf16[4,576,256]{2,1,0:T(8,128)(2,1)} %bitcast.57), calls=%async_computation.6 | async-start | bytes 2359296 | tf_op jit(solution)/shard_map/all_to_all | solution.py:42
  279.9 35.6 %all-to-all-start.7 = ((bf16[4,576,256]{2,1,0:T(8,128)(2,1)}), bf16[4,576,256]{2,1,0:T(8,128)(2,1)S(1)}, u32[]{:S(2)}, u32[]{:S(2)}) async-start(bf16[4,576,256]{2,1,0:T(8,128)(2,1)} %broadcast_in_dim.17), calls=%async_computation.7 | async-start | bytes 2359296 | tf_op jit(solution)/shard_map/all_to_all | solution.py:36
  283.5 153.7 %reduce-scatter.3.cloned.1.call-start = ((), (), s32[]{:S(2)}) async-start(), calls=%async_computation.18 | async-start | bytes 2359296 | tf_op jit(solution)/shard_map/reduce_scatter | solution.py:493
  295.8 18.2 %collective-permute-start = (bf16[2,64,1024]{2,1,0:T(8,128)(2,1)S(1)}, bf16[2,64,1024]{2,1,0:T(8,128)(2,1)S(1)}, u32[]{:S(2)}, u32[]{:S(2)}) collective-permute-start(bf16[2,64,1024]{2,1,0:T(8,128)(2,1)S(1)} %get-tuple-element.55), channel_id=1, source_target_pairs={{0,4},{4,8},{8,12},{12,16},{16,20},{20,24},{24,28},{28,0},{1,5},{5... | collective-permute-start | bytes 786440 | tf_op jit(solution)/shard_map/ppermute | solution.py:475
  295.8 18.8 %collective-permute-start.1 = (bf16[2,64,1024]{2,1,0:T(8,128)(2,1)S(1)}, bf16[2,64,1024]{2,1,0:T(8,128)(2,1)S(1)}, u32[]{:S(2)}, u32[]{:S(2)}) collective-permute-start(bf16[2,64,1024]{2,1,0:T(8,128)(2,1)S(1)} %get-tuple-element.54), channel_id=1, source_target_pairs={{0,8},{4,12},{8,16},{12,20},{16,24},{20,28},{24,0},{28,4},{1,9},{5... | collective-permute-start | bytes 786440 | tf_op jit(solution)/shard_map/ppermute | solution.py:475
  295.9 27.0 %collective-permute-start.2 = (bf16[2,64,1024]{2,1,0:T(8,128)(2,1)S(1)}, bf16[2,64,1024]{2,1,0:T(8,128)(2,1)}, u32[]{:S(2)}, u32[]{:S(2)}) collective-permute-start(bf16[2,64,1024]{2,1,0:T(8,128)(2,1)S(1)} %get-tuple-element.53), channel_id=1, source_target_pairs={{0,12},{4,16},{8,20},{12,24},{16,28},{20,0},{24,4},{28,8},{1,13},{... | collective-permute-start | bytes 786440 | tf_op jit(solution)/shard_map/ppermute | solution.py:475
  299.3 23.6 %collective-permute-start.3 = (bf16[2,64,1024]{2,1,0:T(8,128)(2,1)S(1)}, bf16[2,64,1024]{2,1,0:T(8,128)(2,1)}, u32[]{:S(2)}, u32[]{:S(2)}) collective-permute-start(bf16[2,64,1024]{2,1,0:T(8,128)(2,1)S(1)} %get-tuple-element.52), channel_id=1, source_target_pairs={{0,16},{4,20},{8,24},{12,28},{16,0},{20,4},{24,8},{28,12},{1,17},{... | collective-permute-start | bytes 786440 | tf_op jit(solution)/shard_map/ppermute | solution.py:475
  299.6 23.3 %collective-permute-start.4 = (bf16[2,64,1024]{2,1,0:T(8,128)(2,1)S(1)}, bf16[2,64,1024]{2,1,0:T(8,128)(2,1)}, u32[]{:S(2)}, u32[]{:S(2)}) collective-permute-start(bf16[2,64,1024]{2,1,0:T(8,128)(2,1)S(1)} %get-tuple-element.51), channel_id=1, source_target_pairs={{0,20},{4,24},{8,28},{12,0},{16,4},{20,8},{24,12},{28,16},{1,21},{... | collective-permute-start | bytes 786440 | tf_op jit(solution)/shard_map/ppermute | solution.py:475
  314.0 8.9 %copy-start.6 = (bf16[2,64,1024]{2,1,0:T(8,128)(2,1)}, bf16[2,64,1024]{2,1,0:T(8,128)(2,1)S(1)}, u32[]{:S(2)}) copy-start(bf16[2,64,1024]{2,1,0:T(8,128)(2,1)S(1)} %collective-permute-done.refs_3_) | copy-start | bytes 786436
  314.0 8.9 %collective-permute-start.5 = (bf16[2,64,1024]{2,1,0:T(8,128)(2,1)S(1)}, bf16[2,64,1024]{2,1,0:T(8,128)(2,1)S(1)}, u32[]{:S(2)}, u32[]{:S(2)}) collective-permute-start(bf16[2,64,1024]{2,1,0:T(8,128)(2,1)S(1)} %get-tuple-element.50), channel_id=1, source_target_pairs={{0,24},{4,28},{8,0},{12,4},{16,8},{20,12},{24,16},{28,20},{1,25},{... | collective-permute-start | bytes 786440 | tf_op jit(solution)/shard_map/ppermute | solution.py:475
  314.6 8.2 %copy-start.8 = (bf16[2,64,1024]{2,1,0:T(8,128)(2,1)}, bf16[2,64,1024]{2,1,0:T(8,128)(2,1)S(1)}, u32[]{:S(2)}) copy-start(bf16[2,64,1024]{2,1,0:T(8,128)(2,1)S(1)} %collective-permute-done.1.refs_4_) | copy-start | bytes 786436
  314.6 9.5 %collective-permute-start.6 = (bf16[2,64,1024]{2,1,0:T(8,128)(2,1)S(1)}, bf16[2,64,1024]{2,1,0:T(8,128)(2,1)S(1)}, u32[]{:S(2)}, u32[]{:S(2)}) collective-permute-start(bf16[2,64,1024]{2,1,0:T(8,128)(2,1)S(1)} %get-tuple-element.49), channel_id=1, source_target_pairs={{0,28},{4,0},{8,4},{12,8},{16,12},{20,16},{24,20},{28,24},{1,29},{... | collective-permute-start | bytes 786440 | tf_op jit(solution)/shard_map/ppermute | solution.py:475
  322.9 1.2 copy-start.9
  324.1 0.7 copy-start.10
  330.9 24.0 %all-to-all-start.8 = ((bf16[8,256,256]{2,1,0:T(8,128)(2,1)}), bf16[8,256,256]{2,1,0:T(8,128)(2,1)S(1)}, u32[]{:S(2)}, u32[]{:S(2)}) async-start(bf16[8,256,256]{2,1,0:T(8,128)(2,1)} %bitcast.16), calls=%async_computation.9 | async-start | bytes 2097152 | tf_op jit(solution)/shard_map/all_to_all | solution.py:42
  338.3 7.7 %collective-permute-start.7 = (bf16[2,64,1024]{2,1,0:T(8,128)(2,1)S(1)}, bf16[2,64,1024]{2,1,0:T(8,128)(2,1)S(1)}, u32[]{:S(2)}, u32[]{:S(2)}) collective-permute-start(bf16[2,64,1024]{2,1,0:T(8,128)(2,1)S(1)} %get-tuple-element.63), channel_id=1, source_target_pairs={{0,4},{4,8},{8,12},{12,16},{16,20},{20,24},{24,28},{28,0},{1,5},{5... | collective-permute-start | bytes 786440 | tf_op jit(solution)/shard_map/ppermute | solution.py:475
  338.8 10.0 %collective-permute-start.8 = (bf16[2,64,1024]{2,1,0:T(8,128)(2,1)S(1)}, bf16[2,64,1024]{2,1,0:T(8,128)(2,1)S(1)}, u32[]{:S(2)}, u32[]{:S(2)}) collective-permute-start(bf16[2,64,1024]{2,1,0:T(8,128)(2,1)S(1)} %get-tuple-element.62), channel_id=1, source_target_pairs={{0,8},{4,12},{8,16},{12,20},{16,24},{20,28},{24,0},{28,4},{1,9},{5... | collective-permute-start | bytes 786440 | tf_op jit(solution)/shard_map/ppermute | solution.py:475
  339.2 22.3 %collective-permute-start.9 = (bf16[2,64,1024]{2,1,0:T(8,128)(2,1)S(1)}, bf16[2,64,1024]{2,1,0:T(8,128)(2,1)}, u32[]{:S(2)}, u32[]{:S(2)}) collective-permute-start(bf16[2,64,1024]{2,1,0:T(8,128)(2,1)S(1)} %get-tuple-element.61), channel_id=1, source_target_pairs={{0,12},{4,16},{8,20},{12,24},{16,28},{20,0},{24,4},{28,8},{1,13},{... | collective-permute-start | bytes 786440 | tf_op jit(solution)/shard_map/ppermute | solution.py:475
  342.1 19.4 %collective-permute-start.10 = (bf16[2,64,1024]{2,1,0:T(8,128)(2,1)S(1)}, bf16[2,64,1024]{2,1,0:T(8,128)(2,1)}, u32[]{:S(2)}, u32[]{:S(2)}) collective-permute-start(bf16[2,64,1024]{2,1,0:T(8,128)(2,1)S(1)} %get-tuple-element.60), channel_id=1, source_target_pairs={{0,16},{4,20},{8,24},{12,28},{16,0},{20,4},{24,8},{28,12},{1,17},{... | collective-permute-start | bytes 786440 | tf_op jit(solution)/shard_map/ppermute | solution.py:475
  342.6 18.9 %collective-permute-start.11 = (bf16[2,64,1024]{2,1,0:T(8,128)(2,1)S(1)}, bf16[2,64,1024]{2,1,0:T(8,128)(2,1)}, u32[]{:S(2)}, u32[]{:S(2)}) collective-permute-start(bf16[2,64,1024]{2,1,0:T(8,128)(2,1)S(1)} %get-tuple-element.59), channel_id=1, source_target_pairs={{0,20},{4,24},{8,28},{12,0},{16,4},{20,8},{24,12},{28,16},{1,21},{... | collective-permute-start | bytes 786440 | tf_op jit(solution)/shard_map/ppermute | solution.py:475
  346.0 2.8 copy-start.5
  346.0 15.5 %collective-permute-start.12 = (bf16[2,64,1024]{2,1,0:T(8,128)(2,1)S(1)}, bf16[2,64,1024]{2,1,0:T(8,128)(2,1)}, u32[]{:S(2)}, u32[]{:S(2)}) collective-permute-start(bf16[2,64,1024]{2,1,0:T(8,128)(2,1)S(1)} %get-tuple-element.58), channel_id=1, source_target_pairs={{0,24},{4,28},{8,0},{12,4},{16,8},{20,12},{24,16},{28,20},{1,25},{... | collective-permute-start | bytes 786440 | tf_op jit(solution)/shard_map/ppermute | solution.py:475
  348.8 0.7 copy-start.7
  349.5 17.1 %collective-permute-start.13 = (bf16[2,64,1024]{2,1,0:T(8,128)(2,1)S(1)}, bf16[2,64,1024]{2,1,0:T(8,128)(2,1)}, u32[]{:S(2)}, u32[]{:S(2)}) collective-permute-start(bf16[2,64,1024]{2,1,0:T(8,128)(2,1)S(1)} %get-tuple-element.57), channel_id=1, source_target_pairs={{0,28},{4,0},{8,4},{12,8},{16,12},{20,16},{24,20},{28,24},{1,29},{... | collective-permute-start | bytes 786440 | tf_op jit(solution)/shard_map/ppermute | solution.py:475
  355.7 17.0 %all-to-all-start.9 = ((bf16[32,8,256]{2,1,0:T(8,128)(2,1)}), bf16[32,8,256]{2,1,0:T(8,128)(2,1)S(1)}, u32[]{:S(2)}, u32[]{:S(2)}) async-start(bf16[32,8,256]{2,1,0:T(8,128)(2,1)} %bitcast.27), calls=%async_computation.11 | async-start | bytes 262144 | tf_op jit(solution)/shard_map/all_to_all | solution.py:42
  361.2 76.0 %reduce-scatter.5.cloned.1.call-start = ((), (), s32[]{:S(2)}) async-start(), calls=%async_computation.19 | async-start | bytes 2359296 | tf_op jit(solution)/shard_map/reduce_scatter | solution.py:493
  388.5 21.0 %all-to-all-start.11 = ((bf16[8,256,256]{2,1,0:T(8,128)(2,1)}), bf16[8,256,256]{2,1,0:T(8,128)(2,1)S(1)}, u32[]{:S(2)}, u32[]{:S(2)}) async-start(bf16[8,256,256]{2,1,0:T(8,128)(2,1)} %broadcast_in_dim.19), calls=%async_computation.13 | async-start | bytes 2097152 | tf_op jit(solution)/shard_map/all_to_all | solution.py:36
  409.5 1.0 copy-start.3
Sparse Core Ops, SparseCore 0:
  15.0 52.9 all-gather.4
  69.8 39.2 all-gather.6
  110.9 39.5 all-gather.8
  152.7 39.4 all-gather.10
  331.0 43.2 reduce-scatter.2
  376.8 42.3 reduce-scatter.4

commit v2 on v1

--- a/solution.py
+++ b/solution.py
@@ -43,6 +43,30 @@
     return arrived.astype(f32).sum(axis=0).astype(bf16)
 
 
+def sum_and_spread_body(arrived, out):
+    total = arrived[...].astype(f32).sum(axis=0).astype(bf16)
+    out[...] = jnp.broadcast_to(total[None], out.shape)
+
+
+def sum_and_spread(arrived, steps):
+    devices, lines, width = arrived.shape
+    spec = pl.BlockSpec((devices, lines // steps, width), lambda i: (0, i, 0))
+    return pl.pallas_call(
+        sum_and_spread_body,
+        out_shape=jax.ShapeDtypeStruct(arrived.shape, bf16),
+        grid=(steps,),
+        in_specs=[spec],
+        out_specs=spec,
+        cost_estimate=cost(arrived.size, 4 * arrived.size),
+        compiler_params=pltpu.CompilerParams(vmem_limit_bytes=8 * 2**20),
+        name="sum_and_spread",
+    )(arrived)
+
+
+def exchanged(pieces, axis):
+    return lax.all_to_all(pieces, axis, split_axis=0, concat_axis=0, tiled=True)
+
+
 def gathered(lines, axis):
     return from_everyone(lines, axis).reshape(-1, lines.shape[-1])
 
@@ -57,24 +81,20 @@
     third = (rest - second.astype(f32)).astype(bf16)
     digits = [(target // RADIX).astype(f32), (target % RADIX).astype(f32)]
     parts = digits + [first.astype(f32), second.astype(f32), third.astype(f32)]
-    top = target.shape[1]
-    spare = jnp.zeros((target.shape[0], SIDE - len(parts) * top), f32)
+    top = target.shape[0]
+    spare = jnp.zeros((SIDE - len(parts) * top, target.shape[1]), f32)
     out[:, :width] = tokens[...]
-    out[:, width:] = jnp.concatenate(parts + [spare], 1).astype(bf16)
-
-
-def packed(tokens, half, cap, *routing):
-    count, top = routing[0].shape
-    small = pl.BlockSpec((count, top), lambda i: (0, 0))
+    out[:, width:] = jnp.concatenate(parts + [spare], 0).T.astype(bf16)
+
+
+def packed(tokens, cap, *routing):
+    count, width = tokens.shape
     return pl.pallas_call(
         lambda *refs: packed_body(cap, *refs),
-        out_shape=jax.ShapeDtypeStruct((count, half + SIDE), bf16),
-        grid=(1,),
-        in_specs=[pl.BlockSpec((count, half), lambda i: (0, 0))] + [small] * len(routing),
-        out_specs=pl.BlockSpec((count, half + SIDE), lambda i: (0, 0)),
+        out_shape=jax.ShapeDtypeStruct((count, width + SIDE), bf16),
         cost_estimate=cost(1e6, 6e5),
         name="packed",
-    )(tokens, *routing)
+    )(tokens, *(array.T for array in routing))
 
 
 def want_slots(shape, dim, base, block_of):
@@ -175,29 +195,22 @@
     return value.reshape(-1, value.shape[-1])
 
 
-def forward_body(x0, x1, gate_w, up_w, proj, act, slope_up, hidden, x_proj):
-    half = x0.shape[-1]
-    rows = (flat(x0), flat(x1))
-
-    def times(weight):
-        return dot(rows[0], weight[:half]) + dot(rows[1], weight[half:])
-
-    gate, upper = times(gate_w[0]), times(up_w[0])
+def forward_body(x, gate_w, up_w, proj, act, slope_up, hidden, x_proj):
+    rows = flat(x)
+    gate, upper = dot(rows, gate_w[0]), dot(rows, up_w[0])
     sigma = jax.nn.sigmoid(gate)
     activated = gate * sigma
     act[0] = activated
     slope_up[0] = upper * (sigma * (1.0 + gate * (1.0 - sigma)))
     hidden[0] = (activated * upper).astype(bf16)
-    x_proj[0] = times(proj).astype(bf16)
-
-
-def forward(x0, x1, gate_w, up_w, proj):
-    plane, experts, depth, half = x0.shape
-    width, hid = gate_w.shape[1:]
-    rank = proj.shape[1]
+    x_proj[0] = dot(rows, proj[...]).astype(bf16)
+
+
+def forward(x, gate_w, up_w, proj):
+    plane, experts, depth, width = x.shape
+    hid, rank = gate_w.shape[2], proj.shape[1]
     rows = plane * depth
     part = plane // 2
-    row_spec = pl.BlockSpec((part, 1, depth, half), lambda j, s: (s, j, 0, 0))
     weight = pl.BlockSpec((1, width, hid), lambda j, s: (j, 0, 0))
     out = lambda n: pl.BlockSpec((1, part * depth, n), lambda j, s: (j, s, 0))
     shape = lambda n, t: jax.ShapeDtypeStruct((experts, rows, n), t)
@@ -205,45 +218,19 @@
         forward_body,
         out_shape=(shape(hid, f32), shape(hid, f32), shape(hid, bf16), shape(rank, bf16)),
         grid=(experts, 2),
-        in_specs=[row_spec] * 2 + [weight] * 2 + [pl.BlockSpec((width, rank), lambda j, s: (0, 0))],
+        in_specs=[pl.BlockSpec((part, 1, depth, width), lambda j, s: (s, j, 0, 0))]
+        + [weight] * 2
+        + [pl.BlockSpec((width, rank), lambda j, s: (0, 0))],
         out_specs=(out(hid), out(hid), out(hid), out(rank)),
         cost_estimate=cost(2 * experts * rows * width * (2 * hid + rank), 16e6),
         name="forward",
-    )(x0, x1, gate_w, up_w, proj)
-
-
-def first_half_body(dy, down_w, proj, hidden_grad, dy_proj):
+    )(x, gate_w, up_w, proj)
+
+
+def backward_body(dy, down_w, proj, act, slope_up, hidden, x_proj, gate_grad, up_grad, grads):
     rows = flat(dy)
-    hidden_grad[0] = dot(rows, down_w[0], ((1,), (1,)))
-    dy_proj[0] = dot(rows, proj[...])
-
-
-def first_half(dy, down_w, proj):
-    plane, experts, depth, half = dy.shape
-    hid, rank = down_w.shape[1], proj.shape[1]
-    rows = plane * depth
-    out = lambda n: pl.BlockSpec((1, rows, n), lambda j: (j, 0, 0))
-    return pl.pallas_call(
-        first_half_body,
-        out_shape=tuple(jax.ShapeDtypeStruct((experts, rows, n), f32) for n in (hid, rank)),
-        grid=(experts,),
-        in_specs=[
-            pl.BlockSpec((plane, 1, depth, half), lambda j: (0, j, 0, 0)),
-            pl.BlockSpec((1, hid, half), lambda j: (j, 0, 0)),
-            pl.BlockSpec((half, rank), lambda j: (0, 0)),
-        ],
-        out_specs=(out(hid), out(rank)),
-        cost_estimate=cost(2 * experts * rows * half * (hid + rank), 8e6),
-        name="first_half",
-    )(dy, down_w, proj)
-
-
-def backward_body(
-    dy, down_w, proj, hidden_part, proj_part, act, slope_up, hidden, x_proj, gate_grad, up_grad, grads
-):
-    rows = flat(dy)
-    hidden_grad = hidden_part[0] + dot(rows, down_w[0], ((1,), (1,)))
-    dy_proj = (proj_part[0] + dot(rows, proj[...])).astype(bf16)
+    hidden_grad = dot(rows, down_w[0], ((1,), (1,)))
+    dy_proj = dot(rows, proj[...]).astype(bf16)
     of_up = (hidden_grad * act[0]).astype(bf16)
     of_gate = (hidden_grad * slope_up[0]).astype(bf16)
     up_grad[0] = of_up
@@ -254,8 +241,8 @@
     grads[0, 2] = dot(hidden[0], dy_proj, over).astype(bf16)
 
 
-def backward(dy, down_w, proj, hidden_part, proj_part, act, slope_up, hidden, x_proj):
-    plane, experts, depth, half = dy.shape
+def backward(dy, down_w, proj, act, slope_up, hidden, x_proj):
+    plane, experts, depth, width = dy.shape
     hid, rank = down_w.shape[1], proj.shape[1]
     rows = plane * depth
     mat = lambda n: pl.BlockSpec((1, rows, n), lambda j: (j, 0, 0))
@@ -265,24 +252,21 @@
         out_shape=(shape, shape, jax.ShapeDtypeStruct((experts, 3, hid, rank), bf16)),
         grid=(experts,),
         in_specs=[
-            pl.BlockSpec((plane, 1, depth, half), lambda j: (0, j, 0, 0)),
-            pl.BlockSpec((1, hid, half), lambda j: (j, 0, 1)),
-            pl.BlockSpec((half, rank), lambda j: (1, 0)),
-            mat(hid), mat(rank), mat(hid), mat(hid), mat(hid), mat(rank),
+            pl.BlockSpec((plane, 1, depth, width), lambda j: (0, j, 0, 0)),
+            pl.BlockSpec((1, hid, width), lambda j: (j, 0, 0)),
+            pl.BlockSpec((width, rank), lambda j: (0, 0)),
+            mat(hid), mat(hid), mat(hid), mat(rank),
         ],
         out_specs=(mat(hid), mat(hid), pl.BlockSpec((1, 3, hid, rank), lambda j: (j, 0, 0, 0))),
-        cost_estimate=cost(2 * experts * rows * (half * (hid + rank) + 3 * hid * rank), 12e6),
+        cost_estimate=cost(2 * experts * rows * (width * (hid + rank) + 3 * hid * rank), 16e6),
         name="backward",
-    )(dy, down_w, proj, hidden_part, proj_part, act, slope_up, hidden, x_proj)
-
-
-def row_grads_body(gate_grad, up_grad, gate_w, up_w, out0, out1):
-    half = out0.shape[-1]
+    )(dy, down_w, proj, act, slope_up, hidden, x_proj)
+
+
+def row_grads_body(gate_grad, up_grad, gate_w, up_w, out):
     over = ((1,), (1,))
-    for n, out in enumerate((out0, out1)):
-        part = slice(n * half, (n + 1) * half)
-        value = dot(gate_grad[0], gate_w[0, part], over) + dot(up_grad[0], up_w[0, part], over)
-        out[...] = value.astype(bf16).reshape(out.shape)
+    value = dot(gate_grad[0], gate_w[0], over) + dot(up_grad[0], up_w[0], over)
+    out[...] = value.astype(bf16).reshape(out.shape)
 
 
 def row_grads_of(gate_grad, up_grad, gate_w, up_w, plane):
@@ -291,42 +275,64 @@
     depth, part = rows // plane, plane // 2
     mat = pl.BlockSpec((1, rows // 2, hid), lambda j, s: (j, s, 0))
     weight = pl.BlockSpec((1, width, hid), lambda j, s: (j, 0, 0))
-    shape = jax.ShapeDtypeStruct((plane, experts, depth, width // 2), bf16)
     return pl.pallas_call(
         row_grads_body,
-        out_shape=(shape, shape),
+        out_shape=jax.ShapeDtypeStruct((plane, experts, depth, width), bf16),
         grid=(experts, 2),
         in_specs=[mat, mat, weight, weight],
-        out_specs=[pl.BlockSpec((part, 1, depth, width // 2), lambda j, s: (s, j, 0, 0))] * 2,
+        out_specs=pl.BlockSpec((part, 1, depth, width), lambda j, s: (s, j, 0, 0)),
         cost_estimate=cost(4 * experts * rows * width * hid, 12e6),
         name="row_grads",
     )(gate_grad, up_grad, gate_w, up_w)
 
 
-def weight_grads_body(x0, x1, dy0, dy1, gate_grad, up_grad, hidden, out):
-    half, hid = x0.shape[-1], hidden.shape[-1]
+def weight_grads_body(x, dy, gate_grad, up_grad, hidden, out):
+    hid = hidden.shape[-1]
     over = ((0,), (0,))
-    for n, (x, dy) in enumerate(((x0, dy0), (x1, dy1))):
-        part = pl.ds(n * half, half)
-        out[part, 0:hid] = dot(flat(x), gate_grad[0], over).astype(bf16)
-        out[part, hid : 2 * hid] = dot(flat(x), up_grad[0], over).astype(bf16)
-        out[part, 2 * hid : 3 * hid] = dot(flat(dy), hidden[0], over).astype(bf16)
-
-
-def weight_grads(x0, x1, dy0, dy1, gate_grad, up_grad, hidden):
-    plane, experts, depth, half = x0.shape
+    out[:, 0:hid] = dot(flat(x), gate_grad[0], over).astype(bf16)
+    out[:, hid : 2 * hid] = dot(flat(x), up_grad[0], over).astype(bf16)
+    out[:, 2 * hid : 3 * hid] = dot(flat(dy), hidden[0], over).astype(bf16)
+
+
+def weight_grads(x, dy, gate_grad, up_grad, hidden):
+    plane, experts, depth, width = x.shape
     rows, hid = plane * depth, hidden.shape[2]
-    row_spec = pl.BlockSpec((plane, 1, depth, half), lambda j: (0, j, 0, 0))
-    mat = pl.BlockSpec((1, rows, hid), lambda j: (j, 0, 0))
+    part = width // 2
+    row_spec = pl.BlockSpec((plane, 1, depth, part), lambda j, n: (0, j, 0, n))
+    mat = pl.BlockSpec((1, rows, hid), lambda j, n: (j, 0, 0))
     return pl.pallas_call(
         weight_grads_body,
-        out_shape=jax.ShapeDtypeStruct((2 * half, 3 * hid * experts), bf16),
-        grid=(experts,),
-        in_specs=[row_spec] * 4 + [mat] * 3,
-        out_specs=pl.BlockSpec((2 * half, 3 * hid), lambda j: (0, j)),
-        cost_estimate=cost(12 * experts * rows * half * hid, 24e6),
+        out_shape=jax.ShapeDtypeStruct((width, 3 * hid * experts), bf16),
+        grid=(experts, 2),
+        in_specs=[row_spec] * 2 + [mat] * 3,
+        out_specs=pl.BlockSpec((part, 3 * hid), lambda j, n: (n, j)),
+        cost_estimate=cost(6 * experts * rows * width * hid, 24e6),
+        compiler_params=pltpu.CompilerParams(vmem_limit_bytes=36 * 2**20),
         name="weight_grads",
-    )(x0, x1, dy0, dy1, gate_grad, up_grad, hidden)
+    )(x, dy, gate_grad, up_grad, hidden)
+
+
+def power_body(weights, grads, out):
+    out[...] = dot(weights[...], grads[...]).astype(bf16)
+
+
+def power_of(weights, grads):
+    width, depth = weights.shape
+    rank = grads.shape[1]
+    part = width // 8
+    return pl.pallas_call(
+        power_body,
+        out_shape=jax.ShapeDtypeStruct((width, rank), bf16),
+        grid=(8,),
+        in_specs=[
+            pl.BlockSpec((part, depth), lambda i: (i, 0)),
+            pl.BlockSpec((depth, rank), lambda i: (0, 0)),
+        ],
+        out_specs=pl.BlockSpec((part, rank), lambda i: (i, 0)),
+        cost_estimate=cost(2 * width * depth * rank, 12e6),
+        compiler_params=pltpu.CompilerParams(vmem_limit_bytes=20 * 2**20),
+        name="power",
+    )(weights, grads)
 
 
 def inverse_factor(square):
@@ -338,17 +344,24 @@
     groups = [work[g : g + 8] for g in range(0, size, 8)]
     scales = [jnp.zeros((8, 2 * size), f32) for _ in groups]
     inner = lax.broadcasted_iota(jnp.int32, (8, 2 * size), 0)
-    for j in range(size):
+    for j in range(0, size, 2):
         g, at = divmod(j, 8)
         spread = [jnp.broadcast_to(w[:, j : j + 1], (8, 2 * size)) for w in groups[g:]]
-        pivot = spread[0][at : at + 1]
-        line = groups[g][at : at + 1]
-        scales[g] = jnp.where(inner == at, lax.rsqrt(pivot), scales[g])
-        line = line / pivot
-        factor = jnp.where(inner > at, spread[0], 0.0)
-        groups[g] = groups[g] - factor * line
-        for n in range(g + 1, len(groups)):
-            groups[n] = groups[n] - spread[n - g] * line
+        beside = [jnp.broadcast_to(w[:, j + 1 : j + 2], (8, 2 * size)) for w in groups[g:]]
+        pivot, under = spread[0][at : at + 1], spread[0][at + 1 : at + 2]
+        share = 1.0 / pivot
+        line = groups[g][at : at + 1] * share
+        across = beside[0][at : at + 1] * share
+        next_pivot = beside[0][at + 1 : at + 2] - under * across
+        next_line = (groups[g][at + 1 : at + 2] - under * line) / next_pivot
+        scale = jnp.where(inner == at + 1, lax.rsqrt(next_pivot), scales[g])
+        scales[g] = jnp.where(inner == at, lax.rsqrt(pivot), scale)
+        for n in range(g, len(groups)):
+            first, second = spread[n - g], beside[n - g] - spread[n - g] * across
+            if n == g:
+                first = jnp.where(inner > at, first, 0.0)
+                second = jnp.where(inner > at + 1, second, 0.0)
+            groups[n] = groups[n] - first * line - second * next_line
     return jnp.concatenate([w * s for w, s in zip(groups, scales)], 0)
 
 
@@ -400,6 +413,7 @@
             ],
         ),
         cost_estimate=cost(3e10, 2e6),
+        compiler_params=pltpu.CompilerParams(vmem_limit_bytes=24 * 2**20),
         name="new_basis",
     )(index, power, power)
 
@@ -417,7 +431,6 @@
     projector_basis,
 ):
     tok_count, model_width = tokens.shape
-    half = model_width // 2
     top = expert_ids.shape[1]
     experts = gate_weight.shape[0]
     group_count = lax.axis_size(EXPERT)
@@ -426,8 +439,6 @@
     here = lax.axis_index(PLANE)
     base = jnp.stack([lax.axis_index(Z) * (plane * experts * cap), here]).astype(jnp.int32)
 
-    first_rows = packed(tokens, half, cap, expert_ids, slot_ids, kept_mask, route_weights)
-
     def along_z(value):
         return lax.all_gather(value, Z, axis=0, tiled=True)
 
@@ -436,62 +447,53 @@
 
     projector = (projector_basis * (1.0 / math.sqrt(model_width))).astype(bf16)
     projector = gathered(projector, (Z, X))
+    first_rows = packed(tokens, cap, expert_ids, slot_ids, kept_mask, route_weights)
+    first_rows, projector = after(first_rows, projector)
     pieces = from_everyone(projector, C)
     pieces = pieces.reshape(lax.axis_size(C), -1, *projector_basis.shape).swapaxes(0, 1)
     projector = pieces.reshape(model_width, -1)
 
-    x0_all = along_z(first_rows)
-    x1_in, x0_all, projector = after(tokens[:, half:], x0_all, projector)
-    x1_all = along_z(x1_in)
-    dy0_in, x1_all = after(cotangent[:, :half], x1_all)
-    dy0_all = along_z(dy0_in)
-    dy1_in, dy0_all = after(cotangent[:, half:], dy0_all)
-    dy1_all = along_z(dy1_in)
+    x_all = along_z(first_rows)
+    dy_in, x_all, projector = after(cotangent, x_all, projector)
+    dy_all = along_z(dy_in)
 
     def sent(rows, scaled):
-        picked = pick(base, x0_all, rows, half, top, scaled, plane, experts, cap)
+        picked = pick(base, x_all, rows, model_width, top, scaled, plane, experts, cap)
         return lax.all_to_all(picked, PLANE, split_axis=0, concat_axis=0, tiled=True)
 
-    x0, x1 = sent(x0_all, False), sent(x1_all, False)
-    dy0, dy1 = sent(dy0_all, True), sent(dy1_all, True)
-
-    act, slope_up, hidden, x_proj = forward(x0, x1, gate_weight, up_weight, projector)
-    hidden_part, proj_part = first_half(dy0, down_weight, projector)
+    x, dy = sent(x_all, False), sent(dy_all, True)
+    act, slope_up, hidden, x_proj = forward(x, gate_weight, up_weight, projector)
     gate_grad, up_grad, partial = backward(
-        dy1, down_weight, projector, hidden_part, proj_part, act, slope_up, hidden, x_proj
+        dy, down_weight, projector, act, slope_up, hidden, x_proj
     )
 
-    own_grads = sent_and_summed(partial.reshape(-1, partial.shape[-1]), Y)
-    grads_low = gathered(own_grads, Y)
+    replicas = lax.axis_size(Y)
+    arrived = exchanged(partial.reshape(replicas, -1, partial.shape[-1]), Y)
+    spread = sum_and_spread(arrived, 3)
+    grads_low = exchanged(spread, Y)
     projected_grads = grads_low.astype(f32).reshape(partial.shape)
-
+    grads_low = grads_low.reshape(-1, partial.shape[-1])
+
+    rows = row_grads_of(gate_grad, up_grad, gate_weight, up_weight, plane)
     returned = []
-    halves = row_grads_of(gate_grad, up_grad, gate_weight, up_weight, plane)
-    for rows in halves:
-        pieces = []
-        for d in range(plane):
-            piece = lax.dynamic_index_in_dim(rows, (here + d) % plane, 0, keepdims=False)
-            if d:
-                piece = lax.ppermute(piece, PLANE, [(i, (i + d) % plane) for i in range(plane)])
-            pieces.append(piece)
-        returned.append(pieces)
-
-    late_gate_grad, _ = after(gate_grad, own_grads)
-    own_weight_grads = weight_grads(x0, x1, dy0, dy1, late_gate_grad, up_grad, hidden)
+    for d in range(plane):
+        piece = lax.dynamic_index_in_dim(rows, (here + d) % plane, 0, keepdims=False)
+        if d:
+            piece = lax.ppermute(piece, PLANE, [(i, (i + d) % plane) for i in range(plane)])
+        returned.append(piece)
+
+    late_gate_grad, _ = after(gate_grad, spread)
+    own_weight_grads = weight_grads(x, dy, late_gate_grad, up_grad, hidden)
     near, far = (C, Y), (Z, X)
-    power = dot(own_weight_grads, grads_low).astype(bf16)
-    first_base, power = after(base, power)
+    power = power_of(own_weight_grads, grads_low)
+    late_base, power = after(base, power)
     power = sent_and_summed(power, near)
-    second_base, power = after(base, power)
-    power = sent_and_summed(power, far)
-    power = gathered(gathered(power, far), near)
-
-    token_parts = []
-    for when, pieces in zip((first_base, second_base), returned):
-        token_parts.append(give_back(when, x0_all, pieces, top, cap))
-    token_grads = jnp.concatenate(
-        [lax.psum_scatter(part, Z, scatter_dimension=0, tiled=True) for part in token_parts], 1
-    )
+    power = exchanged(power.reshape(lax.axis_size(far), -1, power.shape[-1]), far)
+    power = exchanged(sum_and_spread(power, 1), far).reshape(-1, power.shape[-1])
+    power = gathered(power, near)
+
+    token_parts = give_back(late_base, x_all, returned, top, cap)
+    token_grads = lax.psum_scatter(token_parts, Z, scatter_dimension=0, tiled=True)
 
     index = lax.axis_index(EXPERT).astype(jnp.int32).reshape(1)
     new_basis = new_basis_of(power, index, model_width // group_count)

time: 450 us -> 399 us (0.89)
  blocking collectives: 19.4 us -> 59.3 us
  starting transfers between devices: 79.7 us -> 53 us
  waiting for transfers between devices: 192 us -> 169 us
  Pallas kernels: 106 us -> 85.5 us
  local copies, waits for them, and re-layouts: 21.4 us -> 11 us
  matrix products: 7.27 us -> 0 us
    all_to_all x0 -> x3, blocking collectives: none -> 54.7 us  [the longest x2 34.2 us: exchanged(): return lax.all_to_all(pieces, axis, split_axis=0, concat_axis=0, tiled=True)]
    all_to_all x2 -> x1, blocking collectives: 19.4 us -> 4.58 us  [from_everyone(): return lax.all_to_all(copies, axis, split_axis=0, concat_axis=0, tiled=True)]
    all_to_all x3 -> x2, waiting for transfers between devices: 16.2 us -> 2.08 us  [exchanged(): return lax.all_to_all(pieces, axis, split_axis=0, concat_axis=0, tiled=True)]
    all_to_all x4 -> x2, waiting for transfers between devices: 51 us -> 37.6 us  [sent(): lax.all_to_all(picked, PLANE, split_axis=0, concat_axis=0, tiled=True)]
    all_to_all x4 -> x2, starting transfers between devices: 20.2 us -> 9.96 us  [sent(): lax.all_to_all(picked, PLANE, split_axis=0, concat_axis=0, tiled=True)]
    pallas_call x1, Pallas kernels: 26.7 us -> 16.9 us  [new_basis_of(): pl.pallas_call(lambda *refs: new_basis_body(math.sqrt(width), *refs), out...]
    all_gather x4 -> x2, waiting for transfers between devices: 82.4 us -> 91.3 us  [along_z(): return lax.all_gather(value, Z, axis=0, tiled=True)]
    pallas_call x4 -> x2, Pallas kernels: 21.9 us -> 13.4 us  [pick(): pl.pallas_call(lambda *refs: pick_body(top, scaled, *refs), out_shape=jax...]
  transfers between devices with their start and end apart: 30 -> 16, of which waited for: 12 -> 8; matrix products, arithmetic and copies ran while one was open for 5% -> 2% of each run, Pallas kernels for 21% -> 18%
where the time goes in v2:
time: 399 us; the launch traced here: 395 us
  waiting for transfers between devices  169 us (42%)
  Pallas kernels  85.5 us (21%)
  blocking collectives  59.3 us (15%)
  starting transfers between devices  53 us (13%)
  between operations  13.9 us (3%)
  local copies, waits for them, and re-layouts  11 us (3%)
    all_gather x2, waiting for transfers between devices, along_z(): return lax.all_gather(value, Z, axis=0, tiled=True)  91.3 us
    all_to_all x2, waiting for transfers between devices, sent(): lax.all_to_all(picked, PLANE, split_axis=0, concat_axis=0, tiled=True)  37.6 us
    all_to_all x2, blocking collectives, exchanged(): return lax.all_to_all(pieces, axis, split_axis=0, concat_axis=0, tiled=True)  34.2 us
    all_to_all x2, waiting for transfers between devices, from_everyone(): return lax.all_to_all(copies, axis, split_axis=0, concat_axis=0, tiled=True)  28.3 us
    all_to_all x1, blocking collectives, sent_and_summed(): lax.all_to_all(pieces, axis, split_axis=0, concat_axis=0, tiled=True)  20.5 us
    ppermute x7, starting transfers between devices, layer(): lax.ppermute(piece, PLANE, [(i, (i + d) % plane) for i in range(plane)])  19.9 us
    pallas_call x1, Pallas kernels, new_basis_of(): pl.pallas_call(lambda *refs: new_basis_body(math.sqrt(width), *refs), out...  16.9 us
    all_to_all x2, starting transfers between devices, from_everyone(): return lax.all_to_all(copies, axis, split_axis=0, concat_axis=0, tiled=True)  15.2 us
  transfers between devices with their start and end apart: 16, of which 8 were waited for; matrix products, arithmetic and copies ran while one was open for 2% of the time, Pallas kernels for 18%

profile of v2, /device:TPU:2, one launch (start us, length us, event | category | flops | bytes accessed | tf_op | source)
XLA Modules:
  0.0 395.2 jit_solution(15698939566947151462)
XLA Ops:
  7.2 0.8 multiply_convert_fusion
  7.9 0.9 broadcast_in_dim.9
  8.8 11.6 %all-to-all-start = ((bf16[32,32,256]{2,1,0:T(8,128)(2,1)}), bf16[32,32,256]{2,1,0:T(8,128)(2,1)S(1)}, u32[]{:S(2)}, u32[]{:S(2)}) async-start(bf16[32,32,256]{2,1,0:T(8,128)(2,1)} %broadcast_in_dim.9), calls=%async_computation | async-start | bytes 1048576 | tf_op jit(solution)/shard_map/all_to_all | solution.py:36
  20.4 0.0 all-gather.3.cloned.1.call-start
  20.5 2.0 packed.1
  22.5 14.8 %all-to-all-done = bf16[32,32,256]{2,1,0:T(8,128)(2,1)S(1)} async-done(((bf16[32,32,256]{2,1,0:T(8,128)(2,1)}), bf16[32,32,256]{2,1,0:T(8,128)(2,1)S(1)}, u32[]{:S(2)}, u32[]{:S(2)}) %all-to-all-start) | async-done | bytes 524320 | tf_op jit(solution)/shard_map/all_to_all | solution.py:36
  37.2 0.0 all-gather.3.cloned.1.call-update
  37.3 0.0 all-gather.5.cloned.1.call-start
  37.3 0.1 broadcast_in_dim.10
  37.4 4.6 %all_to_all.50 = bf16[2,1024,256]{2,1,0:T(8,128)(2,1)S(1)} all-to-all(bf16[2,1024,256]{2,1,0:T(8,128)(2,1)S(1)} %broadcast_in_dim.10), channel_id=1, replica_groups=mesh['expert_0'=8,'expert_1'=4,'expert_2'=2,'replica'=4] {'expert_2'}, dimensions={0} | all-to-all | bytes 2097152 | tf_op jit(solution)/shard_map/all_to_all | solution.py:36
  42.0 1.1 copy.13
  43.1 48.4 %all-gather.3.cloned.1.call-done.refs_1_.refs_2_ = bf16[1024,2176]{1,0:T(8,128)(2,1)} async-done(((bf16[128,2176]{1,0:T(8,128)(2,1)}), bf16[1024,2176]{1,0:T(8,128)(2,1)}) %all-gather.3.cloned.1.call-update) | async-done | bytes 4456464 | tf_op jit(solution)/shard_map/all_gather | solution.py:443
  91.5 0.0 all-gather.5.cloned.1.call-update
  91.6 0.7 pad_add_fusion.refs_0_
  92.2 6.6 %pick.1 = bf16[8,2,64,2048]{3,2,1,0:T(8,128)(2,1)} custom-call(s32[2]{0:T(128)} %pad_add_fusion.refs_0_, bf16[1024,2176]{1,0:T(8,128)(2,1)} %all-gather.3.cloned.1.call-done.refs_1_.refs_2_, bf16[1024,2176]{1,0:T(8,128)(2,1)} %all-gather.3.cloned.1.call-done.refs_1_.refs_2_), custom_call_target="tpu_custom_call" | custom-call | flops 1073741824 | bytes 8388608 | tf_op jit(solution)/shard_map/pick/pallas_call | solution.py:136
  98.9 5.0 %all-to-all-start.2 = ((bf16[8,2,64,2048]{3,2,1,0:T(8,128)(2,1)}), bf16[8,2,64,2048]{3,2,1,0:T(8,128)(2,1)}, u32[]{:S(2)}, u32[]{:S(2)}) async-start(bf16[8,2,64,2048]{3,2,1,0:T(8,128)(2,1)} %pick.1), calls=%async_computation.2 | async-start | bytes 8388608 | tf_op jit(solution)/shard_map/all_to_all | solution.py:462
  103.8 42.9 %all-gather.5.cloned.1.call-done.refs_2_ = bf16[1024,2048]{1,0:T(8,128)(2,1)} async-done(((bf16[128,2048]{1,0:T(8,128)(2,1)}), bf16[1024,2048]{1,0:T(8,128)(2,1)}) %all-gather.5.cloned.1.call-update) | async-done | bytes 4194320 | tf_op jit(solution)/shard_map/all_gather | solution.py:443
  146.7 6.8 %pick_scaled.1 = bf16[8,2,64,2048]{3,2,1,0:T(8,128)(2,1)} custom-call(s32[2]{0:T(128)} %pad_add_fusion.refs_0_, bf16[1024,2176]{1,0:T(8,128)(2,1)} %all-gather.3.cloned.1.call-done.refs_1_.refs_2_, bf16[1024,2048]{1,0:T(8,128)(2,1)} %all-gather.5.cloned.1.call-done.refs_2_), custom_call_target="tpu_custom_call" | custom-call | flops 1073741824 | bytes 8388608 | tf_op jit(solution)/shard_map/pick_scaled/pallas_call | solution.py:136
  153.5 0.0 all-to-all-done.2.x
  153.5 5.0 %all-to-all-start.3 = ((bf16[8,2,64,2048]{3,2,1,0:T(8,128)(2,1)}), bf16[8,2,64,2048]{3,2,1,0:T(8,128)(2,1)}, u32[]{:S(2)}, u32[]{:S(2)}) async-start(bf16[8,2,64,2048]{3,2,1,0:T(8,128)(2,1)} %pick_scaled.1), calls=%async_computation.3 | async-start | bytes 8388608 | tf_op jit(solution)/shard_map/all_to_all | solution.py:462
  158.4 10.7 %forward.1 = (f32[2,512,384]{2,1,0:T(8,128)}, f32[2,512,384]{2,1,0:T(8,128)}, bf16[2,512,384]{2,1,0:T(8,128)(2,1)}, bf16[2,512,256]{2,1,0:T(8,128)(2,1)}) custom-call(bf16[8,2,64,2048]{3,2,1,0:T(8,128)(2,1)} %all-to-all-done.2.x, bf16[2,2048,384]{2,1,0:T(8,128)(2,1)} %gate_w.3, bf16[2,2048,384]{2,1,0:T(8,128)(2,1)} %up_w.3, bf16[2048,256]{1,0:T(8,128)(2,1)} %bitcast.41), custom_call_target="tpu_custom_call" | custom-call | flops 4294967296 | bytes 16000000 | tf_op jit(solution)/shard_map/forward/pallas_call | solution.py:217
  169.1 37.6 %all-to-all-done.3.dy = bf16[8,2,64,2048]{3,2,1,0:T(8,128)(2,1)} async-done(((bf16[8,2,64,2048]{3,2,1,0:T(8,128)(2,1)}), bf16[8,2,64,2048]{3,2,1,0:T(8,128)(2,1)}, u32[]{:S(2)}, u32[]{:S(2)}) %all-to-all-start.3) | async-done | bytes 4194336 | tf_op jit(solution)/shard_map/all_to_all | solution.py:462
  206.8 8.6 %backward.1 = (bf16[2,512,384]{2,1,0:T(8,128)(2,1)}, bf16[2,512,384]{2,1,0:T(8,128)(2,1)}, bf16[2,3,384,256]{3,2,1,0:T(8,128)(2,1)}) custom-call(bf16[8,2,64,2048]{3,2,1,0:T(8,128)(2,1)} %all-to-all-done.3.dy, bf16[2,384,2048]{2,1,0:T(8,128)(2,1)} %down_w.1, bf16[2048,256]{1,0:T(8,128)(2,1)} %bitcast.42, f32[2,512,384]{2,1,0:T(8,128)} %get-tuple-element.23.act, ...), custom_call_target="tpu_custom_call" | custom-call | flops 3288334336 | bytes 16000000 | tf_op jit(solution)/shard_map/backward/pallas_call | solution.py:250
  215.4 4.3 %all-to-all-start.4 = ((bf16[4,576,256]{2,1,0:T(8,128)(2,1)}), bf16[4,576,256]{2,1,0:T(8,128)(2,1)S(1)}, u32[]{:S(2)}, u32[]{:S(2)}) async-start(bf16[4,576,256]{2,1,0:T(8,128)(2,1)} %bitcast.45), calls=%async_computation.4 | async-start | bytes 2359296 | tf_op jit(solution)/shard_map/all_to_all | solution.py:67
  219.6 9.8 %row_grads.1 = bf16[8,2,64,2048]{3,2,1,0:T(8,128)(2,1)} custom-call(bf16[2,512,384]{2,1,0:T(8,128)(2,1)} %get-tuple-element.29.gate_grad, bf16[2,512,384]{2,1,0:T(8,128)(2,1)} %get-tuple-element.30.up_grad, bf16[2,2048,384]{2,1,0:T(8,128)(2,1)} %gate_w.3, bf16[2,2048,384]{2,1,0:T(8,128)(2,1)} %up_w.3), custom_call_target="tpu_custom_call" | custom-call | flops 3221225472 | bytes 12000000 | tf_op jit(solution)/shard_map/row_grads/pallas_call | solution.py:278
  229.4 4.2 %dynamic-slice_bitcast_fusion = (bf16[2,64,2048]{2,1,0:T(8,128)(2,1)}, bf16[2,64,2048]{2,1,0:T(8,128)(2,1)}, bf16[2,64,2048]{2,1,0:T(8,128)(2,1)}, bf16[2,64,204...) fusion(bf16[8,2,64,2048]{3,2,1,0:T(8,128)(2,1)} %row_grads.1, ...), kind=kLoop, calls=%fused_computation | loop fusion | bytes 8388640 | tf_op jit(solution)/shard_map/jit(dynamic_index_in_dim)/squeeze | solution.py:480
  233.6 0.0 copy-start.1
  233.6 0.0 copy-start.3
  233.7 0.0 collective-permute-start
  233.7 0.1 collective-permute-start.1
  233.8 2.1 all-to-all-done.4.arrived
  235.8 1.7 sum_and_spread.2
  237.5 3.5 all-to-all-start.5
  241.1 0.0 reduce-scatter.2.cloned.1.call-start
  241.1 2.3 collective-permute-start.2
  243.4 0.5 collective-permute-start.3
  243.8 2.9 collective-permute-start.4
  246.7 0.8 collective-permute-done.refs_3_
  247.5 2.7 collective-permute-start.5
  250.2 0.0 collective-permute-done.1.refs_4_
  250.2 11.6 %collective-permute-start.6 = (bf16[2,64,2048]{2,1,0:T(8,128)(2,1)}, bf16[2,64,2048]{2,1,0:T(8,128)(2,1)}, u32[]{:S(2)}, u32[]{:S(2)}) collective-permute-start(bf16[2,64,2048]{2,1,0:T(8,128)(2,1)} %get-tuple-element.33), channel_id=1, source_target_pairs={{0,28},{4,0},{8,4},{12,8},{16,12},{20,16},{24,20},{28,24},{1,29},{... | collective-permute-start | bytes 1572872 | tf_op jit(solution)/shard_map/ppermute | solution.py:482
  261.8 0.0 copy-done.1
  261.8 0.0 copy-done.2
  261.8 0.0 copy-done.3
  261.8 11.2 %weight_grads.1.weights = bf16[2048,2304]{1,0:T(8,128)(2,1)} custom-call(bf16[8,2,64,2048]{3,2,1,0:T(8,128)(2,1)} %all-to-all-done.2.x, bf16[8,2,64,2048]{3,2,1,0:T(8,128)(2,1)} %all-to-all-done.3.dy, bf16[2,512,384]{2,1,0:T(8,128)(2,1)S(1)} %copy-done.2, bf16[2,512,384]{2,1,0:T(8,128)(2,1)S(1)} %copy-done.3, bf16[2,512,384]{2,1,0:T(8,128)(2,1)S(1)} %copy-done.1), custom_call_target="tpu_custom_call" | custom-call | flops 4831838208 | bytes 24000000 | tf_op jit(solution)/shard_map/weight_grads/pallas_call | solution.py:303
  272.9 0.0 all-to-all-done.5
  272.9 3.7 copy-done
  276.6 3.8 power.1
  280.5 0.0 collective-permute-done.2.refs_5_
  280.5 0.0 collective-permute-done.3.refs_6_
  280.5 0.0 collective-permute-done.4.refs_7_
  280.5 0.0 collective-permute-done.5.refs_8_
  280.5 9.0 %collective-permute-done.6.refs_9_ = bf16[2,64,2048]{2,1,0:T(8,128)(2,1)} collective-permute-done((bf16[2,64,2048]{2,1,0:T(8,128)(2,1)}, bf16[2,64,2048]{2,1,0:T(8,128)(2,1)}, u32[]{:S(2)}, u32[]{:S(2)}) %collective-permute-start.6) | collective-permute-done | bytes 524320 | tf_op jit(solution)/shard_map/ppermute | solution.py:482
  289.6 7.4 %give_back.1 = bf16[1024,2048]{1,0:T(8,128)(2,1)} custom-call(s32[2]{0:T(128)} %pad_add_fusion.refs_0_, bf16[1024,2176]{1,0:T(8,128)(2,1)} %all-gather.3.cloned.1.call-done.refs_1_.refs_2_, bf16[2,64,2048]{2,1,0:T(8,128)(2,1)} %get-tuple-element.40.refs_2_, bf16[2,64,2048]{2,1,0:T(8,128)(2,1)} %collective-permute-done.refs_3_, ...), custom_call_target="tpu_custom_call" | custom-call | flops 1073741824 | bytes 8388608 | tf_op jit(solution)/shard_map/give_back/pallas_call | solution.py:178
  297.0 0.0 reduce-scatter.2.cloned.1.call-update
  297.0 20.5 %all_to_all.51 = bf16[8,256,256]{2,1,0:T(8,128)(2,1)S(1)} all-to-all(bf16[8,256,256]{2,1,0:T(8,128)(2,1)S(1)} %bitcast.38), channel_id=1, replica_groups=mesh['expert_0'=8,'expert_1'=4,'expert_2'=2,'replica'=4] {'expert_2','re..., dimensions={0} | all-to-all | bytes 2097152 | tf_op jit(solution)/shard_map/all_to_all | solution.py:42
  317.5 0.1 reduce_sum.12
  317.7 18.5 %all_to_all.52.arrived = bf16[32,8,256]{2,1,0:T(8,128)(2,1)S(1)} all-to-all(bf16[32,8,256]{2,1,0:T(8,128)(2,1)S(1)} %bitcast.46), channel_id=1, replica_groups=mesh['expert_0'=8,'expert_1'=4,'expert_2'=2,'replica'=4] {'expert_0','ex..., dimensions={0} | all-to-all | bytes 262144 | tf_op jit(solution)/shard_map/all_to_all | solution.py:67
  336.3 15.6 %all_to_all.53 = bf16[32,8,256]{2,1,0:T(8,128)(2,1)S(1)} all-to-all(bf16[32,8,256]{2,1,0:T(8,128)(2,1)S(1)} %sum_and_spread.3), channel_id=1, replica_groups=mesh['expert_0'=8,'expert_1'=4,'expert_2'=2,'replica'=4] {'expert_0','ex..., dimensions={0} | all-to-all | bytes 262144 | tf_op jit(solution)/shard_map/all_to_all | solution.py:67
  351.9 1.1 broadcast_in_dim.11
  353.0 3.6 all-to-all-start.9
  356.6 1.6 convert.2
  358.2 13.6 %all-to-all-done.9 = bf16[8,256,256]{2,1,0:T(8,128)(2,1)S(1)} async-done(((bf16[8,256,256]{2,1,0:T(8,128)(2,1)}), bf16[8,256,256]{2,1,0:T(8,128)(2,1)S(1)}, u32[]{:S(2)}, u32[]{:S(2)}) %all-to-all-start.9) | async-done | bytes 1048608 | tf_op jit(solution)/shard_map/all_to_all | solution.py:36
  371.7 16.9 %new_basis.1 = f32[32,256]{1,0:T(8,128)} custom-call(s32[1]{0:T(128)} %bitcast.21.refs_0_, bf16[2048,256]{1,0:T(8,128)(2,1)S(1)} %bitcast.39, bf16[2048,256]{1,0:T(8,128)(2,1)S(1)} %bitcast.40), custom_call_target="tpu_custom_call" | custom-call | flops 30000001024 | bytes 2000000 | tf_op jit(solution)/shard_map/new_basis/pallas_call | solution.py:398
  (4 shorter events, 0.0 us)
Async XLA Ops:
  8.8 28.5 %all-to-all-start = ((bf16[32,32,256]{2,1,0:T(8,128)(2,1)}), bf16[32,32,256]{2,1,0:T(8,128)(2,1)S(1)}, u32[]{:S(2)}, u32[]{:S(2)}) async-start(bf16[32,32,256]{2,1,0:T(8,128)(2,1)} %broadcast_in_dim.9), calls=%async_computation | async-start | bytes 1048576 | tf_op jit(solution)/shard_map/all_to_all | solution.py:36
  20.4 71.1 %all-gather.3.cloned.1.call-start = ((), (), s32[]{:S(2)}) async-start(), calls=%async_computation.11 | async-start | bytes 5013504 | tf_op jit(solution)/shard_map/all_gather | solution.py:443
  37.3 109.4 %all-gather.5.cloned.1.call-start = ((), (), s32[]{:S(2)}) async-start(), calls=%async_computation.12 | async-start | bytes 4718592 | tf_op jit(solution)/shard_map/all_gather | solution.py:443
  98.9 54.6 %all-to-all-start.2 = ((bf16[8,2,64,2048]{3,2,1,0:T(8,128)(2,1)}), bf16[8,2,64,2048]{3,2,1,0:T(8,128)(2,1)}, u32[]{:S(2)}, u32[]{:S(2)}) async-start(bf16[8,2,64,2048]{3,2,1,0:T(8,128)(2,1)} %pick.1), calls=%async_computation.2 | async-start | bytes 8388608 | tf_op jit(solution)/shard_map/all_to_all | solution.py:462
  153.5 53.3 %all-to-all-start.3 = ((bf16[8,2,64,2048]{3,2,1,0:T(8,128)(2,1)}), bf16[8,2,64,2048]{3,2,1,0:T(8,128)(2,1)}, u32[]{:S(2)}, u32[]{:S(2)}) async-start(bf16[8,2,64,2048]{3,2,1,0:T(8,128)(2,1)} %pick_scaled.1), calls=%async_computation.3 | async-start | bytes 8388608 | tf_op jit(solution)/shard_map/all_to_all | solution.py:462
  215.4 20.5 %all-to-all-start.4 = ((bf16[4,576,256]{2,1,0:T(8,128)(2,1)}), bf16[4,576,256]{2,1,0:T(8,128)(2,1)S(1)}, u32[]{:S(2)}, u32[]{:S(2)}) async-start(bf16[4,576,256]{2,1,0:T(8,128)(2,1)} %bitcast.45), calls=%async_computation.4 | async-start | bytes 2359296 | tf_op jit(solution)/shard_map/all_to_all | solution.py:67
  233.6 28.1 %copy-start.1 = (bf16[2,512,384]{2,1,0:T(8,128)(2,1)S(1)}, bf16[2,512,384]{2,1,0:T(8,128)(2,1)}, u32[]{:S(2)}) copy-start(bf16[2,512,384]{2,1,0:T(8,128)(2,1)} %get-tuple-element.25.hidden) | copy-start | bytes 2359300
  233.6 28.1 %copy-start.2 = (bf16[2,512,384]{2,1,0:T(8,128)(2,1)S(1)}, bf16[2,512,384]{2,1,0:T(8,128)(2,1)}, u32[]{:S(2)}) copy-start(bf16[2,512,384]{2,1,0:T(8,128)(2,1)} %get-tuple-element.29.gate_grad) | copy-start | bytes 2359300
  233.6 28.1 %copy-start.3 = (bf16[2,512,384]{2,1,0:T(8,128)(2,1)S(1)}, bf16[2,512,384]{2,1,0:T(8,128)(2,1)}, u32[]{:S(2)}) copy-start(bf16[2,512,384]{2,1,0:T(8,128)(2,1)} %get-tuple-element.30.up_grad) | copy-start | bytes 2359300
  233.7 13.9 %collective-permute-start = (bf16[2,64,2048]{2,1,0:T(8,128)(2,1)}, bf16[2,64,2048]{2,1,0:T(8,128)(2,1)}, u32[]{:S(2)}, u32[]{:S(2)}) collective-permute-start(bf16[2,64,2048]{2,1,0:T(8,128)(2,1)} %get-tuple-element.39), channel_id=1, source_target_pairs={{0,4},{4,8},{8,12},{12,16},{16,20},{20,24},{24,28},{28,0},{1,5},{5... | collective-permute-start | bytes 1572872 | tf_op jit(solution)/shard_map/ppermute | solution.py:482
  233.7 16.5 %collective-permute-start.1 = (bf16[2,64,2048]{2,1,0:T(8,128)(2,1)}, bf16[2,64,2048]{2,1,0:T(8,128)(2,1)}, u32[]{:S(2)}, u32[]{:S(2)}) collective-permute-start(bf16[2,64,2048]{2,1,0:T(8,128)(2,1)} %get-tuple-element.38), channel_id=1, source_target_pairs={{0,8},{4,12},{8,16},{12,20},{16,24},{20,28},{24,0},{28,4},{1,9},{5... | collective-permute-start | bytes 1572872 | tf_op jit(solution)/shard_map/ppermute | solution.py:482
  237.5 35.4 %all-to-all-start.5 = ((bf16[4,576,256]{2,1,0:T(8,128)(2,1)}), bf16[4,576,256]{2,1,0:T(8,128)(2,1)S(1)}, u32[]{:S(2)}, u32[]{:S(2)}) async-start(bf16[4,576,256]{2,1,0:T(8,128)(2,1)} %sum_and_spread.2), calls=%async_computation.5 | async-start | bytes 2359296 | tf_op jit(solution)/shard_map/all_to_all | solution.py:67
  241.1 147.6 %reduce-scatter.2.cloned.1.call-start = ((), (), s32[]{:S(2)}) async-start(), calls=%async_computation.13 | async-start | bytes 4718592 | tf_op jit(solution)/shard_map/reduce_scatter | solution.py:496
  241.1 39.4 %collective-permute-start.2 = (bf16[2,64,2048]{2,1,0:T(8,128)(2,1)}, bf16[2,64,2048]{2,1,0:T(8,128)(2,1)}, u32[]{:S(2)}, u32[]{:S(2)}) collective-permute-start(bf16[2,64,2048]{2,1,0:T(8,128)(2,1)} %get-tuple-element.37), channel_id=1, source_target_pairs={{0,12},{4,16},{8,20},{12,24},{16,28},{20,0},{24,4},{28,8},{1,13},{... | collective-permute-start | bytes 1572872 | tf_op jit(solution)/shard_map/ppermute | solution.py:482
  243.4 37.1 %collective-permute-start.3 = (bf16[2,64,2048]{2,1,0:T(8,128)(2,1)}, bf16[2,64,2048]{2,1,0:T(8,128)(2,1)}, u32[]{:S(2)}, u32[]{:S(2)}) collective-permute-start(bf16[2,64,2048]{2,1,0:T(8,128)(2,1)} %get-tuple-element.36), channel_id=1, source_target_pairs={{0,16},{4,20},{8,24},{12,28},{16,0},{20,4},{24,8},{28,12},{1,17},{... | collective-permute-start | bytes 1572872 | tf_op jit(solution)/shard_map/ppermute | solution.py:482
  243.8 36.7 %collective-permute-start.4 = (bf16[2,64,2048]{2,1,0:T(8,128)(2,1)}, bf16[2,64,2048]{2,1,0:T(8,128)(2,1)}, u32[]{:S(2)}, u32[]{:S(2)}) collective-permute-start(bf16[2,64,2048]{2,1,0:T(8,128)(2,1)} %get-tuple-element.35), channel_id=1, source_target_pairs={{0,20},{4,24},{8,28},{12,0},{16,4},{20,8},{24,12},{28,16},{1,21},{... | collective-permute-start | bytes 1572872 | tf_op jit(solution)/shard_map/ppermute | solution.py:482
  247.5 33.0 %collective-permute-start.5 = (bf16[2,64,2048]{2,1,0:T(8,128)(2,1)}, bf16[2,64,2048]{2,1,0:T(8,128)(2,1)}, u32[]{:S(2)}, u32[]{:S(2)}) collective-permute-start(bf16[2,64,2048]{2,1,0:T(8,128)(2,1)} %get-tuple-element.34), channel_id=1, source_target_pairs={{0,24},{4,28},{8,0},{12,4},{16,8},{20,12},{24,16},{28,20},{1,25},{... | collective-permute-start | bytes 1572872 | tf_op jit(solution)/shard_map/ppermute | solution.py:482
  250.2 39.4 %collective-permute-start.6 = (bf16[2,64,2048]{2,1,0:T(8,128)(2,1)}, bf16[2,64,2048]{2,1,0:T(8,128)(2,1)}, u32[]{:S(2)}, u32[]{:S(2)}) collective-permute-start(bf16[2,64,2048]{2,1,0:T(8,128)(2,1)} %get-tuple-element.33), channel_id=1, source_target_pairs={{0,28},{4,0},{8,4},{12,8},{16,12},{20,16},{24,20},{28,24},{1,29},{... | collective-permute-start | bytes 1572872 | tf_op jit(solution)/shard_map/ppermute | solution.py:482
  272.9 3.7 copy-start
  353.0 18.8 %all-to-all-start.9 = ((bf16[8,256,256]{2,1,0:T(8,128)(2,1)}), bf16[8,256,256]{2,1,0:T(8,128)(2,1)S(1)}, u32[]{:S(2)}, u32[]{:S(2)}) async-start(bf16[8,256,256]{2,1,0:T(8,128)(2,1)} %broadcast_in_dim.11), calls=%async_computation.10 | async-start | bytes 2097152 | tf_op jit(solution)/shard_map/all_to_all | solution.py:36
Sparse Core Ops, SparseCore 0:
  37.4 54.0 all-gather.2
  93.3 53.3 all-gather.4
  297.1 61.0 reduce-scatter.1

commit v3 on v2

--- a/solution.py
+++ b/solution.py
@@ -113,21 +113,26 @@
 
 
 def pick_body(top, scaled, base_ref, routes_ref, rows_ref, out_ref):
-    slots = rows_ref.shape[0]
+    slots, width = rows_ref.shape[0] // PAIR, rows_ref.shape[1]
     routes = routes_ref[...].astype(f32).T
-    want = want_slots((slots, slots), 0, base_ref[0], lambda block: block)
-    chosen = jnp.zeros((slots, slots), f32)
-    scale = jnp.zeros((slots, slots), f32)
-    for k, key in keys_of(routes, top, 1):
-        hit = key == want
-        chosen = jnp.where(hit, 1.0, chosen)
+    want = (lax.broadcasted_iota(jnp.int32, (slots, slots), 0) + base_ref[0]).astype(f32)
+    devices, experts, places = out_ref.shape[:3]
+    blocks = []
+    for source in range(PAIR):
+        part = slice(source * slots, (source + 1) * slots)
+        chosen = jnp.zeros((slots, slots), f32)
+        scale = jnp.zeros((slots, slots), f32)
+        for k in range(top):
+            own = [routes[n * top + k : n * top + k + 1, part] for n in range(5)]
+            hit = own[0] * RADIX + own[1] == want
+            chosen = jnp.where(hit, 1.0, chosen)
+            if scaled:
+                scale = jnp.where(hit, own[2] + own[3] + own[4], scale)
+        picked = dot(chosen.astype(bf16), rows_ref[part])
         if scaled:
-            part = lambda n: routes[n * top + k : n * top + k + 1, :]
-            scale = jnp.where(hit, part(2) + part(3) + part(4), scale)
-    picked = dot(chosen.astype(bf16), rows_ref[...])
-    if scaled:
-        picked = picked * jnp.sum(scale, axis=1, keepdims=True)
-    out_ref[...] = picked.astype(bf16).reshape(out_ref.shape)
+            picked = picked * jnp.sum(scale, axis=1, keepdims=True)
+        blocks.append(picked.reshape(devices, experts, places // PAIR, width))
+    out_ref[...] = jnp.concatenate(blocks, 2).astype(bf16)
 
 
 def pick(base, routed, rows, width, top, scaled, devices, experts, cap):
@@ -330,7 +335,7 @@
         ],
         out_specs=pl.BlockSpec((part, rank), lambda i: (i, 0)),
         cost_estimate=cost(2 * width * depth * rank, 12e6),
-        compiler_params=pltpu.CompilerParams(vmem_limit_bytes=20 * 2**20),
+        compiler_params=pltpu.CompilerParams(vmem_limit_bytes=58 * 2**20),
         name="power",
     )(weights, grads)
 
@@ -445,13 +450,17 @@
     def after(value, *earlier):
         return lax.optimization_barrier((value, *earlier))
 
+    first_rows = packed(tokens, cap, expert_ids, slot_ids, kept_mask, route_weights)
+
+    panel_rows, rank = projector_basis.shape
+    replicas = lax.axis_size(Y)
+    share = panel_rows // replicas
     projector = (projector_basis * (1.0 / math.sqrt(model_width))).astype(bf16)
-    projector = gathered(projector, (Z, X))
-    first_rows = packed(tokens, cap, expert_ids, slot_ids, kept_mask, route_weights)
-    first_rows, projector = after(first_rows, projector)
-    pieces = from_everyone(projector, C)
-    pieces = pieces.reshape(lax.axis_size(C), -1, *projector_basis.shape).swapaxes(0, 1)
-    projector = pieces.reshape(model_width, -1)
+    projector = lax.dynamic_slice_in_dim(projector, lax.axis_index(Y) * share, share, 0)
+    projector, first_rows = after(projector, first_rows)
+    pieces = from_everyone(gathered(projector, (Z, X)), (C, Y))
+    pieces = pieces.reshape(lax.axis_size(C), replicas, -1, share, rank)
+    projector = pieces.transpose(2, 0, 1, 3, 4).reshape(model_width, rank)
 
     x_all = along_z(first_rows)
     dy_in, x_all, projector = after(cotangent, x_all, projector)
@@ -467,7 +476,6 @@
         dy, down_weight, projector, act, slope_up, hidden, x_proj
     )
 
-    replicas = lax.axis_size(Y)
     arrived = exchanged(partial.reshape(replicas, -1, partial.shape[-1]), Y)
     spread = sum_and_spread(arrived, 3)
     grads_low = exchanged(spread, Y)

time: 399 us -> 379 us (0.950)
  waiting for transfers between devices: 169 us -> 123 us
  blocking collectives: 59.3 us -> 94.5 us
  starting transfers between devices: 53 us -> 41.4 us
  Pallas kernels: 85.5 us -> 90.3 us
    all_to_all x1 -> x2, blocking collectives: 4.58 us -> 39.8 us  [from_everyone(): return lax.all_to_all(copies, axis, split_axis=0, concat_axis=0, tiled=True)]
    all_gather x2, waiting for transfers between devices: 91.3 us -> 62.4 us  [along_z(): return lax.all_gather(value, Z, axis=0, tiled=True)]
    all_to_all x2 -> x1, waiting for transfers between devices: 28.3 us -> 13.6 us  [from_everyone(): return lax.all_to_all(copies, axis, split_axis=0, concat_axis=0, tiled=True)]
    all_to_all x2 -> x1, starting transfers between devices: 15.2 us -> 3.56 us  [from_everyone(): return lax.all_to_all(copies, axis, split_axis=0, concat_axis=0, tiled=True)]
    pallas_call x1, Pallas kernels: 3.85 us -> 9.02 us  [power_of(): pl.pallas_call(power_body, out_shape=jax.ShapeDtypeStruct((width, rank),...]
  transfers between devices with their start and end apart: 16 -> 15, of which waited for: 8 -> 7; matrix products, arithmetic and copies ran while one was open for 2% -> 2% of each run, Pallas kernels for 18% -> 19%
where the time goes in v3:
time: 379 us; the launch traced here: 375 us
  waiting for transfers between devices  123 us (32%)
  blocking collectives  94.5 us (25%)
  Pallas kernels  90.3 us (24%)
  starting transfers between devices  41.4 us (11%)
  between operations  13.9 us (4%)
  local copies, waits for them, and re-layouts  8.76 us (2%)
    all_gather x2, waiting for transfers between devices, along_z(): return lax.all_gather(value, Z, axis=0, tiled=True)  62.4 us
    all_to_all x2, blocking collectives, from_everyone(): return lax.all_to_all(copies, axis, split_axis=0, concat_axis=0, tiled=True)  39.8 us
    all_to_all x2, waiting for transfers between devices, sent(): lax.all_to_all(picked, PLANE, split_axis=0, concat_axis=0, tiled=True)  37.6 us
    all_to_all x2, blocking collectives, exchanged(): return lax.all_to_all(pieces, axis, split_axis=0, concat_axis=0, tiled=True)  34.2 us
    all_to_all x1, blocking collectives, sent_and_summed(): lax.all_to_all(pieces, axis, split_axis=0, concat_axis=0, tiled=True)  20.5 us
    ppermute x7, starting transfers between devices, layer(): lax.ppermute(piece, PLANE, [(i, (i + d) % plane) for i in range(plane)])  19.9 us
    pallas_call x1, Pallas kernels, new_basis_of(): pl.pallas_call(lambda *refs: new_basis_body(math.sqrt(width), *refs), out...  16.9 us
    all_to_all x1, waiting for transfers between devices, from_everyone(): return lax.all_to_all(copies, axis, split_axis=0, concat_axis=0, tiled=True)  13.6 us
  transfers between devices with their start and end apart: 15, of which 7 were waited for; matrix products, arithmetic and copies ran while one was open for 2% of the time, Pallas kernels for 19%

profile of v3, /device:TPU:2, one launch (start us, length us, event | category | flops | bytes accessed | tf_op | source)
XLA Modules:
  0.0 375.2 jit_solution(5512460961631391560)
XLA Ops:
  7.2 0.0 all-gather.3.cloned.1.call-start
  7.2 0.7 fusion
  7.9 2.0 packed.1
  9.9 0.0 all-gather.3.cloned.1.call-update
  9.9 0.0 all-gather.5.cloned.1.call-start
  10.0 20.3 %all_to_all.50 = bf16[32,8,256]{2,1,0:T(8,128)(2,1)S(1)} all-to-all(bf16[32,8,256]{2,1,0:T(8,128)(2,1)S(1)} %broadcast_in_dim.9), channel_id=1, replica_groups=mesh['expert_0'=8,'expert_1'=4,'expert_2'=2,'replica'=4] {'expert_0','ex..., dimensions={0} | all-to-all | bytes 262144 | tf_op jit(solution)/shard_map/all_to_all | solution.py:36
  30.3 0.1 broadcast_in_dim.10
  30.4 19.6 %all_to_all.51 = bf16[8,256,256]{2,1,0:T(8,128)(2,1)S(1)} all-to-all(bf16[8,256,256]{2,1,0:T(8,128)(2,1)S(1)} %broadcast_in_dim.10), channel_id=1, replica_groups=mesh['expert_0'=8,'expert_1'=4,'expert_2'=2,'replica'=4] {'expert_2','re..., dimensions={0} | all-to-all | bytes 2097152 | tf_op jit(solution)/shard_map/all_to_all | solution.py:36
  49.9 1.2 copy.13
  51.1 19.7 %all-gather.3.cloned.1.call-done.refs_1_.refs_2_ = bf16[1024,2176]{1,0:T(8,128)(2,1)} async-done(((bf16[128,2176]{1,0:T(8,128)(2,1)}), bf16[1024,2176]{1,0:T(8,128)(2,1)}) %all-gather.3.cloned.1.call-update) | async-done | bytes 4456464 | tf_op jit(solution)/shard_map/all_gather | solution.py:448
  70.8 0.0 all-gather.5.cloned.1.call-update
  70.9 0.7 pad_add_fusion.refs_0_
  71.5 6.4 %pick.1 = bf16[8,2,64,2048]{3,2,1,0:T(8,128)(2,1)} custom-call(s32[2]{0:T(128)} %pad_add_fusion.refs_0_, bf16[1024,2176]{1,0:T(8,128)(2,1)} %all-gather.3.cloned.1.call-done.refs_1_.refs_2_, bf16[1024,2176]{1,0:T(8,128)(2,1)} %all-gather.3.cloned.1.call-done.refs_1_.refs_2_), custom_call_target="tpu_custom_call" | custom-call | flops 1073741824 | bytes 8388608 | tf_op jit(solution)/shard_map/pick/pallas_call | solution.py:141
  78.0 5.0 %all-to-all-start.2 = ((bf16[8,2,64,2048]{3,2,1,0:T(8,128)(2,1)}), bf16[8,2,64,2048]{3,2,1,0:T(8,128)(2,1)}, u32[]{:S(2)}, u32[]{:S(2)}) async-start(bf16[8,2,64,2048]{3,2,1,0:T(8,128)(2,1)} %pick.1), calls=%async_computation.2 | async-start | bytes 8388608 | tf_op jit(solution)/shard_map/all_to_all | solution.py:471
  83.0 42.7 %all-gather.5.cloned.1.call-done.refs_2_ = bf16[1024,2048]{1,0:T(8,128)(2,1)} async-done(((bf16[128,2048]{1,0:T(8,128)(2,1)}), bf16[1024,2048]{1,0:T(8,128)(2,1)}) %all-gather.5.cloned.1.call-update) | async-done | bytes 4194320 | tf_op jit(solution)/shard_map/all_gather | solution.py:448
  125.7 6.6 %pick_scaled.1 = bf16[8,2,64,2048]{3,2,1,0:T(8,128)(2,1)} custom-call(s32[2]{0:T(128)} %pad_add_fusion.refs_0_, bf16[1024,2176]{1,0:T(8,128)(2,1)} %all-gather.3.cloned.1.call-done.refs_1_.refs_2_, bf16[1024,2048]{1,0:T(8,128)(2,1)} %all-gather.5.cloned.1.call-done.refs_2_), custom_call_target="tpu_custom_call" | custom-call | flops 1073741824 | bytes 8388608 | tf_op jit(solution)/shard_map/pick_scaled/pallas_call | solution.py:141
  132.3 0.0 all-to-all-done.2.x
  132.3 5.0 %all-to-all-start.3 = ((bf16[8,2,64,2048]{3,2,1,0:T(8,128)(2,1)}), bf16[8,2,64,2048]{3,2,1,0:T(8,128)(2,1)}, u32[]{:S(2)}, u32[]{:S(2)}) async-start(bf16[8,2,64,2048]{3,2,1,0:T(8,128)(2,1)} %pick_scaled.1), calls=%async_computation.3 | async-start | bytes 8388608 | tf_op jit(solution)/shard_map/all_to_all | solution.py:471
  137.3 10.7 %forward.1 = (f32[2,512,384]{2,1,0:T(8,128)}, f32[2,512,384]{2,1,0:T(8,128)}, bf16[2,512,384]{2,1,0:T(8,128)(2,1)}, bf16[2,512,256]{2,1,0:T(8,128)(2,1)}) custom-call(bf16[8,2,64,2048]{3,2,1,0:T(8,128)(2,1)} %all-to-all-done.2.x, bf16[2,2048,384]{2,1,0:T(8,128)(2,1)} %gate_w.3, bf16[2,2048,384]{2,1,0:T(8,128)(2,1)} %up_w.3, bf16[2048,256]{1,0:T(8,128)(2,1)} %bitcast.40), custom_call_target="tpu_custom_call" | custom-call | flops 4294967296 | bytes 16000000 | tf_op jit(solution)/shard_map/forward/pallas_call | solution.py:222
  147.9 37.6 %all-to-all-done.3.dy = bf16[8,2,64,2048]{3,2,1,0:T(8,128)(2,1)} async-done(((bf16[8,2,64,2048]{3,2,1,0:T(8,128)(2,1)}), bf16[8,2,64,2048]{3,2,1,0:T(8,128)(2,1)}, u32[]{:S(2)}, u32[]{:S(2)}) %all-to-all-start.3) | async-done | bytes 4194336 | tf_op jit(solution)/shard_map/all_to_all | solution.py:471
  185.6 8.6 %backward.1 = (bf16[2,512,384]{2,1,0:T(8,128)(2,1)}, bf16[2,512,384]{2,1,0:T(8,128)(2,1)}, bf16[2,3,384,256]{3,2,1,0:T(8,128)(2,1)}) custom-call(bf16[8,2,64,2048]{3,2,1,0:T(8,128)(2,1)} %all-to-all-done.3.dy, bf16[2,384,2048]{2,1,0:T(8,128)(2,1)} %down_w.1, bf16[2048,256]{1,0:T(8,128)(2,1)} %bitcast.41, f32[2,512,384]{2,1,0:T(8,128)} %get-tuple-element.23.act, ...), custom_call_target="tpu_custom_call" | custom-call | flops 3288334336 | bytes 16000000 | tf_op jit(solution)/shard_map/backward/pallas_call | solution.py:255
  194.2 4.3 %all-to-all-start.4 = ((bf16[4,576,256]{2,1,0:T(8,128)(2,1)}), bf16[4,576,256]{2,1,0:T(8,128)(2,1)S(1)}, u32[]{:S(2)}, u32[]{:S(2)}) async-start(bf16[4,576,256]{2,1,0:T(8,128)(2,1)} %bitcast.44), calls=%async_computation.4 | async-start | bytes 2359296 | tf_op jit(solution)/shard_map/all_to_all | solution.py:67
  198.5 9.8 %row_grads.1 = bf16[8,2,64,2048]{3,2,1,0:T(8,128)(2,1)} custom-call(bf16[2,512,384]{2,1,0:T(8,128)(2,1)} %get-tuple-element.29.gate_grad, bf16[2,512,384]{2,1,0:T(8,128)(2,1)} %get-tuple-element.30.up_grad, bf16[2,2048,384]{2,1,0:T(8,128)(2,1)} %gate_w.3, bf16[2,2048,384]{2,1,0:T(8,128)(2,1)} %up_w.3), custom_call_target="tpu_custom_call" | custom-call | flops 3221225472 | bytes 12000000 | tf_op jit(solution)/shard_map/row_grads/pallas_call | solution.py:283
  208.3 4.2 %dynamic-slice_bitcast_fusion = (bf16[2,64,2048]{2,1,0:T(8,128)(2,1)}, bf16[2,64,2048]{2,1,0:T(8,128)(2,1)}, bf16[2,64,2048]{2,1,0:T(8,128)(2,1)}, bf16[2,64,204...) fusion(bf16[8,2,64,2048]{3,2,1,0:T(8,128)(2,1)} %row_grads.1, ...), kind=kLoop, calls=%fused_computation | loop fusion | bytes 8388640 | tf_op jit(solution)/shard_map/jit(dynamic_index_in_dim)/squeeze | solution.py:488
  212.5 0.0 copy-start.2
  212.5 0.0 collective-permute-start
  212.5 0.1 collective-permute-start.1
  212.6 2.1 all-to-all-done.4.arrived
  214.7 1.7 sum_and_spread.2
  216.4 3.5 all-to-all-start.5
  219.9 0.0 reduce-scatter.2.cloned.1.call-start
  219.9 2.3 collective-permute-start.2
  222.2 0.5 collective-permute-start.3
  222.7 2.9 collective-permute-start.4
  225.6 0.8 collective-permute-done.refs_3_
  226.4 2.7 collective-permute-start.5
  229.0 0.0 collective-permute-done.1.refs_4_
  229.0 11.6 %collective-permute-start.6 = (bf16[2,64,2048]{2,1,0:T(8,128)(2,1)}, bf16[2,64,2048]{2,1,0:T(8,128)(2,1)}, u32[]{:S(2)}, u32[]{:S(2)}) collective-permute-start(bf16[2,64,2048]{2,1,0:T(8,128)(2,1)} %get-tuple-element.33), channel_id=1, source_target_pairs={{0,28},{4,0},{8,4},{12,8},{16,12},{20,16},{24,20},{28,24},{1,29},{... | collective-permute-start | bytes 1572872 | tf_op jit(solution)/shard_map/ppermute | solution.py:490
  240.6 0.0 copy-done
  240.6 0.0 copy-done.1
  240.6 0.0 copy-done.2
  240.6 11.2 %weight_grads.1.weights = bf16[2048,2304]{1,0:T(8,128)(2,1)} custom-call(bf16[8,2,64,2048]{3,2,1,0:T(8,128)(2,1)} %all-to-all-done.2.x, bf16[8,2,64,2048]{3,2,1,0:T(8,128)(2,1)} %all-to-all-done.3.dy, bf16[2,512,384]{2,1,0:T(8,128)(2,1)S(1)} %copy-done.1, bf16[2,512,384]{2,1,0:T(8,128)(2,1)S(1)} %copy-done.2, bf16[2,512,384]{2,1,0:T(8,128)(2,1)S(1)} %copy-done), custom_call_target="tpu_custom_call" | custom-call | flops 4831838208 | bytes 24000000 | tf_op jit(solution)/shard_map/weight_grads/pallas_call | solution.py:308
  251.8 0.0 all-to-all-done.5
  251.8 1.0 copy-done.3
  252.8 9.0 %power.1 = bf16[2048,256]{1,0:T(8,128)(2,1)} custom-call(bf16[2048,2304]{1,0:T(8,128)(2,1)} %weight_grads.1.weights, bf16[2304,256]{1,0:T(8,128)(2,1)} %bitcast.38), custom_call_target="tpu_custom_call" | custom-call | flops 2415919104 | bytes 12000000 | tf_op jit(solution)/shard_map/power/pallas_call | solution.py:328
  261.8 0.0 collective-permute-done.2.refs_5_
  261.8 0.0 collective-permute-done.3.refs_6_
  261.8 0.0 collective-permute-done.4.refs_7_
  261.8 0.0 collective-permute-done.5.refs_8_
  261.8 6.5 %collective-permute-done.6.refs_9_ = bf16[2,64,2048]{2,1,0:T(8,128)(2,1)} collective-permute-done((bf16[2,64,2048]{2,1,0:T(8,128)(2,1)}, bf16[2,64,2048]{2,1,0:T(8,128)(2,1)}, u32[]{:S(2)}, u32[]{:S(2)}) %collective-permute-start.6) | collective-permute-done | bytes 524320 | tf_op jit(solution)/shard_map/ppermute | solution.py:490
  268.4 7.4 %give_back.1 = bf16[1024,2048]{1,0:T(8,128)(2,1)} custom-call(s32[2]{0:T(128)} %pad_add_fusion.refs_0_, bf16[1024,2176]{1,0:T(8,128)(2,1)} %all-gather.3.cloned.1.call-done.refs_1_.refs_2_, bf16[2,64,2048]{2,1,0:T(8,128)(2,1)} %get-tuple-element.40.refs_2_, bf16[2,64,2048]{2,1,0:T(8,128)(2,1)} %collective-permute-done.refs_3_, ...), custom_call_target="tpu_custom_call" | custom-call | flops 1073741824 | bytes 8388608 | tf_op jit(solution)/shard_map/give_back/pallas_call | solution.py:183
  275.8 0.0 reduce-scatter.2.cloned.1.call-update
  275.8 0.0 copy-start.4
  275.9 1.2 copy-done.5
  277.0 20.5 %all_to_all.52 = bf16[8,256,256]{2,1,0:T(8,128)(2,1)S(1)} all-to-all(bf16[8,256,256]{2,1,0:T(8,128)(2,1)S(1)} %bitcast.42), channel_id=1, replica_groups=mesh['expert_0'=8,'expert_1'=4,'expert_2'=2,'replica'=4] {'expert_2','re..., dimensions={0} | all-to-all | bytes 2097152 | tf_op jit(solution)/shard_map/all_to_all | solution.py:42
  297.6 0.1 reduce_sum.12
  297.7 18.5 %all_to_all.53.arrived = bf16[32,8,256]{2,1,0:T(8,128)(2,1)S(1)} all-to-all(bf16[32,8,256]{2,1,0:T(8,128)(2,1)S(1)} %bitcast.45), channel_id=1, replica_groups=mesh['expert_0'=8,'expert_1'=4,'expert_2'=2,'replica'=4] {'expert_0','ex..., dimensions={0} | all-to-all | bytes 262144 | tf_op jit(solution)/shard_map/all_to_all | solution.py:67
  316.3 15.6 %all_to_all.54 = bf16[32,8,256]{2,1,0:T(8,128)(2,1)S(1)} all-to-all(bf16[32,8,256]{2,1,0:T(8,128)(2,1)S(1)} %sum_and_spread.3), channel_id=1, replica_groups=mesh['expert_0'=8,'expert_1'=4,'expert_2'=2,'replica'=4] {'expert_0','ex..., dimensions={0} | all-to-all | bytes 262144 | tf_op jit(solution)/shard_map/all_to_all | solution.py:67
  331.9 1.1 broadcast_in_dim.11
  333.0 3.6 all-to-all-start.9
  336.6 0.0 copy-done.4
  336.6 1.6 convert.2
  338.2 13.6 %all-to-all-done.9 = bf16[8,256,256]{2,1,0:T(8,128)(2,1)S(1)} async-done(((bf16[8,256,256]{2,1,0:T(8,128)(2,1)}), bf16[8,256,256]{2,1,0:T(8,128)(2,1)S(1)}, u32[]{:S(2)}, u32[]{:S(2)}) %all-to-all-start.9) | async-done | bytes 1048608 | tf_op jit(solution)/shard_map/all_to_all | solution.py:36
  351.8 16.9 %new_basis.1 = f32[32,256]{1,0:T(8,128)} custom-call(s32[1]{0:T(128)} %bitcast.21.refs_0_, bf16[2048,256]{1,0:T(8,128)(2,1)S(1)} %bitcast.36, bf16[2048,256]{1,0:T(8,128)(2,1)S(1)} %bitcast.37), custom_call_target="tpu_custom_call" | custom-call | flops 30000001024 | bytes 2000000 | tf_op jit(solution)/shard_map/new_basis/pallas_call | solution.py:403
  (7 shorter events, 0.1 us)
Async XLA Ops:
  7.2 63.7 %all-gather.3.cloned.1.call-start = ((), (), s32[]{:S(2)}) async-start(), calls=%async_computation.11 | async-start | bytes 5013504 | tf_op jit(solution)/shard_map/all_gather | solution.py:448
  9.9 115.8 %all-gather.5.cloned.1.call-start = ((), (), s32[]{:S(2)}) async-start(), calls=%async_computation.12 | async-start | bytes 4718592 | tf_op jit(solution)/shard_map/all_gather | solution.py:448
  78.0 54.3 %all-to-all-start.2 = ((bf16[8,2,64,2048]{3,2,1,0:T(8,128)(2,1)}), bf16[8,2,64,2048]{3,2,1,0:T(8,128)(2,1)}, u32[]{:S(2)}, u32[]{:S(2)}) async-start(bf16[8,2,64,2048]{3,2,1,0:T(8,128)(2,1)} %pick.1), calls=%async_computation.2 | async-start | bytes 8388608 | tf_op jit(solution)/shard_map/all_to_all | solution.py:471
  132.3 53.3 %all-to-all-start.3 = ((bf16[8,2,64,2048]{3,2,1,0:T(8,128)(2,1)}), bf16[8,2,64,2048]{3,2,1,0:T(8,128)(2,1)}, u32[]{:S(2)}, u32[]{:S(2)}) async-start(bf16[8,2,64,2048]{3,2,1,0:T(8,128)(2,1)} %pick_scaled.1), calls=%async_computation.3 | async-start | bytes 8388608 | tf_op jit(solution)/shard_map/all_to_all | solution.py:471
  194.2 20.5 %all-to-all-start.4 = ((bf16[4,576,256]{2,1,0:T(8,128)(2,1)}), bf16[4,576,256]{2,1,0:T(8,128)(2,1)S(1)}, u32[]{:S(2)}, u32[]{:S(2)}) async-start(bf16[4,576,256]{2,1,0:T(8,128)(2,1)} %bitcast.44), calls=%async_computation.4 | async-start | bytes 2359296 | tf_op jit(solution)/shard_map/all_to_all | solution.py:67
  212.5 28.1 %copy-start = (bf16[2,512,384]{2,1,0:T(8,128)(2,1)S(1)}, bf16[2,512,384]{2,1,0:T(8,128)(2,1)}, u32[]{:S(2)}) copy-start(bf16[2,512,384]{2,1,0:T(8,128)(2,1)} %get-tuple-element.25.hidden) | copy-start | bytes 2359300
  212.5 28.1 %copy-start.1 = (bf16[2,512,384]{2,1,0:T(8,128)(2,1)S(1)}, bf16[2,512,384]{2,1,0:T(8,128)(2,1)}, u32[]{:S(2)}) copy-start(bf16[2,512,384]{2,1,0:T(8,128)(2,1)} %get-tuple-element.29.gate_grad) | copy-start | bytes 2359300
  212.5 28.1 %copy-start.2 = (bf16[2,512,384]{2,1,0:T(8,128)(2,1)S(1)}, bf16[2,512,384]{2,1,0:T(8,128)(2,1)}, u32[]{:S(2)}) copy-start(bf16[2,512,384]{2,1,0:T(8,128)(2,1)} %get-tuple-element.30.up_grad) | copy-start | bytes 2359300
  212.5 13.9 %collective-permute-start = (bf16[2,64,2048]{2,1,0:T(8,128)(2,1)}, bf16[2,64,2048]{2,1,0:T(8,128)(2,1)}, u32[]{:S(2)}, u32[]{:S(2)}) collective-permute-start(bf16[2,64,2048]{2,1,0:T(8,128)(2,1)} %get-tuple-element.39), channel_id=1, source_target_pairs={{0,4},{4,8},{8,12},{12,16},{16,20},{20,24},{24,28},{28,0},{1,5},{5... | collective-permute-start | bytes 1572872 | tf_op jit(solution)/shard_map/ppermute | solution.py:490
  212.5 16.5 %collective-permute-start.1 = (bf16[2,64,2048]{2,1,0:T(8,128)(2,1)}, bf16[2,64,2048]{2,1,0:T(8,128)(2,1)}, u32[]{:S(2)}, u32[]{:S(2)}) collective-permute-start(bf16[2,64,2048]{2,1,0:T(8,128)(2,1)} %get-tuple-element.38), channel_id=1, source_target_pairs={{0,8},{4,12},{8,16},{12,20},{16,24},{20,28},{24,0},{28,4},{1,9},{5... | collective-permute-start | bytes 1572872 | tf_op jit(solution)/shard_map/ppermute | solution.py:490
  216.4 35.4 %all-to-all-start.5 = ((bf16[4,576,256]{2,1,0:T(8,128)(2,1)}), bf16[4,576,256]{2,1,0:T(8,128)(2,1)S(1)}, u32[]{:S(2)}, u32[]{:S(2)}) async-start(bf16[4,576,256]{2,1,0:T(8,128)(2,1)} %sum_and_spread.2), calls=%async_computation.5 | async-start | bytes 2359296 | tf_op jit(solution)/shard_map/all_to_all | solution.py:67
  219.9 148.7 %reduce-scatter.2.cloned.1.call-start = ((), (), s32[]{:S(2)}) async-start(), calls=%async_computation.13 | async-start | bytes 4718592 | tf_op jit(solution)/shard_map/reduce_scatter | solution.py:504
  219.9 41.9 %collective-permute-start.2 = (bf16[2,64,2048]{2,1,0:T(8,128)(2,1)}, bf16[2,64,2048]{2,1,0:T(8,128)(2,1)}, u32[]{:S(2)}, u32[]{:S(2)}) collective-permute-start(bf16[2,64,2048]{2,1,0:T(8,128)(2,1)} %get-tuple-element.37), channel_id=1, source_target_pairs={{0,12},{4,16},{8,20},{12,24},{16,28},{20,0},{24,4},{28,8},{1,13},{... | collective-permute-start | bytes 1572872 | tf_op jit(solution)/shard_map/ppermute | solution.py:490
  222.2 39.6 %collective-permute-start.3 = (bf16[2,64,2048]{2,1,0:T(8,128)(2,1)}, bf16[2,64,2048]{2,1,0:T(8,128)(2,1)}, u32[]{:S(2)}, u32[]{:S(2)}) collective-permute-start(bf16[2,64,2048]{2,1,0:T(8,128)(2,1)} %get-tuple-element.36), channel_id=1, source_target_pairs={{0,16},{4,20},{8,24},{12,28},{16,0},{20,4},{24,8},{28,12},{1,17},{... | collective-permute-start | bytes 1572872 | tf_op jit(solution)/shard_map/ppermute | solution.py:490
  222.7 39.2 %collective-permute-start.4 = (bf16[2,64,2048]{2,1,0:T(8,128)(2,1)}, bf16[2,64,2048]{2,1,0:T(8,128)(2,1)}, u32[]{:S(2)}, u32[]{:S(2)}) collective-permute-start(bf16[2,64,2048]{2,1,0:T(8,128)(2,1)} %get-tuple-element.35), channel_id=1, source_target_pairs={{0,20},{4,24},{8,28},{12,0},{16,4},{20,8},{24,12},{28,16},{1,21},{... | collective-permute-start | bytes 1572872 | tf_op jit(solution)/shard_map/ppermute | solution.py:490
  226.4 35.5 %collective-permute-start.5 = (bf16[2,64,2048]{2,1,0:T(8,128)(2,1)}, bf16[2,64,2048]{2,1,0:T(8,128)(2,1)}, u32[]{:S(2)}, u32[]{:S(2)}) collective-permute-start(bf16[2,64,2048]{2,1,0:T(8,128)(2,1)} %get-tuple-element.34), channel_id=1, source_target_pairs={{0,24},{4,28},{8,0},{12,4},{16,8},{20,12},{24,16},{28,20},{1,25},{... | collective-permute-start | bytes 1572872 | tf_op jit(solution)/shard_map/ppermute | solution.py:490
  229.0 39.4 %collective-permute-start.6 = (bf16[2,64,2048]{2,1,0:T(8,128)(2,1)}, bf16[2,64,2048]{2,1,0:T(8,128)(2,1)}, u32[]{:S(2)}, u32[]{:S(2)}) collective-permute-start(bf16[2,64,2048]{2,1,0:T(8,128)(2,1)} %get-tuple-element.33), channel_id=1, source_target_pairs={{0,28},{4,0},{8,4},{12,8},{16,12},{20,16},{24,20},{28,24},{1,29},{... | collective-permute-start | bytes 1572872 | tf_op jit(solution)/shard_map/ppermute | solution.py:490
  251.8 1.0 copy-start.3
  275.8 1.2 copy-start.5
  275.8 60.7 %copy-start.4 = (bf16[4,576,256]{2,1,0:T(8,128)(2,1)S(1)}, bf16[4,576,256]{2,1,0:T(8,128)(2,1)}, u32[]{:S(2)}) copy-start(bf16[4,576,256]{2,1,0:T(8,128)(2,1)} %copy-done.3) | copy-start | bytes 3538948
  333.0 18.8 %all-to-all-start.9 = ((bf16[8,256,256]{2,1,0:T(8,128)(2,1)}), bf16[8,256,256]{2,1,0:T(8,128)(2,1)S(1)}, u32[]{:S(2)}, u32[]{:S(2)}) async-start(bf16[8,256,256]{2,1,0:T(8,128)(2,1)} %broadcast_in_dim.11), calls=%async_computation.10 | async-start | bytes 2097152 | tf_op jit(solution)/shard_map/all_to_all | solution.py:36
Sparse Core Ops, SparseCore 0:
  10.3 60.4 all-gather.2
  72.6 53.0 all-gather.4
  276.0 61.0 reduce-scatter.1

commit v4 on v3

--- a/solution.py
+++ b/solution.py
@@ -315,29 +315,6 @@
         compiler_params=pltpu.CompilerParams(vmem_limit_bytes=36 * 2**20),
         name="weight_grads",
     )(x, dy, gate_grad, up_grad, hidden)
-
-
-def power_body(weights, grads, out):
-    out[...] = dot(weights[...], grads[...]).astype(bf16)
-
-
-def power_of(weights, grads):
-    width, depth = weights.shape
-    rank = grads.shape[1]
-    part = width // 8
-    return pl.pallas_call(
-        power_body,
-        out_shape=jax.ShapeDtypeStruct((width, rank), bf16),
-        grid=(8,),
-        in_specs=[
-            pl.BlockSpec((part, depth), lambda i: (i, 0)),
-            pl.BlockSpec((depth, rank), lambda i: (0, 0)),
-        ],
-        out_specs=pl.BlockSpec((part, rank), lambda i: (i, 0)),
-        cost_estimate=cost(2 * width * depth * rank, 12e6),
-        compiler_params=pltpu.CompilerParams(vmem_limit_bytes=58 * 2**20),
-        name="power",
-    )(weights, grads)
 
 
 def inverse_factor(square):
@@ -477,25 +454,27 @@
     )
 
     arrived = exchanged(partial.reshape(replicas, -1, partial.shape[-1]), Y)
+    rows = row_grads_of(gate_grad, up_grad, gate_weight, up_weight, plane)
+    pieces = [
+        lax.dynamic_index_in_dim(rows, (here + d) % plane, 0, keepdims=False) for d in range(plane)
+    ]
+    arrived, *pieces = after(arrived, *pieces)
     spread = sum_and_spread(arrived, 3)
     grads_low = exchanged(spread, Y)
     projected_grads = grads_low.astype(f32).reshape(partial.shape)
     grads_low = grads_low.reshape(-1, partial.shape[-1])
 
-    rows = row_grads_of(gate_grad, up_grad, gate_weight, up_weight, plane)
-    returned = []
-    for d in range(plane):
-        piece = lax.dynamic_index_in_dim(rows, (here + d) % plane, 0, keepdims=False)
-        if d:
-            piece = lax.ppermute(piece, PLANE, [(i, (i + d) % plane) for i in range(plane)])
-        returned.append(piece)
+    returned = [pieces[0]]
+    for d in range(1, plane):
+        places = [(i, (i + d) % plane) for i in range(plane)]
+        returned.append(lax.ppermute(pieces[d], PLANE, places))
 
     late_gate_grad, _ = after(gate_grad, spread)
     own_weight_grads = weight_grads(x, dy, late_gate_grad, up_grad, hidden)
     near, far = (C, Y), (Z, X)
-    power = power_of(own_weight_grads, grads_low)
+    power = dot(own_weight_grads, grads_low).astype(bf16)
+    power = sent_and_summed(power, near)
     late_base, power = after(base, power)
-    power = sent_and_summed(power, near)
     power = exchanged(power.reshape(lax.axis_size(far), -1, power.shape[-1]), far)
     power = exchanged(sum_and_spread(power, 1), far).reshape(-1, power.shape[-1])
     power = gathered(power, near)

time: 379 us -> 384 us (1.013)
  waiting for transfers between devices: 123 us -> 161 us
  blocking collectives: 94.5 us -> 73.4 us
  starting transfers between devices: 41.4 us -> 32.1 us
  Pallas kernels: 90.3 us -> 81.3 us
  matrix products: 0 us -> 7.73 us
    ppermute x7, waiting for transfers between devices: 7.38 us -> 32 us  [layer(): returned.append(lax.ppermute(pieces[d], PLANE, places))]
    all_to_all x1 -> x0, blocking collectives: 20.5 us -> none  [sent_and_summed(): lax.all_to_all(pieces, axis, split_axis=0, concat_axis=0, tiled=True)]
    ppermute x7, starting transfers between devices: 19.9 us -> 5.96 us  [layer(): returned.append(lax.ppermute(pieces[d], PLANE, places))]
    all_to_all x0 -> x1, waiting for transfers between devices: none -> 9.52 us  [sent_and_summed(): lax.all_to_all(pieces, axis, split_axis=0, concat_axis=0, tiled=True)]
    pallas_call x1 -> x0, Pallas kernels: 9.02 us -> none  [power_of(): pl.pallas_call(power_body, out_shape=jax.ShapeDtypeStruct((width, rank),...]
    dot_general x0 -> x1, matrix products: none -> 7.73 us  [dot(): lax.dot_general(a, b, (over, ((), ())), precision=precision, preferred_el...]
    all_to_all x2, waiting for transfers between devices: 2.08 us -> 6.01 us  [exchanged(): return lax.all_to_all(pieces, axis, split_axis=0, concat_axis=0, tiled=True)]
  transfers between devices with their start and end apart: 15 -> 16, of which waited for: 7 -> 11; matrix products, arithmetic and copies ran while one was open for 2% -> 4% of each run, Pallas kernels for 19% -> 16%
where the time goes in v4:
time: 384 us; the launch traced here: 379 us
  waiting for transfers between devices  161 us (42%)
  Pallas kernels  81.3 us (21%)
  blocking collectives  73.4 us (19%)
  starting transfers between devices  32.1 us (8%)
  between operations  13.9 us (4%)
  matrix products  7.73 us (2%)
  local copies, waits for them, and re-layouts  6.54 us (2%)
    all_gather x2, waiting for transfers between devices, along_z(): return lax.all_gather(value, Z, axis=0, tiled=True)  62.5 us
    all_to_all x2, blocking collectives, from_everyone(): return lax.all_to_all(copies, axis, split_axis=0, concat_axis=0, tiled=True)  39.8 us
    all_to_all x2, waiting for transfers between devices, sent(): lax.all_to_all(picked, PLANE, split_axis=0, concat_axis=0, tiled=True)  37.6 us
    all_to_all x2, blocking collectives, exchanged(): return lax.all_to_all(pieces, axis, split_axis=0, concat_axis=0, tiled=True)  33.5 us
    ppermute x7, waiting for transfers between devices, layer(): returned.append(lax.ppermute(pieces[d], PLANE, places))  32 us
    pallas_call x1, Pallas kernels, new_basis_of(): pl.pallas_call(lambda *refs: new_basis_body(math.sqrt(width), *refs), out...  16.9 us
    all_to_all x1, waiting for transfers between devices, from_everyone(): return lax.all_to_all(copies, axis, split_axis=0, concat_axis=0, tiled=True)  13.6 us
    pallas_call x2, Pallas kernels, pick(): pl.pallas_call(lambda *refs: pick_body(top, scaled, *refs), out_shape=jax...  13 us
  transfers between devices with their start and end apart: 16, of which 11 were waited for; matrix products, arithmetic and copies ran while one was open for 4% of the time, Pallas kernels for 16%

profile of v4, /device:TPU:2, one launch (start us, length us, event | category | flops | bytes accessed | tf_op | source)
XLA Modules:
  0.0 379.3 jit_solution(238454056851816694)
XLA Ops:
  7.2 0.0 all-gather.3.cloned.1.call-start
  7.2 0.7 fusion
  7.9 2.0 packed.1
  9.9 0.0 all-gather.3.cloned.1.call-update
  9.9 0.0 all-gather.5.cloned.1.call-start
  10.0 20.3 %all_to_all.50 = bf16[32,8,256]{2,1,0:T(8,128)(2,1)S(1)} all-to-all(bf16[32,8,256]{2,1,0:T(8,128)(2,1)S(1)} %broadcast_in_dim.9), channel_id=1, replica_groups=mesh['expert_0'=8,'expert_1'=4,'expert_2'=2,'replica'=4] {'expert_0','ex..., dimensions={0} | all-to-all | bytes 262144 | tf_op jit(solution)/shard_map/all_to_all | solution.py:36
  30.3 0.1 broadcast_in_dim.10
  30.4 19.6 %all_to_all.51 = bf16[8,256,256]{2,1,0:T(8,128)(2,1)S(1)} all-to-all(bf16[8,256,256]{2,1,0:T(8,128)(2,1)S(1)} %broadcast_in_dim.10), channel_id=1, replica_groups=mesh['expert_0'=8,'expert_1'=4,'expert_2'=2,'replica'=4] {'expert_2','re..., dimensions={0} | all-to-all | bytes 2097152 | tf_op jit(solution)/shard_map/all_to_all | solution.py:36
  49.9 1.2 copy.13
  51.1 19.8 %all-gather.3.cloned.1.call-done.refs_1_.refs_2_ = bf16[1024,2176]{1,0:T(8,128)(2,1)} async-done(((bf16[128,2176]{1,0:T(8,128)(2,1)}), bf16[1024,2176]{1,0:T(8,128)(2,1)}) %all-gather.3.cloned.1.call-update) | async-done | bytes 4456464 | tf_op jit(solution)/shard_map/all_gather | solution.py:425
  70.8 0.0 all-gather.5.cloned.1.call-update
  70.9 0.6 pad_add_fusion.refs_0_
  71.4 6.5 %pick.1 = bf16[8,2,64,2048]{3,2,1,0:T(8,128)(2,1)} custom-call(s32[2]{0:T(128)} %pad_add_fusion.refs_0_, bf16[1024,2176]{1,0:T(8,128)(2,1)} %all-gather.3.cloned.1.call-done.refs_1_.refs_2_, bf16[1024,2176]{1,0:T(8,128)(2,1)} %all-gather.3.cloned.1.call-done.refs_1_.refs_2_), custom_call_target="tpu_custom_call" | custom-call | flops 1073741824 | bytes 8388608 | tf_op jit(solution)/shard_map/pick/pallas_call | solution.py:141
  77.9 5.1 %all-to-all-start.2 = ((bf16[8,2,64,2048]{3,2,1,0:T(8,128)(2,1)}), bf16[8,2,64,2048]{3,2,1,0:T(8,128)(2,1)}, u32[]{:S(2)}, u32[]{:S(2)}) async-start(bf16[8,2,64,2048]{3,2,1,0:T(8,128)(2,1)} %pick.1), calls=%async_computation.2 | async-start | bytes 8388608 | tf_op jit(solution)/shard_map/all_to_all | solution.py:448
  82.9 42.7 %all-gather.5.cloned.1.call-done.refs_2_ = bf16[1024,2048]{1,0:T(8,128)(2,1)} async-done(((bf16[128,2048]{1,0:T(8,128)(2,1)}), bf16[1024,2048]{1,0:T(8,128)(2,1)}) %all-gather.5.cloned.1.call-update) | async-done | bytes 4194320 | tf_op jit(solution)/shard_map/all_gather | solution.py:425
  125.7 6.6 %pick_scaled.1 = bf16[8,2,64,2048]{3,2,1,0:T(8,128)(2,1)} custom-call(s32[2]{0:T(128)} %pad_add_fusion.refs_0_, bf16[1024,2176]{1,0:T(8,128)(2,1)} %all-gather.3.cloned.1.call-done.refs_1_.refs_2_, bf16[1024,2048]{1,0:T(8,128)(2,1)} %all-gather.5.cloned.1.call-done.refs_2_), custom_call_target="tpu_custom_call" | custom-call | flops 1073741824 | bytes 8388608 | tf_op jit(solution)/shard_map/pick_scaled/pallas_call | solution.py:141
  132.3 0.0 all-to-all-done.2.x
  132.3 5.0 %all-to-all-start.3 = ((bf16[8,2,64,2048]{3,2,1,0:T(8,128)(2,1)}), bf16[8,2,64,2048]{3,2,1,0:T(8,128)(2,1)}, u32[]{:S(2)}, u32[]{:S(2)}) async-start(bf16[8,2,64,2048]{3,2,1,0:T(8,128)(2,1)} %pick_scaled.1), calls=%async_computation.3 | async-start | bytes 8388608 | tf_op jit(solution)/shard_map/all_to_all | solution.py:448
  137.3 10.7 %forward.1 = (f32[2,512,384]{2,1,0:T(8,128)}, f32[2,512,384]{2,1,0:T(8,128)}, bf16[2,512,384]{2,1,0:T(8,128)(2,1)}, bf16[2,512,256]{2,1,0:T(8,128)(2,1)}) custom-call(bf16[8,2,64,2048]{3,2,1,0:T(8,128)(2,1)} %all-to-all-done.2.x, bf16[2,2048,384]{2,1,0:T(8,128)(2,1)} %gate_w.3, bf16[2,2048,384]{2,1,0:T(8,128)(2,1)} %up_w.3, bf16[2048,256]{1,0:T(8,128)(2,1)} %bitcast.42), custom_call_target="tpu_custom_call" | custom-call | flops 4294967296 | bytes 16000000 | tf_op jit(solution)/shard_map/forward/pallas_call | solution.py:222
  148.0 37.6 %all-to-all-done.3.dy = bf16[8,2,64,2048]{3,2,1,0:T(8,128)(2,1)} async-done(((bf16[8,2,64,2048]{3,2,1,0:T(8,128)(2,1)}), bf16[8,2,64,2048]{3,2,1,0:T(8,128)(2,1)}, u32[]{:S(2)}, u32[]{:S(2)}) %all-to-all-start.3) | async-done | bytes 4194336 | tf_op jit(solution)/shard_map/all_to_all | solution.py:448
  185.6 8.6 %backward.1 = (bf16[2,512,384]{2,1,0:T(8,128)(2,1)}, bf16[2,512,384]{2,1,0:T(8,128)(2,1)}, bf16[2,3,384,256]{3,2,1,0:T(8,128)(2,1)}) custom-call(bf16[8,2,64,2048]{3,2,1,0:T(8,128)(2,1)} %all-to-all-done.3.dy, bf16[2,384,2048]{2,1,0:T(8,128)(2,1)} %down_w.1, bf16[2048,256]{1,0:T(8,128)(2,1)} %bitcast.43, f32[2,512,384]{2,1,0:T(8,128)} %get-tuple-element.32.act, ...), custom_call_target="tpu_custom_call" | custom-call | flops 3288334336 | bytes 16000000 | tf_op jit(solution)/shard_map/backward/pallas_call | solution.py:255
  194.2 4.3 %all-to-all-start.4 = ((bf16[4,576,256]{2,1,0:T(8,128)(2,1)}), bf16[4,576,256]{2,1,0:T(8,128)(2,1)S(1)}, u32[]{:S(2)}, u32[]{:S(2)}) async-start(bf16[4,576,256]{2,1,0:T(8,128)(2,1)} %bitcast.45), calls=%async_computation.4 | async-start | bytes 2359296 | tf_op jit(solution)/shard_map/all_to_all | solution.py:67
  198.5 9.8 %row_grads.1 = bf16[8,2,64,2048]{3,2,1,0:T(8,128)(2,1)} custom-call(bf16[2,512,384]{2,1,0:T(8,128)(2,1)} %get-tuple-element.40.gate_grad, bf16[2,512,384]{2,1,0:T(8,128)(2,1)} %get-tuple-element.38.up_grad, bf16[2,2048,384]{2,1,0:T(8,128)(2,1)} %gate_w.3, bf16[2,2048,384]{2,1,0:T(8,128)(2,1)} %up_w.3), custom_call_target="tpu_custom_call" | custom-call | flops 3221225472 | bytes 12000000 | tf_op jit(solution)/shard_map/row_grads/pallas_call | solution.py:283
  208.3 4.2 %dynamic-slice_bitcast_fusion = (bf16[2,64,2048]{2,1,0:T(8,128)(2,1)}, bf16[2,64,2048]{2,1,0:T(8,128)(2,1)}, bf16[2,64,2048]{2,1,0:T(8,128)(2,1)}, bf16[2,64,204...) fusion(bf16[8,2,64,2048]{3,2,1,0:T(8,128)(2,1)} %row_grads.1, ...), kind=kLoop, calls=%fused_computation.1 | loop fusion | bytes 8388640 | tf_op jit(solution)/shard_map/jit(dynamic_index_in_dim)/squeeze | solution.py:459
  212.5 0.0 copy-start.2
  212.6 2.1 all-to-all-done.4.arrived
  214.7 1.7 sum_and_spread.2
  216.3 3.5 all-to-all-start.5
  219.9 0.0 collective-permute-start
  219.9 0.3 collective-permute-start.1
  220.2 0.0 copy-done
  220.2 0.0 copy-done.1
  220.2 0.0 copy-done.2
  220.2 11.1 %weight_grads.1 = bf16[2048,2304]{1,0:T(8,128)(2,1)} custom-call(bf16[8,2,64,2048]{3,2,1,0:T(8,128)(2,1)} %all-to-all-done.2.x, bf16[8,2,64,2048]{3,2,1,0:T(8,128)(2,1)} %all-to-all-done.3.dy, bf16[2,512,384]{2,1,0:T(8,128)(2,1)S(1)} %copy-done.1, bf16[2,512,384]{2,1,0:T(8,128)(2,1)S(1)} %copy-done.2, bf16[2,512,384]{2,1,0:T(8,128)(2,1)S(1)} %copy-done), custom_call_target="tpu_custom_call" | custom-call | flops 4831838208 | bytes 24000000 | tf_op jit(solution)/shard_map/weight_grads/pallas_call | solution.py:308
  231.3 3.9 %all-to-all-done.5 = bf16[4,576,256]{2,1,0:T(8,128)(2,1)S(1)} async-done(((bf16[4,576,256]{2,1,0:T(8,128)(2,1)}), bf16[4,576,256]{2,1,0:T(8,128)(2,1)S(1)}, u32[]{:S(2)}, u32[]{:S(2)}) %all-to-all-start.5) | async-done | bytes 1179680 | tf_op jit(solution)/shard_map/all_to_all | solution.py:67
  235.2 7.7 %convolution_convert_fusion = bf16[2048,256]{1,0:T(8,128)(2,1)} fusion(bf16[2048,2304]{1,0:T(8,128)(2,1)} %weight_grads.1, bf16[2304,256]{1,0:T(8,128)(2,1)S(1)} %bitcast.40), kind=kOutput, calls=%fused_computation | convolution fusion | flops 2416443392 | bytes 11665408 | tf_op jit(solution)/shard_map/dot_general | solution.py:27
  242.9 0.0 copy-done.3
  242.9 3.6 all-to-all-start.6
  246.5 0.0 reduce-scatter.2.cloned.1.call-start
  246.6 0.6 collective-permute-start.2
  247.1 2.9 collective-permute-start.3
  250.0 1.0 collective-permute-start.4
  251.0 0.0 collective-permute-done.refs_3_
  251.0 1.1 collective-permute-start.5
  252.2 0.0 collective-permute-done.1.refs_4_
  252.2 0.0 collective-permute-start.6
  252.2 9.5 %all-to-all-done.6 = bf16[8,256,256]{2,1,0:T(8,128)(2,1)S(1)} async-done(((bf16[8,256,256]{2,1,0:T(8,128)(2,1)}), bf16[8,256,256]{2,1,0:T(8,128)(2,1)S(1)}, u32[]{:S(2)}, u32[]{:S(2)}) %all-to-all-start.6) | async-done | bytes 1048608 | tf_op jit(solution)/shard_map/all_to_all | solution.py:42
  261.7 0.1 reduce_sum.12
  261.8 0.0 collective-permute-done.2.refs_5_
  261.9 0.0 copy-start.5
  261.9 1.9 collective-permute-done.3.refs_6_
  263.7 21.2 %collective-permute-done.4.refs_7_ = bf16[2,64,2048]{2,1,0:T(8,128)(2,1)S(1)} collective-permute-done((bf16[2,64,2048]{2,1,0:T(8,128)(2,1)}, bf16[2,64,2048]{2,1,0:T(8,128)(2,1)S(1)}, u32[]{:S(2)}, u32[]{:S(2)}) %collective-permute-start.4) | collective-permute-done | bytes 524320 | tf_op jit(solution)/shard_map/ppermute | solution.py:470
  284.9 0.2 collective-permute-done.5.refs_8_
  285.2 8.7 %collective-permute-done.6.refs_9_ = bf16[2,64,2048]{2,1,0:T(8,128)(2,1)} collective-permute-done((bf16[2,64,2048]{2,1,0:T(8,128)(2,1)}, bf16[2,64,2048]{2,1,0:T(8,128)(2,1)}, u32[]{:S(2)}, u32[]{:S(2)}) %collective-permute-start.6) | collective-permute-done | bytes 524320 | tf_op jit(solution)/shard_map/ppermute | solution.py:470
  293.9 0.0 copy-done.6
  293.9 7.5 %give_back.1 = bf16[1024,2048]{1,0:T(8,128)(2,1)} custom-call(s32[2]{0:T(128)} %pad_add_fusion.refs_0_, bf16[1024,2176]{1,0:T(8,128)(2,1)} %all-gather.3.cloned.1.call-done.refs_1_.refs_2_, bf16[2,64,2048]{2,1,0:T(8,128)(2,1)} %get-tuple-element.42.refs_2_, bf16[2,64,2048]{2,1,0:T(8,128)(2,1)} %collective-permute-done.refs_3_, ...), custom_call_target="tpu_custom_call" | custom-call | flops 1073741824 | bytes 8388608 | tf_op jit(solution)/shard_map/give_back/pallas_call | solution.py:183
  301.4 0.0 reduce-scatter.2.cloned.1.call-update
  301.4 17.6 %all_to_all.52.arrived = bf16[32,8,256]{2,1,0:T(8,128)(2,1)S(1)} all-to-all(bf16[32,8,256]{2,1,0:T(8,128)(2,1)S(1)} %bitcast.46), channel_id=1, replica_groups=mesh['expert_0'=8,'expert_1'=4,'expert_2'=2,'replica'=4] {'expert_0','ex..., dimensions={0} | all-to-all | bytes 262144 | tf_op jit(solution)/shard_map/all_to_all | solution.py:67
  319.1 15.9 %all_to_all.53 = bf16[32,8,256]{2,1,0:T(8,128)(2,1)S(1)} all-to-all(bf16[32,8,256]{2,1,0:T(8,128)(2,1)S(1)} %sum_and_spread.3), channel_id=1, replica_groups=mesh['expert_0'=8,'expert_1'=4,'expert_2'=2,'replica'=4] {'expert_0','ex..., dimensions={0} | all-to-all | bytes 262144 | tf_op jit(solution)/shard_map/all_to_all | solution.py:67
  335.0 1.1 broadcast_in_dim.11
  336.0 4.6 %all-to-all-start.9 = ((bf16[8,256,256]{2,1,0:T(8,128)(2,1)}), bf16[8,256,256]{2,1,0:T(8,128)(2,1)S(1)}, u32[]{:S(2)}, u32[]{:S(2)}) async-start(bf16[8,256,256]{2,1,0:T(8,128)(2,1)} %broadcast_in_dim.11), calls=%async_computation.10 | async-start | bytes 2097152 | tf_op jit(solution)/shard_map/all_to_all | solution.py:36
  340.6 1.6 convert.2
  342.3 13.6 %all-to-all-done.9 = bf16[8,256,256]{2,1,0:T(8,128)(2,1)S(1)} async-done(((bf16[8,256,256]{2,1,0:T(8,128)(2,1)}), bf16[8,256,256]{2,1,0:T(8,128)(2,1)S(1)}, u32[]{:S(2)}, u32[]{:S(2)}) %all-to-all-start.9) | async-done | bytes 1048608 | tf_op jit(solution)/shard_map/all_to_all | solution.py:36
  355.9 16.9 %new_basis.1 = f32[32,256]{1,0:T(8,128)} custom-call(s32[1]{0:T(128)} %bitcast.22.refs_0_, bf16[2048,256]{1,0:T(8,128)(2,1)S(1)} %bitcast.38, bf16[2048,256]{1,0:T(8,128)(2,1)S(1)} %bitcast.39), custom_call_target="tpu_custom_call" | custom-call | flops 30000001024 | bytes 2000000 | tf_op jit(solution)/shard_map/new_basis/pallas_call | solution.py:380
  (14 shorter events, 0.1 us)
Async XLA Ops:
  7.2 63.7 %all-gather.3.cloned.1.call-start = ((), (), s32[]{:S(2)}) async-start(), calls=%async_computation.11 | async-start | bytes 5013504 | tf_op jit(solution)/shard_map/all_gather | solution.py:425
  9.9 115.8 %all-gather.5.cloned.1.call-start = ((), (), s32[]{:S(2)}) async-start(), calls=%async_computation.12 | async-start | bytes 4718592 | tf_op jit(solution)/shard_map/all_gather | solution.py:425
  77.9 54.4 %all-to-all-start.2 = ((bf16[8,2,64,2048]{3,2,1,0:T(8,128)(2,1)}), bf16[8,2,64,2048]{3,2,1,0:T(8,128)(2,1)}, u32[]{:S(2)}, u32[]{:S(2)}) async-start(bf16[8,2,64,2048]{3,2,1,0:T(8,128)(2,1)} %pick.1), calls=%async_computation.2 | async-start | bytes 8388608 | tf_op jit(solution)/shard_map/all_to_all | solution.py:448
  132.3 53.3 %all-to-all-start.3 = ((bf16[8,2,64,2048]{3,2,1,0:T(8,128)(2,1)}), bf16[8,2,64,2048]{3,2,1,0:T(8,128)(2,1)}, u32[]{:S(2)}, u32[]{:S(2)}) async-start(bf16[8,2,64,2048]{3,2,1,0:T(8,128)(2,1)} %pick_scaled.1), calls=%async_computation.3 | async-start | bytes 8388608 | tf_op jit(solution)/shard_map/all_to_all | solution.py:448
  194.2 20.5 %all-to-all-start.4 = ((bf16[4,576,256]{2,1,0:T(8,128)(2,1)}), bf16[4,576,256]{2,1,0:T(8,128)(2,1)S(1)}, u32[]{:S(2)}, u32[]{:S(2)}) async-start(bf16[4,576,256]{2,1,0:T(8,128)(2,1)} %bitcast.45), calls=%async_computation.4 | async-start | bytes 2359296 | tf_op jit(solution)/shard_map/all_to_all | solution.py:67
  212.5 7.7 %copy-start = (bf16[2,512,384]{2,1,0:T(8,128)(2,1)S(1)}, bf16[2,512,384]{2,1,0:T(8,128)(2,1)}, u32[]{:S(2)}) copy-start(bf16[2,512,384]{2,1,0:T(8,128)(2,1)} %get-tuple-element.34.hidden) | copy-start | bytes 2359300
  212.5 7.7 %copy-start.1 = (bf16[2,512,384]{2,1,0:T(8,128)(2,1)S(1)}, bf16[2,512,384]{2,1,0:T(8,128)(2,1)}, u32[]{:S(2)}) copy-start(bf16[2,512,384]{2,1,0:T(8,128)(2,1)} %get-tuple-element.40.gate_grad) | copy-start | bytes 2359300
  212.5 7.7 %copy-start.2 = (bf16[2,512,384]{2,1,0:T(8,128)(2,1)S(1)}, bf16[2,512,384]{2,1,0:T(8,128)(2,1)}, u32[]{:S(2)}) copy-start(bf16[2,512,384]{2,1,0:T(8,128)(2,1)} %get-tuple-element.38.up_grad) | copy-start | bytes 2359300
  216.3 18.9 %all-to-all-start.5 = ((bf16[4,576,256]{2,1,0:T(8,128)(2,1)}), bf16[4,576,256]{2,1,0:T(8,128)(2,1)S(1)}, u32[]{:S(2)}, u32[]{:S(2)}) async-start(bf16[4,576,256]{2,1,0:T(8,128)(2,1)} %sum_and_spread.2), calls=%async_computation.5 | async-start | bytes 2359296 | tf_op jit(solution)/shard_map/all_to_all | solution.py:67
  219.9 31.2 %collective-permute-start = (bf16[2,64,2048]{2,1,0:T(8,128)(2,1)}, bf16[2,64,2048]{2,1,0:T(8,128)(2,1)}, u32[]{:S(2)}, u32[]{:S(2)}) collective-permute-start(bf16[2,64,2048]{2,1,0:T(8,128)(2,1)} %get-tuple-element.43), channel_id=1, source_target_pairs={{0,4},{4,8},{8,12},{12,16},{16,20},{20,24},{24,28},{28,0},{1,5},{5... | collective-permute-start | bytes 1572872 | tf_op jit(solution)/shard_map/ppermute | solution.py:470
  219.9 32.3 %collective-permute-start.1 = (bf16[2,64,2048]{2,1,0:T(8,128)(2,1)}, bf16[2,64,2048]{2,1,0:T(8,128)(2,1)}, u32[]{:S(2)}, u32[]{:S(2)}) collective-permute-start(bf16[2,64,2048]{2,1,0:T(8,128)(2,1)} %get-tuple-element.44), channel_id=1, source_target_pairs={{0,8},{4,12},{8,16},{12,20},{16,24},{20,28},{24,0},{28,4},{1,9},{5... | collective-permute-start | bytes 1572872 | tf_op jit(solution)/shard_map/ppermute | solution.py:470
  235.2 7.7 %copy-start.3 = (bf16[4,576,256]{2,1,0:T(8,128)(2,1)}, bf16[4,576,256]{2,1,0:T(8,128)(2,1)S(1)}, u32[]{:S(2)}) copy-start(bf16[4,576,256]{2,1,0:T(8,128)(2,1)S(1)} %all-to-all-done.5) | copy-start | bytes 3538948
  242.9 18.8 %all-to-all-start.6 = ((bf16[8,256,256]{2,1,0:T(8,128)(2,1)}), bf16[8,256,256]{2,1,0:T(8,128)(2,1)S(1)}, u32[]{:S(2)}, u32[]{:S(2)}) async-start(bf16[8,256,256]{2,1,0:T(8,128)(2,1)} %bitcast.20), calls=%async_computation.6 | async-start | bytes 2097152 | tf_op jit(solution)/shard_map/all_to_all | solution.py:42
  246.5 126.3 %reduce-scatter.2.cloned.1.call-start = ((), (), s32[]{:S(2)}) async-start(), calls=%async_computation.13 | async-start | bytes 4718592 | tf_op jit(solution)/shard_map/reduce_scatter | solution.py:483
  246.6 15.3 %collective-permute-start.2 = (bf16[2,64,2048]{2,1,0:T(8,128)(2,1)}, bf16[2,64,2048]{2,1,0:T(8,128)(2,1)S(1)}, u32[]{:S(2)}, u32[]{:S(2)}) collective-permute-start(bf16[2,64,2048]{2,1,0:T(8,128)(2,1)} %get-tuple-element.45), channel_id=1, source_target_pairs={{0,12},{4,16},{8,20},{12,24},{16,28},{20,0},{24,4},{28,8},{1,13},{... | collective-permute-start | bytes 1572872 | tf_op jit(solution)/shard_map/ppermute | solution.py:470
  247.1 16.6 %collective-permute-start.3 = (bf16[2,64,2048]{2,1,0:T(8,128)(2,1)}, bf16[2,64,2048]{2,1,0:T(8,128)(2,1)S(1)}, u32[]{:S(2)}, u32[]{:S(2)}) collective-permute-start(bf16[2,64,2048]{2,1,0:T(8,128)(2,1)} %get-tuple-element.46), channel_id=1, source_target_pairs={{0,16},{4,20},{8,24},{12,28},{16,0},{20,4},{24,8},{28,12},{1,17},{... | collective-permute-start | bytes 1572872 | tf_op jit(solution)/shard_map/ppermute | solution.py:470
  250.0 34.9 %collective-permute-start.4 = (bf16[2,64,2048]{2,1,0:T(8,128)(2,1)}, bf16[2,64,2048]{2,1,0:T(8,128)(2,1)S(1)}, u32[]{:S(2)}, u32[]{:S(2)}) collective-permute-start(bf16[2,64,2048]{2,1,0:T(8,128)(2,1)} %get-tuple-element.47), channel_id=1, source_target_pairs={{0,20},{4,24},{8,28},{12,0},{16,4},{20,8},{24,12},{28,16},{1,21},{... | collective-permute-start | bytes 1572872 | tf_op jit(solution)/shard_map/ppermute | solution.py:470
  251.0 34.1 %collective-permute-start.5 = (bf16[2,64,2048]{2,1,0:T(8,128)(2,1)}, bf16[2,64,2048]{2,1,0:T(8,128)(2,1)S(1)}, u32[]{:S(2)}, u32[]{:S(2)}) collective-permute-start(bf16[2,64,2048]{2,1,0:T(8,128)(2,1)} %get-tuple-element.48), channel_id=1, source_target_pairs={{0,24},{4,28},{8,0},{12,4},{16,8},{20,12},{24,16},{28,20},{1,25},{... | collective-permute-start | bytes 1572872 | tf_op jit(solution)/shard_map/ppermute | solution.py:470
  252.2 41.7 %collective-permute-start.6 = (bf16[2,64,2048]{2,1,0:T(8,128)(2,1)}, bf16[2,64,2048]{2,1,0:T(8,128)(2,1)}, u32[]{:S(2)}, u32[]{:S(2)}) collective-permute-start(bf16[2,64,2048]{2,1,0:T(8,128)(2,1)} %get-tuple-element.49), channel_id=1, source_target_pairs={{0,28},{4,0},{8,4},{12,8},{16,12},{20,16},{24,20},{28,24},{1,29},{... | collective-permute-start | bytes 1572872 | tf_op jit(solution)/shard_map/ppermute | solution.py:470
  261.9 32.0 %copy-start.5 = (bf16[2,64,2048]{2,1,0:T(8,128)(2,1)}, bf16[2,64,2048]{2,1,0:T(8,128)(2,1)S(1)}, u32[]{:S(2)}) copy-start(bf16[2,64,2048]{2,1,0:T(8,128)(2,1)S(1)} %collective-permute-done.2.refs_5_) | copy-start | bytes 1572868
  263.7 30.2 %copy-start.6 = (bf16[2,64,2048]{2,1,0:T(8,128)(2,1)}, bf16[2,64,2048]{2,1,0:T(8,128)(2,1)S(1)}, u32[]{:S(2)}) copy-start(bf16[2,64,2048]{2,1,0:T(8,128)(2,1)S(1)} %collective-permute-done.3.refs_6_) | copy-start | bytes 1572868
  284.9 8.9 %copy-start.7 = (bf16[2,64,2048]{2,1,0:T(8,128)(2,1)}, bf16[2,64,2048]{2,1,0:T(8,128)(2,1)S(1)}, u32[]{:S(2)}) copy-start(bf16[2,64,2048]{2,1,0:T(8,128)(2,1)S(1)} %collective-permute-done.4.refs_7_) | copy-start | bytes 1572868
  285.2 8.7 %copy-start.8 = (bf16[2,64,2048]{2,1,0:T(8,128)(2,1)}, bf16[2,64,2048]{2,1,0:T(8,128)(2,1)S(1)}, u32[]{:S(2)}) copy-start(bf16[2,64,2048]{2,1,0:T(8,128)(2,1)S(1)} %collective-permute-done.5.refs_8_) | copy-start | bytes 1572868
  301.4 39.3 %copy-start.4 = (bf16[4,576,256]{2,1,0:T(8,128)(2,1)S(1)}, bf16[4,576,256]{2,1,0:T(8,128)(2,1)}, u32[]{:S(2)}) copy-start(bf16[4,576,256]{2,1,0:T(8,128)(2,1)} %copy-done.3) | copy-start | bytes 3538948
  336.0 19.8 %all-to-all-start.9 = ((bf16[8,256,256]{2,1,0:T(8,128)(2,1)}), bf16[8,256,256]{2,1,0:T(8,128)(2,1)S(1)}, u32[]{:S(2)}, u32[]{:S(2)}) async-start(bf16[8,256,256]{2,1,0:T(8,128)(2,1)} %broadcast_in_dim.11), calls=%async_computation.10 | async-start | bytes 2097152 | tf_op jit(solution)/shard_map/all_to_all | solution.py:36
Sparse Core Ops, SparseCore 0:
  10.3 60.4 all-gather.2
  72.6 53.0 all-gather.4
  301.5 58.9 reduce-scatter.1
